TPU v7x, 8 devices: a whole 2x2x1 slice. The times are simulated.
8 devices in a mesh: rep: 1 (over z), data: 2 (over y), expert: 4 (over x, core).
Axes of the slice: x: 2, y: 2, z: 1, core: 2. Of those that a mesh axis runs over, the one named last changes fastest.
Arguments:
- x: bfloat16 [32768, 2048], P(('rep', 'expert', 'data'))
- expert_idx: int32 [32768, 6], P(('rep', 'expert', 'data'))
- gate: float32 [32768, 6], P(('rep', 'expert', 'data'))
- w_gate: bfloat16 [64, 2048, 1408], P('expert', 'data')
- w_up: bfloat16 [64, 2048, 1408], P('expert', 'data')
- w_down: bfloat16 [64, 1408, 2048], P('expert', None, 'data')
Outputs:
- output: bfloat16 [32768, 2048], P(('rep', 'expert', 'data'))
All inputs are finite; a program needn't handle non-finite values.
Results may differ from a plain program's by a relative error of at most 0.00113.
Values are sent between devices in bfloat16 or wider.
A program may use at most 1 GiB of HBM per device.

v0:
```python
import jax
import jax.numpy as jnp
from jax import lax
from jax.sharding import PartitionSpec as P


def capacity_rows(tok_rows, top_k, n_exp):
    return max(8, ((5 * top_k * tok_rows) // (4 * n_exp) + 7) // 8 * 8)


def slot_table(ids_flat, n_exp, n_group, capacity):
    n_local = n_exp // n_group
    one_hot = (ids_flat[:, None] == jnp.arange(n_exp, dtype=jnp.int32)[None, :]).astype(jnp.int32)
    slot_ids = jnp.sum((jnp.cumsum(one_hot, axis=0) - one_hot) * one_hot, axis=1)
    row_base = (ids_flat % n_local) * (n_group * capacity) + (ids_flat // n_local) * capacity
    return jnp.where(slot_ids < capacity, row_base + slot_ids, n_exp * capacity)


def dispatch_rows(x_loc, dest_row, n_slots, top_k):
    tok_rows = x_loc.shape[0]
    pair_token = jnp.arange(dest_row.shape[0], dtype=jnp.int32) // top_k
    src_tok = jnp.full((n_slots,), tok_rows, jnp.int32).at[dest_row].set(pair_token, mode="drop")
    return jnp.take(x_loc, src_tok, axis=0, mode="fill", fill_value=0)


def combine_rows(x_loc, gate_loc, back_rows, dest_row):
    tok_rows, d_model = x_loc.shape
    pair_out = jnp.take(back_rows, dest_row, axis=0, mode="fill", fill_value=0)
    mixed = jnp.sum(pair_out.reshape(tok_rows, gate_loc.shape[1], d_model) * gate_loc[:, :, None], axis=1)
    return (x_loc.astype(jnp.float32) + mixed).astype(jnp.bfloat16)


def expert_ffn(expert_rows, w_gate, w_up, w_down):
    gate_act = jnp.einsum("erd,edf->erf", expert_rows, w_gate, preferred_element_type=jnp.float32)
    up_act = jnp.einsum("erd,edf->erf", expert_rows, w_up, preferred_element_type=jnp.float32)
    hidden = (jax.nn.silu(gate_act) * up_act).astype(jnp.bfloat16)
    return jnp.einsum("erf,efd->erd", hidden, w_down, preferred_element_type=jnp.float32).astype(jnp.bfloat16)


def solution(mesh):
    n_group = mesh.shape["expert"]
    tok_spec = P(("rep", "expert", "data"), None)
    wide_spec = P("expert", "data", None)
    down_spec = P("expert", None, "data")

    def device_step(x_loc, idx_loc, gate_loc, wg_loc, wu_loc, wd_loc):
        tok_rows, d_model = x_loc.shape
        top_k = idx_loc.shape[1]
        n_local = wg_loc.shape[0]
        n_exp = n_local * n_group
        capacity = capacity_rows(tok_rows, top_k, n_exp)
        dest_row = slot_table(idx_loc.reshape(tok_rows * top_k), n_exp, n_group, capacity)
        send_rows = dispatch_rows(x_loc, dest_row, n_exp * capacity, top_k).reshape(n_local, n_group, capacity, d_model)
        recv_rows = lax.all_to_all(send_rows, "expert", 1, 1, tiled=True)
        wg_full = lax.all_gather(wg_loc, "data", axis=1, tiled=True)
        wu_full = lax.all_gather(wu_loc, "data", axis=1, tiled=True)
        wd_full = lax.all_gather(wd_loc, "data", axis=2, tiled=True)
        out_rows = expert_ffn(recv_rows.reshape(n_local, n_group * capacity, d_model), wg_full, wu_full, wd_full)
        back_rows = lax.all_to_all(out_rows.reshape(n_local, n_group, capacity, d_model), "expert", 1, 1, tiled=True)
        return combine_rows(x_loc, gate_loc, back_rows.reshape(n_exp * capacity, d_model), dest_row)

    return jax.shard_map(device_step, mesh=mesh, in_specs=(tok_spec, tok_spec, tok_spec, wide_spec, wide_spec, down_spec), out_specs=tok_spec, check_vma=False)
```

profile of v0, /device:TPU:0, one launch (start us, length us, event | category | flops | bytes accessed | tf_op | source)
XLA Modules:
  0.0 6177.0 jit_solution(13849149926190981991)
XLA Ops:
  15.1 3.4 copy-done.2
  19.5 8.4 broadcast_add_fusion
  28.0 8.6 copy.43
  36.6 8.5 fusion.4
  46.1 90.7 %scatter_custom_fusion = s32[30720]{0:T(1024)S(1)} fusion(s32[24576]{0:T(1024)S(1)} %bitcast.44, s32[24576]{0:T(1024)S(1)} %add_select_fusion.2, s32[]{:T(128)} %constant.77.clone.1), kind=kCustom, calls=%fused_computation.62 | custom fusion | bytes 122884 | tf_op jit(solution)/shard_map/scatter | solution.py:22
  137.6 234.3 %gather_fusion = bf16[30720,2048]{1,0:T(8,128)(2,1)} fusion(bf16[4096,2048]{1,0:T(8,128)(2,1)} %param.6, s32[30720]{0:T(1024)S(1)} %fusion.15), kind=kCustom, calls=%fused_computation | custom fusion | bytes 251781120 | tf_op jit(solution)/shard_map/jit(_take)/gather | solution.py:23
  372.0 81.6 %copy_select_fusion = bf16[16,4,480,2048]{3,2,0,1:T(8,128)(2,1)} fusion(bf16[16,4,480,2048]{3,2,1,0:T(8,128)(2,1)} %bitcast.4, pred[16,4,480]{2,0,1:T(8,128)(4,1)S(1)} %copy-done.9), kind=kLoop, calls=%fused_computation.5 | loop fusion | flops 62914560 | bytes 251688960 | tf_op jit(solution)/shard_map/jit(_take)/select_n | solution.py:23
  453.5 24.8 all-to-all-start
  479.0 1351.5 %all-to-all-done = bf16[16,4,480,2048]{3,2,0,1:T(8,128)(2,1)} async-done(((bf16[16,4,480,2048]{3,2,0,1:T(8,128)(2,1)}), bf16[16,4,480,2048]{3,2,0,1:T(8,128)(2,1)}, u32[]{:S(2)}, u32[]{:S(2)}) %all-to-all-start) | async-done | bytes 125829152 | tf_op jit(solution)/shard_map/all_to_all | solution.py:54
  1830.5 82.0 %copy.51 = bf16[16,4,480,2048]{3,2,1,0:T(8,128)(2,1)} copy(bf16[16,4,480,2048]{3,2,0,1:T(8,128)(2,1)} %all-to-all-done) | data formatting | bytes 251658240 | tf_op jit(solution)/shard_map/all_to_all | solution.py:54
  1912.5 208.2 %fusion.24 = f32[16,1920,1408]{2,1,0:T(8,128)} fusion(bf16[16,1920,2048]{2,1,0:T(8,128)(2,1)} %bitcast.5, bf16[16,2048,1408]{2,1,0:T(8,128)(2,1)} %all-gather.4.cloned.1.call-done), kind=kOutput, calls=%fused_computation.65 | convolution fusion | flops 177167400960 | bytes 391118848 | tf_op jit(solution)/shard_map/erd,edf->erf/dot_general | solution.py:34
  2120.7 230.6 %multiply_convert_fusion = bf16[16,1920,1408]{2,1,0:T(8,128)(2,1)} fusion(f32[16,1920,1408]{2,1,0:T(8,128)} %fusion.24, bf16[16,1920,2048]{2,1,0:T(8,128)(2,1)} %bitcast.5, bf16[16,2048,1408]{2,1,0:T(8,128)(2,1)} %all-gather.6.cloned.1.call-done), kind=kOutput, calls=%fused_computation.4 | convolution fusion | flops 177426923520 | bytes 477626368 | tf_op jit(solution)/shard_map/erd,edf->erf/dot_general | solution.py:35
  2351.3 805.2 %all-gather.8.cloned.1.call-done = bf16[16,1408,2048]{2,1,0:T(8,128)(2,1)} async-done(((bf16[16,1408,1024]{2,1,0:T(8,128)(2,1)}), bf16[16,1408,2048]{2,1,0:T(8,128)(2,1)}) %all-gather.8.cloned.1.call-update) | async-done | bytes 92274704 | tf_op jit(solution)/shard_map/all_gather | solution.py:57
  3156.5 206.6 %convolution_convert_fusion = bf16[16,1920,2048]{2,1,0:T(8,128)(2,1)} fusion(bf16[16,1920,1408]{2,1,0:T(8,128)(2,1)} %multiply_convert_fusion, bf16[16,1408,2048]{2,1,0:T(8,128)(2,1)} %all-gather.8.cloned.1.call-done), kind=kOutput, calls=%fused_computation.6 | convolution fusion | flops 177230315520 | bytes 304611328 | tf_op jit(solution)/shard_map/erf,efd->erd/dot_general | solution.py:37
  3363.2 81.8 %copy.52 = bf16[16,4,480,2048]{3,2,0,1:T(8,128)(2,1)} copy(bf16[16,4,480,2048]{3,2,1,0:T(8,128)(2,1)} %bitcast.6) | data formatting | bytes 251658240 | tf_op jit(solution)/shard_map/reshape | solution.py:59
  3445.0 25.1 all-to-all-start.1
  3470.1 3.5 reduce_sum.23
  3475.6 4.7 compare_and_fusion
  3480.4 1341.0 %all-to-all-done.1 = bf16[16,4,480,2048]{3,2,0,1:T(8,128)(2,1)} async-done(((bf16[16,4,480,2048]{3,2,0,1:T(8,128)(2,1)}), bf16[16,4,480,2048]{3,2,0,1:T(8,128)(2,1)}, u32[]{:S(2)}, u32[]{:S(2)}) %all-to-all-start.1) | async-done | bytes 125829152 | tf_op jit(solution)/shard_map/all_to_all | solution.py:59
  4821.3 81.7 %copy.53 = bf16[16,4,480,2048]{3,2,1,0:T(8,128)(2,1)} copy(bf16[16,4,480,2048]{3,2,0,1:T(8,128)(2,1)} %all-to-all-done.1) | data formatting | bytes 251658240 | tf_op jit(solution)/shard_map/all_to_all | solution.py:59
  4903.0 938.7 %gather_fusion.1 = bf16[24576,2048]{1,0:T(8,128)(2,1)} fusion(bf16[30720,2048]{1,0:T(8,128)(2,1)} %bitcast.7, s32[24576]{0:T(1024)S(1)} %broadcast_clamp_fusion), kind=kCustom, calls=%fused_computation.1 | custom fusion | bytes 201424896 | tf_op jit(solution)/shard_map/jit(_take)/gather | solution.py:28
  5841.7 153.8 %gather.15 = bf16[4096,6,2048]{2,1,0:T(8,128)(2,1)} reshape(bf16[24576,2048]{1,0:T(8,128)(2,1)} %gather_fusion.1) | data formatting | bytes 201326592 | tf_op jit(solution)/shard_map/jit(_take)/gather | solution.py:28
  5995.5 152.4 %multiply_reduce_fusion = f32[4096,2048]{1,0:T(8,128)} fusion(f32[4096,6]{1,0:T(8,128)S(1)} %copy-done.3, bf16[4096,6,2048]{2,1,0:T(8,128)(2,1)} %gather.15, pred[4096,6]{1,0:T(8,128)(4,1)S(1)} %copy-done.4), kind=kLoop, calls=%fused_computation.3 | loop fusion | flops 192937984 | bytes 134340608 | tf_op jit(solution)/shard_map/reduce_sum | solution.py:29
  6147.9 22.3 add_convert_fusion
  (53 shorter events, 14.0 us)
Async XLA Ops:
  6.5 1.5 copy-start.10
  6.5 1905.9 %all-gather.4.cloned.1.call-start = ((), (), s32[]{:S(2)}) async-start(), calls=%async_computation.2 | async-start | bytes 138412032 | tf_op jit(solution)/shard_map/all_gather | solution.py:55
  7.3 2113.4 %all-gather.6.cloned.1.call-start = ((), (), s32[]{:S(2)}) async-start(), calls=%async_computation.3 | async-start | bytes 138412032 | tf_op jit(solution)/shard_map/all_gather | solution.py:56
  8.7 363.3 %copy-start = (s32[4096,6]{1,0:T(8,128)}, s32[4096,6]{1,0:T(8,128)S(1)}, u32[]{:S(2)}) copy-start(s32[4096,6]{1,0:T(8,128)S(1)} %copy.38) | copy-start | bytes 294916
  15.1 3.4 copy-start.2
  45.1 0.9 copy-start.5
  46.0 90.9 %copy-start.7 = (s32[24576,1]{0,1:T(1,128)}, s32[24576,1]{0,1:T(1,128)S(1)}, u32[]{:S(2)}) copy-start(s32[24576,1]{0,1:T(1,128)S(1)} %compare_select_fusion.1) | copy-start | bytes 294916
  137.6 234.4 %copy-start.9 = (pred[16,4,480]{2,0,1:T(8,128)(4,1)S(1)}, pred[16,4,480]{2,0,1:T(8,128)(4,1)}, u32[]{:S(2)}) copy-start(pred[16,4,480]{2,0,1:T(8,128)(4,1)} %copy.49) | copy-start | bytes 92164
  453.5 1377.0 %all-to-all-start = ((bf16[16,4,480,2048]{3,2,0,1:T(8,128)(2,1)}), bf16[16,4,480,2048]{3,2,0,1:T(8,128)(2,1)}, u32[]{:S(2)}, u32[]{:S(2)}) async-start(bf16[16,4,480,2048]{3,2,0,1:T(8,128)(2,1)} %copy_select_fusion), calls=%async_computation | async-start | bytes 251658240 | tf_op jit(solution)/shard_map/all_to_all | solution.py:54
  478.3 2678.2 %all-gather.8.cloned.1.call-start = ((), (), s32[]{:S(2)}) async-start(), calls=%async_computation.4 | async-start | bytes 138412032 | tf_op jit(solution)/shard_map/all_gather | solution.py:57
  3445.0 25.1 copy-start.6
  3445.0 28.6 copy-start.11
  3445.0 30.6 copy-start.8
  3445.0 30.6 copy-start.1
  3445.0 1376.3 %all-to-all-start.1 = ((bf16[16,4,480,2048]{3,2,0,1:T(8,128)(2,1)}), bf16[16,4,480,2048]{3,2,0,1:T(8,128)(2,1)}, u32[]{:S(2)}, u32[]{:S(2)}) async-start(bf16[16,4,480,2048]{3,2,0,1:T(8,128)(2,1)} %copy.52), calls=%async_computation.1 | async-start | bytes 251658240 | tf_op jit(solution)/shard_map/all_to_all | solution.py:59
  5841.7 153.8 %copy-start.3 = (f32[4096,6]{1,0:T(8,128)S(1)}, f32[4096,6]{1,0:T(8,128)}, u32[]{:S(2)}) copy-start(f32[4096,6]{1,0:T(8,128)} %copy.54) | copy-start | bytes 294916
  5841.7 153.8 %copy-start.4 = (pred[4096,6]{1,0:T(8,128)(4,1)S(1)}, pred[4096,6]{1,0:T(8,128)(4,1)}, u32[]{:S(2)}) copy-start(pred[4096,6]{1,0:T(8,128)(4,1)} %compare_and_fusion) | copy-start | bytes 73732
Sparse Core Ops, SparseCore 0:
  8.8 1050.4 all-gather.3
  1060.9 1047.6 all-gather.5
  2110.1 1046.3 all-gather.7
where the time goes:
time: 6210 us; the launch traced here: 6180 us
  waiting for transfers between devices  3500 us (56%)
  local copies, waits for them, and re-layouts  1690 us (27%)
  matrix products  646 us (10%)
  other arithmetic  281 us (5%)
    all_to_all x1, waiting for transfers between devices, device_step(): recv_rows = lax.all_to_all(send_rows, 'expert', 1, 1, tiled=True)  1350 us
    all_to_all x1, waiting for transfers between devices, device_step(): lax.all_to_all(out_rows.reshape(n_local, n_group, capacity, d_model), 'ex...  1340 us
    gather x2, local copies, waits for them, and re-layouts, combine_rows(): pair_out = jnp.take(back_rows, dest_row, axis=0, mode='fill', fill_value=0)  1090 us
    all_gather x1, waiting for transfers between devices, device_step(): wd_full = lax.all_gather(wd_loc, 'data', axis=2, tiled=True)  805 us
    gather x1, local copies, waits for them, and re-layouts, dispatch_rows(): return jnp.take(x_loc, src_tok, axis=0, mode='fill', fill_value=0)  234 us
    dot_general x1, matrix products, expert_ffn(): jnp.einsum('erd,edf->erf', expert_rows, w_up, preferred_element_type=jnp....  231 us
    dot_general x1, matrix products, expert_ffn(): jnp.einsum('erd,edf->erf', expert_rows, w_gate, preferred_element_type=jn...  208 us
    dot_general x1, matrix products, expert_ffn(): jnp.einsum('erf,efd->erd', hidden, w_down, preferred_element_type=jnp.flo...  207 us
  transfers between devices with their start and end apart: 5, of which 3 were waited for; matrix products, arithmetic and copies ran while one was open for 16% of the time, Pallas kernels for 0%

commit v1 on v0

v1 whole, which is shorter than its diff:
```python
import functools

import jax
import jax.numpy as jnp
from jax import lax
from jax.experimental import pallas as pl
from jax.experimental.pallas import tpu as pltpu
from jax.sharding import PartitionSpec as P


LANES = 128
NO_EXPERT = LANES - 1
TILE = 256
WINDOW = 128
MOVES = 2
TAIL, TAIL_CAP = 3, 16
BF16, F32, I32 = jnp.bfloat16, jnp.float32, jnp.int32
ANY = pl.BlockSpec(memory_space=pl.ANY)
SMEM = pl.BlockSpec(memory_space=pltpu.SMEM)
VMEM_LIMIT = 62 * 1024 * 1024
TOKEN = jax.ShapeDtypeStruct((1,), I32)


def capacity_rows(tok_rows, top_k, n_exp):
    return max(8, ((5 * top_k * tok_rows) // (4 * n_exp) + 7) // 8 * 8)


def params(n_axes=0):
    return pltpu.CompilerParams(dimension_semantics=("arbitrary",) * n_axes if n_axes else None, vmem_limit_bytes=VMEM_LIMIT)


def cost(flops, bytes_accessed):
    return pl.CostEstimate(flops=flops, bytes_accessed=bytes_accessed, transcendentals=0)


def route_body(capacity, ids_ref, gate_ref, slot_ref, slot_t_ref, gate_te_ref, start_ref, count_ref, seen):
    @pl.when(pl.program_id(0) == 0)
    def _():
        seen[...] = jnp.zeros_like(seen)

    top_k, tile = ids_ref.shape
    expert = lax.broadcasted_iota(I32, (LANES, tile), 0)
    mask = jnp.zeros((LANES, tile), F32)
    gate_t = jnp.zeros((LANES, tile), F32)
    for j in range(top_k):
        hit = ids_ref[j : j + 1, :] == expert
        mask = jnp.where(hit, 1.0, mask)
        gate_t = jnp.where(hit, gate_ref[j : j + 1, :], gate_t)
    before = lax.broadcasted_iota(I32, (tile, tile), 0) < lax.broadcasted_iota(I32, (tile, tile), 1)
    earlier = jnp.dot(mask.astype(BF16), jnp.where(before, 1.0, 0.0).astype(BF16), preferred_element_type=F32) + seen[:, 0:1]
    slot = jnp.where((mask > 0.0) & (earlier < capacity), earlier, -1.0)
    slot_t_ref[...] = slot.astype(I32)
    slot_ref[...] = slot.T.astype(I32)
    gate_te_ref[...] = gate_t.T
    start_ref[0] = jnp.minimum(seen[...].T[:8], capacity).astype(I32)
    seen[...] = seen[...] + jnp.sum(mask, axis=1, keepdims=True)
    count_ref[...] = jnp.minimum(seen[...].T[:8], capacity).astype(I32)


def route(ids_t, gate_t, capacity):
    top_k, tok_rows = ids_t.shape
    n_tiles = tok_rows // TILE
    col = pl.BlockSpec((TILE, LANES), lambda i: (i, 0))
    return pl.pallas_call(
        functools.partial(route_body, capacity),
        grid=(n_tiles,),
        in_specs=[pl.BlockSpec((top_k, TILE), lambda i: (0, i))] * 2,
        out_specs=[
            col,
            pl.BlockSpec((LANES, TILE), lambda i: (0, i)),
            col,
            pl.BlockSpec((1, 8, LANES), lambda i: (i, 0, 0)),
            pl.BlockSpec((8, LANES), lambda i: (0, 0)),
        ],
        out_shape=[
            jax.ShapeDtypeStruct((tok_rows, LANES), I32),
            jax.ShapeDtypeStruct((LANES, tok_rows), I32),
            jax.ShapeDtypeStruct((tok_rows, LANES), F32),
            jax.ShapeDtypeStruct((n_tiles, 8, LANES), I32),
            jax.ShapeDtypeStruct((8, LANES), I32),
        ],
        scratch_shapes=[pltpu.VMEM((LANES, LANES), F32)],
        compiler_params=params(1),
        name="route",
    )(ids_t, gate_t)


def windows(start_ref, tile, e, capacity, step):
    lo, hi = start_ref[tile, e], start_ref[tile + 1, e]
    floor = lo // 16 * 16
    n_win = jnp.where(hi > lo, (hi - floor + WINDOW - 1) // WINDOW, 0)

    @pl.loop(0, n_win)
    def _(w):
        first = floor + w * WINDOW
        step(first, pl.multiple_of(jnp.minimum(first, capacity - WINDOW), 16))


def pick_body(r_ref, tab_ref, start_ref, slot_t_ref, x_ref, *refs):
    outs, token = refs[:-1], refs[-1]
    tile = pl.program_id(0)
    token[0] = 0

    @pl.when(tile == 0)
    def _():
        for out in outs:
            out[...] = jnp.zeros_like(out)

    for k, out in enumerate(outs):
        e = tab_ref[r_ref[0] + 1, k]

        def step(first, base, out=out, e=e):
            slots = slot_t_ref[pl.ds(e, 1), :]
            row = lax.broadcasted_iota(I32, (WINDOW, TILE), 0) + base
            hot = jnp.where((row == slots) & (slots >= first), 1.0, 0.0).astype(BF16)
            out[pl.ds(base, WINDOW), :] += jnp.dot(hot, x_ref[...], preferred_element_type=F32).astype(BF16)

        windows(start_ref, tile, e, out.shape[0], step)


def pick(r, table, starts, slot_t, x_loc, capacity):
    n_pick = table.shape[1]
    tok_rows, d_model = x_loc.shape
    return pl.pallas_call(
        pick_body,
        grid=(tok_rows // TILE,),
        in_specs=[
            SMEM,
            SMEM,
            SMEM,
            pl.BlockSpec((LANES, TILE), lambda i: (0, i)),
            pl.BlockSpec((TILE, d_model), lambda i: (i, 0)),
        ],
        out_specs=[pl.BlockSpec((capacity, d_model), lambda i: (0, 0))] * n_pick + [SMEM],
        out_shape=[jax.ShapeDtypeStruct((capacity, d_model), BF16)] * n_pick + [TOKEN],
        compiler_params=params(1),
        cost_estimate=cost(2 * n_pick * capacity * TILE * d_model, 2 * tok_rows * d_model),
        name="pick",
    )(r, table, starts, slot_t, x_loc)


def pick_tail_body(tail_ref, slot_t_ref, x_ref, *outs):
    tile = pl.program_id(0)
    n_tail = tail_ref.shape[1]
    group = n_tail * TAIL_CAP
    hots = []
    for k in range(len(outs)):
        for i in range(n_tail):
            row = lax.broadcasted_iota(I32, (TAIL_CAP, x_ref.shape[0]), 0)
            hots.append(jnp.where(row == slot_t_ref[pl.ds(tail_ref[k, i], 1), :], 1.0, 0.0).astype(BF16))
    picked = jnp.dot(jnp.concatenate(hots, axis=0), x_ref[...], preferred_element_type=F32).astype(BF16)

    @pl.when(tile == 0)
    def _():
        for out in outs:
            out[...] = jnp.zeros_like(out)

    for k, out in enumerate(outs):
        out[...] += picked[k * group : (k + 1) * group]


def pick_tail(tail, slot_t, x_loc):
    n_pos, n_tail = tail.shape
    tok_rows, d_model = x_loc.shape
    group = n_tail * TAIL_CAP
    return pl.pallas_call(
        pick_tail_body,
        grid=(tok_rows // TILE,),
        in_specs=[SMEM, pl.BlockSpec((LANES, TILE), lambda i: (0, i)), pl.BlockSpec((TILE, d_model), lambda i: (i, 0))],
        out_specs=[pl.BlockSpec((group, d_model), lambda i: (0, 0))] * n_pos,
        out_shape=[jax.ShapeDtypeStruct((group, d_model), BF16)] * n_pos,
        compiler_params=params(1),
        cost_estimate=cost(2 * n_pos * group * tok_rows * d_model, 2 * tok_rows * d_model),
        name="pick_tail",
    )(tail, slot_t, x_loc)


def ffn_body(n_local, r_ref, src_ref, used_ref, *refs):
    n_src = 1 + MOVES
    own, (pg, pu, pd) = refs[: 3 * n_src], refs[3 * n_src : 3 * n_src + 3]
    refs = refs[3 * n_src + 3 :]
    n_rows = used_ref.shape[1]
    rows, outs, token = refs[:n_rows], refs[n_rows : 2 * n_rows], refs[2 * n_rows]
    x_buf, w_in, w_out, o_buf, x_sem, w_sem, o_sem = refs[2 * n_rows + 1 :]
    half, ffn = pg.shape
    q = lax.axis_index("data")
    r = r_ref[0]
    src = src_ref[r]
    token[0] = 0

    def load(place, parts, first):
        at = pl.ds(pl.multiple_of(place * half, half), half)
        places = (w_in.at[at, pl.ds(0, ffn)], w_in.at[at, pl.ds(ffn, ffn)], w_out.at[:, at])
        return [pltpu.make_async_copy(part, dst, w_sem.at[first + i]) for i, (part, dst) in enumerate(zip(parts, places))]

    row_loads = [pltpu.make_async_copy(rows[i], x_buf.at[i], x_sem.at[i]) for i in range(n_rows)]
    row_loads[0].start()
    theirs = load(1 - q, (pg, pu, pd), 3)
    for copy in theirs[:2]:
        copy.start()
    for s in range(n_src):
        @pl.when(jnp.maximum(src - n_local + 1, 0) == s)
        def _():
            parts = own[3 * s : 3 * s + 3]
            for copy in load(q, [part.at[jnp.minimum(src, n_local - 1)] for part in parts] if s == 0 else parts, 0):
                copy.start()
    theirs[2].start()
    for copy in row_loads[1:]:
        copy.start()
    ours = load(q, (pg, pu, pd), 0)
    for copy in row_loads + ours + theirs:
        copy.wait()

    n_part = 2
    part = x_buf.shape[1] // n_part

    @pl.loop(0, n_rows)
    def _(i):
        @pl.loop(0, n_part)
        def _(j):
            at = pl.ds(pl.multiple_of(j * part, part), part)

            @pl.when(used_ref[r, i] > j * part)
            def _():
                act = jnp.dot(x_buf[i, at], w_in[...], preferred_element_type=F32)
                gate_act, up_act = act[:, :ffn], act[:, ffn:]
                hidden = (jax.nn.silu(gate_act) * up_act).astype(BF16)
                o_buf[i, at] = jnp.dot(hidden, w_out[...], preferred_element_type=F32).astype(BF16)

            @pl.when(used_ref[r, i] <= j * part)
            def _():
                o_buf[i, at] = jnp.zeros((part, o_buf.shape[2]), BF16)

        for s in range(n_rows):
            @pl.when(i == s)
            def _():
                pltpu.make_async_copy(o_buf.at[s], outs[s], o_sem.at[s]).start()

    for s in range(n_rows):
        pltpu.make_async_copy(o_buf.at[s], outs[s], o_sem.at[s]).wait()


def expert_ffn(r, sources, used, weights, extras, peer, rows):
    capacity, d_model = rows[0].shape
    n_local, half, ffn = weights[0].shape
    n_rows = len(rows)
    own = list(weights) + [part for extra in extras for part in extra]
    out = pl.pallas_call(
        functools.partial(ffn_body, n_local),
        in_specs=[SMEM] * 3 + [ANY] * (len(own) + 3 + n_rows),
        out_specs=[ANY] * n_rows + [SMEM],
        out_shape=[jax.ShapeDtypeStruct((capacity, d_model), BF16)] * n_rows + [TOKEN],
        scratch_shapes=[
            pltpu.VMEM((n_rows, capacity, d_model), BF16),
            pltpu.VMEM((2 * half, 2 * ffn), BF16),
            pltpu.VMEM((ffn, d_model), BF16),
            pltpu.VMEM((n_rows, capacity, d_model), BF16),
            pltpu.SemaphoreType.DMA((n_rows,)),
            pltpu.SemaphoreType.DMA((6,)),
            pltpu.SemaphoreType.DMA((n_rows,)),
        ],
        compiler_params=params(),
        cost_estimate=cost(6 * n_rows * capacity * d_model * ffn, 6 * d_model * ffn),
        name="ffn",
    )(r, sources, used, *own, *peer, *rows)
    return tuple(out[:n_rows]), out[n_rows]


def tail_sum(tail_ref, slot_ref, gate_ref, rows_ref, total):
    n_pos, n_tail = tail_ref.shape
    n_col = rows_ref.shape[0]
    row = lax.broadcasted_iota(I32, (LANES, n_col), 0)
    group = lax.broadcasted_iota(I32, (LANES, n_col), 1) // TAIL_CAP
    wanted = jnp.full((LANES, n_col), NO_EXPERT, I32)
    for k in range(n_pos):
        for i in range(n_tail):
            wanted = jnp.where(group == k * n_tail + i, tail_ref[k, i], wanted)
    select = jnp.where(row == wanted, 1.0, 0.0).astype(BF16)
    slots = jnp.dot(slot_ref[...].astype(F32).astype(BF16), select, preferred_element_type=F32)
    place = lax.broadcasted_iota(I32, (TILE, n_col), 1) % TAIL_CAP
    here = slots == place.astype(F32)
    rest = gate_ref[...]
    weights = []
    for _ in range(3):
        piece = rest.astype(BF16)
        rest = rest - piece.astype(F32)
        weights.append(jnp.where(here, jnp.dot(piece, select, preferred_element_type=F32), 0.0).astype(BF16))
    parts = jnp.dot(jnp.concatenate(weights, axis=0), rows_ref[...], preferred_element_type=F32)
    total[...] += parts[:TILE] + parts[TILE : 2 * TILE] + parts[2 * TILE :]


def mix_body(has_tail, r_ref, tab_ref, start_ref, slot_ref, gate_ref, *refs):
    n_rows = tab_ref.shape[1]
    rows, refs = refs[:n_rows], refs[n_rows:]
    acc_ref, tails, (out_ref, token, total) = refs[0], refs[1:-3], refs[-3:]
    tile = pl.program_id(0)
    token[0] = 0
    total[...] = acc_ref[...]
    if has_tail:
        tail_sum(tails[0], slot_ref, gate_ref, tails[1], total)
    lane = lax.broadcasted_iota(I32, (TILE, LANES), 1)
    for k in range(n_rows):
        e = tab_ref[r_ref[0] + 1, k]

        def step(first, base, k=k, e=e):
            here = lane == e
            slots = jnp.max(jnp.where(here, slot_ref[...], -1), axis=1, keepdims=True)
            gates = jnp.sum(jnp.where(here, gate_ref[...], 0.0), axis=1, keepdims=True)
            column = lax.broadcasted_iota(I32, (TILE, WINDOW), 1) + base
            hot = jnp.where((column == slots) & (slots >= first), 1.0, 0.0).astype(BF16)
            total[...] += gates * jnp.dot(hot, rows[k][pl.ds(base, WINDOW), :], preferred_element_type=F32)

        windows(start_ref, tile, e, rows[k].shape[0], step)
    out_ref[...] = total[...].astype(out_ref.dtype)


def mix(r, table, starts, slot, gate_te, rows, acc, out_dtype, tail=()):
    _, d_model = rows[0].shape
    tok_rows = acc.shape[0]
    n_rows = len(rows)
    col = pl.BlockSpec((TILE, LANES), lambda i: (i, 0))
    wide = pl.BlockSpec((TILE, d_model), lambda i: (i, 0))

    def held(value):
        return pl.BlockSpec(value.shape, lambda i: (0, 0), pipeline_mode=pl.Buffered(1))

    return pl.pallas_call(
        functools.partial(mix_body, bool(tail)),
        grid=(tok_rows // TILE,),
        in_specs=[SMEM, SMEM, SMEM, col, col] + [held(row) for row in rows] + [wide] + ([SMEM, held(tail[1])] if tail else []),
        out_specs=[wide, SMEM],
        out_shape=[jax.ShapeDtypeStruct((tok_rows, d_model), out_dtype), TOKEN],
        scratch_shapes=[pltpu.VMEM((TILE, d_model), F32)],
        input_output_aliases={5 + n_rows: 0} if acc.dtype == out_dtype else {},
        compiler_params=params(1),
        cost_estimate=cost(2 * n_rows * tok_rows * WINDOW * d_model, 8 * tok_rows * d_model),
        name="mix",
    )(r, table, starts, slot, gate_te, *rows, acc, *tail)


def tail_in_body(idx_ref, x_ref, wg_ref, wu_ref, out_ref):
    n_src, _, rows, half = x_ref.shape
    ffn = wg_ref.shape[2]
    x = x_ref[...].reshape(n_src * rows, half)
    out_ref[:, 0, :, :ffn] = jnp.dot(x, wg_ref[0], preferred_element_type=F32).reshape(n_src, rows, ffn)
    out_ref[:, 0, :, ffn:] = jnp.dot(x, wu_ref[0], preferred_element_type=F32).reshape(n_src, rows, ffn)


def tail_in(idx, x, w_gate, w_up):
    n_src, n_tail, rows, half = x.shape
    ffn = w_gate.shape[2]
    weight = pl.BlockSpec((1, half, ffn), lambda i, idx: (idx[i], 0, 0))
    return pl.pallas_call(
        tail_in_body,
        grid_spec=pltpu.PrefetchScalarGridSpec(
            num_scalar_prefetch=1,
            grid=(n_tail,),
            in_specs=[pl.BlockSpec((n_src, 1, rows, half), lambda i, idx: (0, i, 0, 0)), weight, weight],
            out_specs=pl.BlockSpec((n_src, 1, rows, 2 * ffn), lambda i, idx: (0, i, 0, 0)),
        ),
        out_shape=jax.ShapeDtypeStruct((n_src, n_tail, rows, 2 * ffn), F32),
        compiler_params=params(1),
        cost_estimate=cost(4 * n_src * n_tail * rows * half * ffn, 4 * n_tail * half * ffn),
        name="tail_in",
    )(idx, x, w_gate, w_up)


def tail_out_body(idx_ref, h_ref, wd_ref, out_ref):
    n_src, _, rows, ffn = h_ref.shape
    out = jnp.dot(h_ref[...].reshape(n_src * rows, ffn), wd_ref[0], preferred_element_type=F32)
    out_ref[:, 0] = out.reshape(n_src, rows, -1).astype(BF16)


def tail_out(idx, hidden, w_down):
    n_src, n_tail, rows, ffn = hidden.shape
    half = w_down.shape[2]
    return pl.pallas_call(
        tail_out_body,
        grid_spec=pltpu.PrefetchScalarGridSpec(
            num_scalar_prefetch=1,
            grid=(n_tail,),
            in_specs=[
                pl.BlockSpec((n_src, 1, rows, ffn), lambda i, idx: (0, i, 0, 0)),
                pl.BlockSpec((1, ffn, half), lambda i, idx: (idx[i], 0, 0)),
            ],
            out_specs=pl.BlockSpec((n_src, 1, rows, half), lambda i, idx: (0, i, 0, 0)),
        ),
        out_shape=jax.ShapeDtypeStruct((n_src, n_tail, rows, half), BF16),
        compiler_params=params(1),
        cost_estimate=cost(2 * n_src * n_tail * rows * half * ffn, 2 * n_tail * half * ffn),
        name="tail_out",
    )(idx, hidden, w_down)


def plan(counts, n_group):
    load = jnp.max(counts, axis=0).reshape(n_group, -1)
    n_local = load.shape[1]
    ids = jnp.arange(n_local, dtype=I32)
    ahead = (load[:, None, :] > load[:, :, None]) | ((load[:, None, :] == load[:, :, None]) & (ids[None, None, :] < ids[None, :, None]))
    rank = jnp.sum(ahead.astype(I32), axis=2)
    active = jnp.sum((load > 0).astype(I32), axis=1)
    tail = jnp.minimum(jnp.sum(((load > 0) & (load <= TAIL_CAP)).astype(I32), axis=1), TAIL)
    full = active - tail
    partner = full.reshape(-1, 2)[:, ::-1].reshape(-1)
    give = jnp.clip((full - partner) // 2, 0, MOVES)
    keep = full - give
    partner_keep = keep.reshape(-1, 2)[:, ::-1].reshape(-1)
    position = jnp.arange(n_group, dtype=I32)[:, None]
    kept = rank < keep[:, None]
    in_round = rank < full[:, None]
    to = jnp.where(kept, position, position ^ 1)
    at = jnp.where(kept, rank, partner_keep[:, None] + rank - keep[:, None])
    source = jnp.where(kept, ids[None, :], n_local + rank - keep[:, None])
    tail_at = jnp.where((rank >= full[:, None]) & (rank < active[:, None]), rank - full[:, None], -1)
    n_slots = n_local + MOVES + 2
    flat = lambda a: jnp.broadcast_to(a, load.shape).reshape(-1)
    expert = jnp.arange(load.size, dtype=I32)
    rounds = jnp.arange(n_slots, dtype=I32)
    hit = (flat(to)[None, None, :] == position[:, :, None]) & (flat(at)[None, None, :] == rounds[None, :, None]) & flat(in_round)[None, None, :]
    table = jnp.max(jnp.where(hit, (expert + LANES * flat(source))[None, None, :], -1), axis=2)
    experts = jnp.where(table < 0, NO_EXPERT, table % LANES)
    sources = jnp.where(table < 0, 0, table // LANES)
    steps = jnp.arange(max(TAIL, MOVES), dtype=I32)
    tail_hit = tail_at[:, None, :] == steps[None, :TAIL, None]
    tails = jnp.max(jnp.where(tail_hit, ids[None, None, :], -1), axis=2)
    move_hit = (rank - keep[:, None])[:, None, :] == steps[None, :MOVES, None]
    moves = jnp.max(jnp.where(move_hit, ids[None, None, :], 0), axis=2)
    return experts, sources, tails, moves, jnp.maximum(jnp.max(keep + give.reshape(-1, 2)[:, ::-1].reshape(-1)), 1)


def solution(mesh):
    n_group, n_data = mesh.shape["expert"], mesh.shape["data"]
    assert n_group == 4 and n_data == 2
    tok_spec = P(("rep", "expert", "data"), None)
    wide_spec = P("expert", "data", None)
    down_spec = P("expert", None, "data")
    swap = [(0, 1), (1, 0)]

    def across(value, k):
        return lax.ppermute(value, "expert", [(p, p ^ k) for p in range(n_group)])

    def spread(groups):
        return (groups[0],) + tuple(across(groups[k], k) for k in range(1, n_group))

    def swapped(parts):
        return tuple(lax.ppermute(part, "data", swap) for part in parts)

    def device_body(x_loc, idx_loc, gate_loc, wg_loc, wu_loc, wd_loc):
        tok_rows, d_model = x_loc.shape
        top_k = idx_loc.shape[1]
        n_local = wg_loc.shape[0]
        n_exp = n_local * n_group
        capacity = capacity_rows(tok_rows, top_k, n_exp)
        me, q = lax.axis_index("expert"), lax.axis_index("data")
        weights = (wg_loc, wu_loc, wd_loc)
        slot, slot_t, gate_te, tile_starts, count = route(idx_loc.T, gate_loc.T, capacity)
        starts = jnp.concatenate([tile_starts[:, 0], count[:1]], axis=0)
        counts = lax.all_gather(count[0, :n_exp], ("expert", "data"))
        experts, sources, tails, moves, n_round = plan(counts, n_group)
        mine = me ^ jnp.arange(n_group, dtype=I32)
        table = jnp.concatenate([jnp.full((1, n_group), NO_EXPERT, I32), experts[mine].T], axis=0)
        my_sources = sources[me]
        my_hot = (experts[me][:, None] == jnp.arange(n_exp, dtype=I32)[None, :]).astype(I32)
        my_counts = counts.reshape(n_group, n_data, n_exp)[mine, q]
        used = jnp.sum(my_hot[:, None, :] * my_counts[None, :, :], axis=2)
        tail_local = jnp.maximum(tails[me], 0)
        tail_global = jnp.where(tails < 0, NO_EXPERT, tails + n_local * jnp.arange(n_group, dtype=I32)[:, None])[mine]

        def slices(e, source=None):
            return tuple(lax.dynamic_index_in_dim(w, e, axis=0, keepdims=False) for w in source or weights)

        def outgoing(r):
            s = my_sources[r]
            kind = jnp.maximum(s - n_local + 1, 0)
            return lax.switch(kind, [lambda: slices(jnp.minimum(s, n_local - 1))] + [lambda i=i: extras[i] for i in range(MOVES)])

        def one_round(r, carry):
            token, peer, rows, back, send, acc = carry
            peer_next = swapped(send)
            *picked, token = pick(r + 1 + token, table, starts, slot_t, x_loc, capacity)
            rows_next = spread(picked)
            out_rows, token = expert_ffn(r + token, my_sources, used, weights, extras, peer, rows)
            back_next = spread(out_rows)
            send_next, token = lax.optimization_barrier((outgoing(r[0] + 2 + token[0]), token))
            acc, token = mix(r - 1 + token, table, starts, slot, gate_te, back, acc, F32)
            return token, peer_next, rows_next, back_next, send_next, acc

        peer = swapped(slices(my_sources[0]))
        *picked, token = pick(jnp.zeros((1,), I32), table, starts, slot_t, x_loc, capacity)
        rows = spread(picked)
        later, token = lax.optimization_barrier((weights, token))
        extras = tuple(tuple(across(part, 1) for part in slices(moves[me, i] + token[0], later)) for i in range(MOVES))
        send, token = lax.optimization_barrier((outgoing(1 + token[0]), token))
        tail_rows = spread(pick_tail(tail_global + token, slot_t, x_loc))
        blank = tuple(jnp.zeros((capacity, d_model), BF16) for _ in range(n_group))
        carry = (token, peer, rows, blank, send, x_loc.astype(F32))
        tail_x = jnp.stack([rows.reshape(TAIL, TAIL_CAP, d_model) for rows in tail_rows], axis=1).reshape(TAIL, n_group * TAIL_CAP, d_model)
        half = d_model // n_data
        tail_mine = lax.dynamic_slice_in_dim(tail_x, q * half, half, axis=2)
        tail_peer = lax.ppermute(lax.dynamic_slice_in_dim(tail_x, (1 - q) * half, half, axis=2), "data", swap)

        odd = (n_round - 1) % 2
        carry = lax.fori_loop(0, odd, lambda i, c: one_round(jnp.full((1,), i, I32), c), carry)

        def two_rounds(i, c):
            r = jnp.full((1,), odd + 2 * i, I32)
            return one_round(r + 1, one_round(r, c))

        token, peer, rows, back, _, acc = lax.fori_loop(0, (n_round - 1) // 2, two_rounds, carry)
        last = jnp.full((1,), n_round - 1, I32)
        partial = tail_in(tail_local + token, jnp.stack([tail_mine, tail_peer]), wg_loc, wu_loc)
        partial, token = lax.optimization_barrier((partial, token))
        partial_sum = partial[0] + lax.ppermute(partial[1], "data", swap)
        out_last, token = expert_ffn(last + token, my_sources, used, weights, extras, peer, rows)
        back_last = spread(out_last)
        acc, token = mix(last - 1 + token, table, starts, slot, gate_te, back, acc, F32)
        ffn = wg_loc.shape[2]
        tail_h = (jax.nn.silu(partial_sum[..., :ffn]) * partial_sum[..., ffn:]).astype(BF16)
        tail_o = tail_out(tail_local + token, jnp.stack([tail_h, lax.ppermute(tail_h, "data", swap)]), wd_loc)
        other_half = lax.ppermute(tail_o[1], "data", swap)
        whole = jnp.where(q == 0, jnp.concatenate([tail_o[0], other_half], axis=2), jnp.concatenate([other_half, tail_o[0]], axis=2))
        whole = whole.reshape(TAIL, n_group, TAIL_CAP, d_model)
        tail_back = spread([whole[:, k].reshape(TAIL * TAIL_CAP, d_model) for k in range(n_group)])
        tail = (tail_global, jnp.concatenate(tail_back, axis=0))
        return mix(last + token, table, starts, slot, gate_te, back_last, acc, BF16, tail)[0]

    return jax.shard_map(device_body, mesh=mesh, in_specs=(tok_spec, tok_spec, tok_spec, wide_spec, wide_spec, down_spec), out_specs=tok_spec, check_vma=False)
```

time: 6210 us -> 2730 us (0.44)
  waiting for transfers between devices: 3500 us -> 1160 us
  local copies, waits for them, and re-layouts: 1690 us -> 186 us
  Pallas kernels: 0 us -> 1110 us
  matrix products: 646 us -> 0 us
  other arithmetic: 281 us -> 35.9 us
  starting transfers between devices: 49.9 us -> 151 us
    all_to_all x2 -> x0, waiting for transfers between devices: 2690 us -> none  [the longest x1 1350 us: device_step(): recv_rows = lax.all_to_all(send_rows, 'expert', 1, 1, tiled=True)]
    gather x3 -> x4, local copies, waits for them, and re-layouts: 1330 us -> 1.79 us  [the longest x2 0.66 us: device_body(): experts[mine]]
    ppermute x0 -> x106, waiting for transfers between devices: none -> 1160 us  [the longest x30 641 us: swapped(): return tuple((lax.ppermute(part, 'data', swap) for part in parts))]
    pallas_call x0 -> x35, Pallas kernels: none -> 1110 us  [the longest x11 460 us: mix(): pl.pallas_call(functools.partial(mix_body, bool(tail)), grid=(tok_rows //...]
    all_gather x3 -> x0, waiting for transfers between devices: 805 us -> none  [the longest x1 805 us: device_step(): wd_full = lax.all_gather(wd_loc, 'data', axis=2, tiled=True)]
    dot_general x3 -> x0, matrix products: 646 us -> none  [the longest x1 231 us: expert_ffn(): jnp.einsum('erd,edf->erf', expert_rows, w_up, preferred_element_type=jnp....]
    all_to_all x2 -> x0, local copies, waits for them, and re-layouts: 164 us -> none  [the longest x1 82 us: device_step(): recv_rows = lax.all_to_all(send_rows, 'expert', 1, 1, tiled=True)]
    reduce_sum x2 -> x3, other arithmetic: 161 us -> 0.78 us  [the longest x1 0.41 us: device_body(): used = jnp.sum(my_hot[:, None, :] * my_counts[None, :, :], axis=2)]
  transfers between devices with their start and end apart: 5 -> 106, of which waited for: 3 -> 40; matrix products, arithmetic and copies ran while one was open for 16% -> 7% of each run, Pallas kernels for 0% -> 33%
where the time goes in v1:
time: 2730 us; the launch traced here: 2710 us
  waiting for transfers between devices  1160 us (42%)
  Pallas kernels  1110 us (41%)
  local copies, waits for them, and re-layouts  186 us (7%)
  starting transfers between devices  151 us (6%)
  loops' own time  50.3 us (2%)
  other arithmetic  35.9 us (1%)
    ppermute x30, waiting for transfers between devices, swapped(): return tuple((lax.ppermute(part, 'data', swap) for part in parts))  641 us
    ppermute x72, waiting for transfers between devices, across(): return lax.ppermute(value, 'expert', [(p, p ^ k) for p in range(n_group)])  478 us
    pallas_call x11, Pallas kernels, mix(): pl.pallas_call(functools.partial(mix_body, bool(tail)), grid=(tok_rows //...  460 us
    pallas_call x10, Pallas kernels, expert_ffn(): pl.pallas_call(functools.partial(ffn_body, n_local), in_specs=[SMEM] * 3...  374 us
    pallas_call x10, Pallas kernels, pick(): pl.pallas_call(pick_body, grid=(tok_rows // TILE,), in_specs=[SMEM, SMEM,...  233 us
    squeeze x26, local copies, waits for them, and re-layouts, slices(): lax.dynamic_index_in_dim(w, e, axis=0, keepdims=False)  119 us
    ppermute x72, starting transfers between devices, across(): return lax.ppermute(value, 'expert', [(p, p ^ k) for p in range(n_group)])  113 us
  transfers between devices with their start and end apart: 106, of which 40 were waited for; matrix products, arithmetic and copies ran while one was open for 7% of the time, Pallas kernels for 33%

profile of v1, /device:TPU:0, one launch (start us, length us, event | category | flops | bytes accessed | tf_op | source)
XLA Modules:
  0.0 2713.3 jit_solution(10848809820741026115)
XLA Ops:
  214.3 59.7 %collective-permute-done.35 = bf16[1408,1024]{1,0:T(8,128)(2,1)} collective-permute-done((bf16[1408,1024]{1,0:T(8,128)(2,1)}, bf16[1408,1024]{1,0:T(8,128)(2,1)}, u32[]{:S(2)}, u32[]{:S(2)}) %collective-permute-start.35) | collective-permute-done | bytes 2883616 | tf_op jit(solution)/shard_map/ppermute | solution.py:446
  280.0 284.8 %while.89 = (s32[]{:T(128)}, s32[1]{0:T(128)}, bf16[1024,1408]{1,0:T(8,128)(2,1)}, bf16[1024,1408]{1,0:T(8,128)(2,1)}, bf16[1408,1024]{1,0:T(8,128)(2,1)}, /*ind...) while((s32[]{:T(128)}, s32[1]{0:T(128)}, ...), condition=%wide.region_16.17_spmd, body=%wide.region_12.16_spmd.sunk | while | flops 43822088192 | bytes 268436544 | solution.py:503
  306.3 51.7 %ffn.25 = (bf16[480,2048]{1,0:T(8,128)(2,1)}, bf16[480,2048]{1,0:T(8,128)(2,1)}, bf16[480,2048]{1,0:T(8,128)(2,1)}, bf16[480,2048]{1,0:T(8,128)(2,1)}, s32[1]{0:T(128)}) custom-call(s32[1]{0:T(128)S(6)} %add.573.r_ref, s32[20]{0:T(128)S(1)} %get-tuple-element.2614.src_ref, s32[20,4]{1,0:T(8,128)S(1)} %get-tuple-element.2615.used_ref, ...), custom_call_target="tpu_custom_call" | custom-call | flops 33218887680 | bytes 17301504 | tf_op jit(solution)/shard_map/while/body/ffn/pallas_call | solution.py:248
  489.5 61.0 %collective-permute-done.2 = bf16[1408,1024]{1,0:T(8,128)(2,1)} collective-permute-done((bf16[1408,1024]{1,0:T(8,128)(2,1)}, bf16[1408,1024]{1,0:T(8,128)(2,1)}, u32[]{:S(2)}, u32[]{:S(2)}) %collective-permute-start.2) | collective-permute-done | bytes 2883616 | tf_op jit(solution)/shard_map/while/body/ppermute | solution.py:446
  564.9 1867.7 %while.90 = (s32[]{:T(128)}, s32[1]{0:T(128)}, bf16[1024,1408]{1,0:T(8,128)(2,1)}, bf16[1024,1408]{1,0:T(8,128)(2,1)}, bf16[1408,1024]{1,0:T(8,128)(2,1)}, /*ind...) while((s32[]{:T(128)}, s32[1]{0:T(128)}, ...), condition=%wide.region_24.25_spmd, body=%wide.region_17.24_spmd.sunk | while | flops 87644176384 | bytes 424150464 | solution.py:509
  590.2 51.8 %ffn.26 = (bf16[480,2048]{1,0:T(8,128)(2,1)}, bf16[480,2048]{1,0:T(8,128)(2,1)}, bf16[480,2048]{1,0:T(8,128)(2,1)}, bf16[480,2048]{1,0:T(8,128)(2,1)}, s32[1]{0:T(128)}) custom-call(s32[1]{0:T(128)S(6)} %add.585.r_ref, s32[20]{0:T(128)S(1)} %get-tuple-element.2747.src_ref, s32[20,4]{1,0:T(8,128)S(1)} %get-tuple-element.2748.used_ref, ...), custom_call_target="tpu_custom_call" | custom-call | flops 33218887680 | bytes 17301504 | tf_op jit(solution)/shard_map/while/body/ffn/pallas_call | solution.py:248
  790.6 54.6 %collective-permute-done.11.refs_11_ = bf16[1408,1024]{1,0:T(8,128)(2,1)} collective-permute-done((bf16[1408,1024]{1,0:T(8,128)(2,1)}, bf16[1408,1024]{1,0:T(8,128)(2,1)}, u32[]{:S(2)}, u32[]{:S(2)}) %collective-permute-start.11) | collective-permute-done | bytes 2883616 | tf_op jit(solution)/shard_map/while/body/ppermute | solution.py:446
  845.2 51.7 %ffn.27 = (bf16[480,2048]{1,0:T(8,128)(2,1)}, bf16[480,2048]{1,0:T(8,128)(2,1)}, bf16[480,2048]{1,0:T(8,128)(2,1)}, bf16[480,2048]{1,0:T(8,128)(2,1)}, s32[1]{0:T(128)}) custom-call(s32[1]{0:T(128)S(6)} %add.591.r_ref, s32[20]{0:T(128)S(1)} %get-tuple-element.2747.src_ref, s32[20,4]{1,0:T(8,128)S(1)} %get-tuple-element.2748.used_ref, ...), custom_call_target="tpu_custom_call" | custom-call | flops 33218887680 | bytes 17301504 | tf_op jit(solution)/shard_map/while/body/ffn/pallas_call | solution.py:248
  968.8 60.6 %collective-permute-done.20 = bf16[1408,1024]{1,0:T(8,128)(2,1)} collective-permute-done((bf16[1408,1024]{1,0:T(8,128)(2,1)}, bf16[1408,1024]{1,0:T(8,128)(2,1)}, u32[]{:S(2)}, u32[]{:S(2)}) %collective-permute-start.20) | collective-permute-done | bytes 2883616 | tf_op jit(solution)/shard_map/while/body/ppermute | solution.py:446
  1056.2 51.7 %ffn.26 = (bf16[480,2048]{1,0:T(8,128)(2,1)}, bf16[480,2048]{1,0:T(8,128)(2,1)}, bf16[480,2048]{1,0:T(8,128)(2,1)}, bf16[480,2048]{1,0:T(8,128)(2,1)}, s32[1]{0:T(128)}) custom-call(s32[1]{0:T(128)S(6)} %add.585.r_ref, s32[20]{0:T(128)S(1)} %get-tuple-element.2747.src_ref, s32[20,4]{1,0:T(8,128)S(1)} %get-tuple-element.2748.used_ref, ...), custom_call_target="tpu_custom_call" | custom-call | flops 33218887680 | bytes 17301504 | tf_op jit(solution)/shard_map/while/body/ffn/pallas_call | solution.py:248
  1257.8 53.4 %collective-permute-done.11.refs_11_ = bf16[1408,1024]{1,0:T(8,128)(2,1)} collective-permute-done((bf16[1408,1024]{1,0:T(8,128)(2,1)}, bf16[1408,1024]{1,0:T(8,128)(2,1)}, u32[]{:S(2)}, u32[]{:S(2)}) %collective-permute-start.11) | collective-permute-done | bytes 2883616 | tf_op jit(solution)/shard_map/while/body/ppermute | solution.py:446
  1311.2 46.5 %ffn.27 = (bf16[480,2048]{1,0:T(8,128)(2,1)}, bf16[480,2048]{1,0:T(8,128)(2,1)}, bf16[480,2048]{1,0:T(8,128)(2,1)}, bf16[480,2048]{1,0:T(8,128)(2,1)}, s32[1]{0:T(128)}) custom-call(s32[1]{0:T(128)S(6)} %add.591.r_ref, s32[20]{0:T(128)S(1)} %get-tuple-element.2747.src_ref, s32[20,4]{1,0:T(8,128)S(1)} %get-tuple-element.2748.used_ref, ...), custom_call_target="tpu_custom_call" | custom-call | flops 33218887680 | bytes 17301504 | tf_op jit(solution)/shard_map/while/body/ffn/pallas_call | solution.py:248
  1434.7 60.7 %collective-permute-done.20 = bf16[1408,1024]{1,0:T(8,128)(2,1)} collective-permute-done((bf16[1408,1024]{1,0:T(8,128)(2,1)}, bf16[1408,1024]{1,0:T(8,128)(2,1)}, u32[]{:S(2)}, u32[]{:S(2)}) %collective-permute-start.20) | collective-permute-done | bytes 2883616 | tf_op jit(solution)/shard_map/while/body/ppermute | solution.py:446
  1682.2 42.4 %collective-permute-done.17.refs_3_ = bf16[480,2048]{1,0:T(8,128)(2,1)} collective-permute-done((bf16[480,2048]{1,0:T(8,128)(2,1)S(1)}, bf16[480,2048]{1,0:T(8,128)(2,1)}, u32[]{:S(2)}, u32[]{:S(2)}) %collective-permute-start.17) | collective-permute-done | bytes 1966112 | tf_op jit(solution)/shard_map/while/body/ppermute | solution.py:440
  1727.4 53.8 %collective-permute-done.11.refs_11_ = bf16[1408,1024]{1,0:T(8,128)(2,1)} collective-permute-done((bf16[1408,1024]{1,0:T(8,128)(2,1)}, bf16[1408,1024]{1,0:T(8,128)(2,1)}, u32[]{:S(2)}, u32[]{:S(2)}) %collective-permute-start.11) | collective-permute-done | bytes 2883616 | tf_op jit(solution)/shard_map/while/body/ppermute | solution.py:446
  1855.4 45.6 %mix.29 = (f32[4096,2048]{1,0:T(8,128)}, s32[1]{0:T(128)}) custom-call(s32[1]{0:T(128)S(6)} %add.595.r_ref, s32[21,4]{1,0:T(8,128)S(1)} %get-tuple-element.2743.tab_ref, s32[17,128]{1,0:T(8,128)S(1)} %get-tuple-element.2744.start_ref, s32[4096,128]{1,0:T(8,128)} %get-tuple-element.2758.slot_ref, ...), custom_call_target="tpu_custom_call", output_to_operand_aliasing={{0}: (9, {})} | custom-call | flops 8589934592 | bytes 67108864 | tf_op jit(solution)/shard_map/while/body/mix/pallas_call | solution.py:327
  1904.8 61.0 %collective-permute-done.20 = bf16[1408,1024]{1,0:T(8,128)(2,1)} collective-permute-done((bf16[1408,1024]{1,0:T(8,128)(2,1)}, bf16[1408,1024]{1,0:T(8,128)(2,1)}, u32[]{:S(2)}, u32[]{:S(2)}) %collective-permute-start.20) | collective-permute-done | bytes 2883616 | tf_op jit(solution)/shard_map/while/body/ppermute | solution.py:446
  2077.6 51.1 %mix.28 = (f32[4096,2048]{1,0:T(8,128)}, s32[1]{0:T(128)}) custom-call(s32[1]{0:T(128)S(6)} %add.589.r_ref, s32[21,4]{1,0:T(8,128)S(1)} %get-tuple-element.2743.tab_ref, s32[17,128]{1,0:T(8,128)S(1)} %get-tuple-element.2744.start_ref, s32[4096,128]{1,0:T(8,128)} %get-tuple-element.2758.slot_ref, ...), custom_call_target="tpu_custom_call", output_to_operand_aliasing={{0}: (9, {})} | custom-call | flops 8589934592 | bytes 67108864 | tf_op jit(solution)/shard_map/while/body/mix/pallas_call | solution.py:327
  2151.6 43.2 %collective-permute-done.17.refs_3_ = bf16[480,2048]{1,0:T(8,128)(2,1)} collective-permute-done((bf16[480,2048]{1,0:T(8,128)(2,1)S(1)}, bf16[480,2048]{1,0:T(8,128)(2,1)}, u32[]{:S(2)}, u32[]{:S(2)}) %collective-permute-start.17) | collective-permute-done | bytes 1966112 | tf_op jit(solution)/shard_map/while/body/ppermute | solution.py:440
  2197.8 48.7 %collective-permute-done.11.refs_11_ = bf16[1408,1024]{1,0:T(8,128)(2,1)} collective-permute-done((bf16[1408,1024]{1,0:T(8,128)(2,1)}, bf16[1408,1024]{1,0:T(8,128)(2,1)}, u32[]{:S(2)}, u32[]{:S(2)}) %collective-permute-start.11) | collective-permute-done | bytes 2883616 | tf_op jit(solution)/shard_map/while/body/ppermute | solution.py:446
  2321.1 43.9 %mix.29 = (f32[4096,2048]{1,0:T(8,128)}, s32[1]{0:T(128)}) custom-call(s32[1]{0:T(128)S(6)} %add.595.r_ref, s32[21,4]{1,0:T(8,128)S(1)} %get-tuple-element.2743.tab_ref, s32[17,128]{1,0:T(8,128)S(1)} %get-tuple-element.2744.start_ref, s32[4096,128]{1,0:T(8,128)} %get-tuple-element.2758.slot_ref, ...), custom_call_target="tpu_custom_call", output_to_operand_aliasing={{0}: (9, {})} | custom-call | flops 8589934592 | bytes 67108864 | tf_op jit(solution)/shard_map/while/body/mix/pallas_call | solution.py:327
  2370.1 61.0 %collective-permute-done.20 = bf16[1408,1024]{1,0:T(8,128)(2,1)} collective-permute-done((bf16[1408,1024]{1,0:T(8,128)(2,1)}, bf16[1408,1024]{1,0:T(8,128)(2,1)}, u32[]{:S(2)}, u32[]{:S(2)}) %collective-permute-start.20) | collective-permute-done | bytes 2883616 | tf_op jit(solution)/shard_map/while/body/ppermute | solution.py:446
  2578.7 83.2 %collective-permute-done.51 = bf16[48,2048]{1,0:T(8,128)(2,1)S(1)} collective-permute-done((bf16[48,2048]{1,0:T(8,128)(2,1)S(1)}, bf16[48,2048]{1,0:T(8,128)(2,1)S(1)}, u32[]{:S(2)}, u32[]{:S(2)}) %collective-permute-start.51) | collective-permute-done | bytes 196640 | tf_op jit(solution)/shard_map/ppermute | solution.py:440
  2668.5 44.3 %mix.26 = (bf16[4096,2048]{1,0:T(8,128)(2,1)}, s32[1]{0:T(128)}) custom-call(s32[1]{0:T(128)S(6)} %add.507.r_ref, s32[21,4]{1,0:T(8,128)S(1)} %get-tuple-element.2786, s32[17,128]{1,0:T(8,128)S(1)} %get-tuple-element.2788, s32[4096,128]{1,0:T(8,128)} %get-tuple-element.2780, f32[4096,128]{1,0:T(8,128)} %get-tuple-element.2782, ...), custom_call_target="tpu_custom_call" | custom-call | flops 8589934592 | bytes 67108864 | tf_op jit(solution)/shard_map/mix/pallas_call | solution.py:327
  (410 shorter events, 1573.4 us)
Async XLA Ops:
  87.2 186.7 %collective-permute-start.35 = (bf16[1408,1024]{1,0:T(8,128)(2,1)}, bf16[1408,1024]{1,0:T(8,128)(2,1)}, u32[]{:S(2)}, u32[]{:S(2)}) collective-permute-start(bf16[1408,1024]{1,0:T(8,128)(2,1)} %dynamic-slice_bitcast_fusion.12), channel_id=1, source_target_pairs={{0,4},{4,0},{1,5},{5,1},{2,6},{6,2},{3,7},{7,3}} | collective-permute-start | bytes 8650760 | tf_op jit(solution)/shard_map/ppermute | solution.py:446
  371.5 179.0 %collective-permute-start.2 = (bf16[1408,1024]{1,0:T(8,128)(2,1)}, bf16[1408,1024]{1,0:T(8,128)(2,1)}, u32[]{:S(2)}, u32[]{:S(2)}) collective-permute-start(bf16[1408,1024]{1,0:T(8,128)(2,1)} %copy.138), channel_id=1, source_target_pairs={{0,4},{4,0},{1,5},{5,1},{2,6},{6,2},{3,7},{7,3}} | collective-permute-start | bytes 8650760 | tf_op jit(solution)/shard_map/while/body/ppermute | solution.py:446
  674.9 170.3 %collective-permute-start.11 = (bf16[1408,1024]{1,0:T(8,128)(2,1)}, bf16[1408,1024]{1,0:T(8,128)(2,1)}, u32[]{:S(2)}, u32[]{:S(2)}) collective-permute-start(bf16[1408,1024]{1,0:T(8,128)(2,1)} %get-tuple-element.2694), channel_id=1, source_target_pairs={{0,4},{4,0},{1,5},{5,1},{2,6},{6,2},{3,7},{7,3}} | collective-permute-start | bytes 8650760 | tf_op jit(solution)/shard_map/while/body/ppermute | solution.py:446
  786.5 182.3 %collective-permute-start.19 = (bf16[1024,1408]{1,0:T(8,128)(2,1)}, bf16[1024,1408]{1,0:T(8,128)(2,1)}, u32[]{:S(2)}, u32[]{:S(2)}) collective-permute-start(bf16[1024,1408]{1,0:T(8,128)(2,1)} %get-tuple-element.2458), channel_id=1, source_target_pairs={{0,4},{4,0},{1,5},{5,1},{2,6},{6,2},{3,7},{7,3}} | collective-permute-start | bytes 8650760 | tf_op jit(solution)/shard_map/while/body/ppermute | solution.py:446
  786.7 242.7 %collective-permute-start.20 = (bf16[1408,1024]{1,0:T(8,128)(2,1)}, bf16[1408,1024]{1,0:T(8,128)(2,1)}, u32[]{:S(2)}, u32[]{:S(2)}) collective-permute-start(bf16[1408,1024]{1,0:T(8,128)(2,1)} %get-tuple-element.2459), channel_id=1, source_target_pairs={{0,4},{4,0},{1,5},{5,1},{2,6},{6,2},{3,7},{7,3}} | collective-permute-start | bytes 8650760 | tf_op jit(solution)/shard_map/while/body/ppermute | solution.py:446
  1121.9 133.4 %collective-permute-start.9 = (bf16[1024,1408]{1,0:T(8,128)(2,1)}, bf16[1024,1408]{1,0:T(8,128)(2,1)}, u32[]{:S(2)}, u32[]{:S(2)}) collective-permute-start(bf16[1024,1408]{1,0:T(8,128)(2,1)} %get-tuple-element.2692), channel_id=1, source_target_pairs={{0,4},{4,0},{1,5},{5,1},{2,6},{6,2},{3,7},{7,3}} | collective-permute-start | bytes 8650760 | tf_op jit(solution)/shard_map/while/body/ppermute | solution.py:446
  1123.2 134.1 %collective-permute-start.10 = (bf16[1024,1408]{1,0:T(8,128)(2,1)}, bf16[1024,1408]{1,0:T(8,128)(2,1)}, u32[]{:S(2)}, u32[]{:S(2)}) collective-permute-start(bf16[1024,1408]{1,0:T(8,128)(2,1)} %get-tuple-element.2693), channel_id=1, source_target_pairs={{0,4},{4,0},{1,5},{5,1},{2,6},{6,2},{3,7},{7,3}} | collective-permute-start | bytes 8650760 | tf_op jit(solution)/shard_map/while/body/ppermute | solution.py:446
  1140.9 170.3 %collective-permute-start.11 = (bf16[1408,1024]{1,0:T(8,128)(2,1)}, bf16[1408,1024]{1,0:T(8,128)(2,1)}, u32[]{:S(2)}, u32[]{:S(2)}) collective-permute-start(bf16[1408,1024]{1,0:T(8,128)(2,1)} %get-tuple-element.2694), channel_id=1, source_target_pairs={{0,4},{4,0},{1,5},{5,1},{2,6},{6,2},{3,7},{7,3}} | collective-permute-start | bytes 8650760 | tf_op jit(solution)/shard_map/while/body/ppermute | solution.py:446
  1255.3 179.5 %collective-permute-start.19 = (bf16[1024,1408]{1,0:T(8,128)(2,1)}, bf16[1024,1408]{1,0:T(8,128)(2,1)}, u32[]{:S(2)}, u32[]{:S(2)}) collective-permute-start(bf16[1024,1408]{1,0:T(8,128)(2,1)} %get-tuple-element.2458), channel_id=1, source_target_pairs={{0,4},{4,0},{1,5},{5,1},{2,6},{6,2},{3,7},{7,3}} | collective-permute-start | bytes 8650760 | tf_op jit(solution)/shard_map/while/body/ppermute | solution.py:446
  1255.3 240.2 %collective-permute-start.20 = (bf16[1408,1024]{1,0:T(8,128)(2,1)}, bf16[1408,1024]{1,0:T(8,128)(2,1)}, u32[]{:S(2)}, u32[]{:S(2)}) collective-permute-start(bf16[1408,1024]{1,0:T(8,128)(2,1)} %get-tuple-element.2459), channel_id=1, source_target_pairs={{0,4},{4,0},{1,5},{5,1},{2,6},{6,2},{3,7},{7,3}} | collective-permute-start | bytes 8650760 | tf_op jit(solution)/shard_map/while/body/ppermute | solution.py:446
  1357.7 137.8 %collective-permute-start.24 = (bf16[480,2048]{1,0:T(8,128)(2,1)}, bf16[480,2048]{1,0:T(8,128)(2,1)S(1)}, u32[]{:S(2)}, u32[]{:S(2)}) collective-permute-start(bf16[480,2048]{1,0:T(8,128)(2,1)} %get-tuple-element.2465), channel_id=1, source_target_pairs={{0,1},{1,0},{2,3},{3,2},{4,5},{5,4},{6,7},{7,6}} | collective-permute-start | bytes 5898248 | tf_op jit(solution)/shard_map/while/body/ppermute | solution.py:440
  1591.9 134.7 %collective-permute-start.9 = (bf16[1024,1408]{1,0:T(8,128)(2,1)}, bf16[1024,1408]{1,0:T(8,128)(2,1)}, u32[]{:S(2)}, u32[]{:S(2)}) collective-permute-start(bf16[1024,1408]{1,0:T(8,128)(2,1)} %get-tuple-element.2692), channel_id=1, source_target_pairs={{0,4},{4,0},{1,5},{5,1},{2,6},{6,2},{3,7},{7,3}} | collective-permute-start | bytes 8650760 | tf_op jit(solution)/shard_map/while/body/ppermute | solution.py:446
  1612.0 169.2 %collective-permute-start.11 = (bf16[1408,1024]{1,0:T(8,128)(2,1)}, bf16[1408,1024]{1,0:T(8,128)(2,1)}, u32[]{:S(2)}, u32[]{:S(2)}) collective-permute-start(bf16[1408,1024]{1,0:T(8,128)(2,1)} %get-tuple-element.2694), channel_id=1, source_target_pairs={{0,4},{4,0},{1,5},{5,1},{2,6},{6,2},{3,7},{7,3}} | collective-permute-start | bytes 8650760 | tf_op jit(solution)/shard_map/while/body/ppermute | solution.py:446
  1724.6 180.2 %collective-permute-start.19 = (bf16[1024,1408]{1,0:T(8,128)(2,1)}, bf16[1024,1408]{1,0:T(8,128)(2,1)}, u32[]{:S(2)}, u32[]{:S(2)}) collective-permute-start(bf16[1024,1408]{1,0:T(8,128)(2,1)} %get-tuple-element.2458), channel_id=1, source_target_pairs={{0,4},{4,0},{1,5},{5,1},{2,6},{6,2},{3,7},{7,3}} | collective-permute-start | bytes 8650760 | tf_op jit(solution)/shard_map/while/body/ppermute | solution.py:446
  1726.6 239.2 %collective-permute-start.20 = (bf16[1408,1024]{1,0:T(8,128)(2,1)}, bf16[1408,1024]{1,0:T(8,128)(2,1)}, u32[]{:S(2)}, u32[]{:S(2)}) collective-permute-start(bf16[1408,1024]{1,0:T(8,128)(2,1)} %get-tuple-element.2459), channel_id=1, source_target_pairs={{0,4},{4,0},{1,5},{5,1},{2,6},{6,2},{3,7},{7,3}} | collective-permute-start | bytes 8650760 | tf_op jit(solution)/shard_map/while/body/ppermute | solution.py:446
  1812.8 153.0 %collective-permute-start.24 = (bf16[480,2048]{1,0:T(8,128)(2,1)}, bf16[480,2048]{1,0:T(8,128)(2,1)S(1)}, u32[]{:S(2)}, u32[]{:S(2)}) collective-permute-start(bf16[480,2048]{1,0:T(8,128)(2,1)} %get-tuple-element.2465), channel_id=1, source_target_pairs={{0,1},{1,0},{2,3},{3,2},{4,5},{5,4},{6,7},{7,6}} | collective-permute-start | bytes 5898248 | tf_op jit(solution)/shard_map/while/body/ppermute | solution.py:440
  1826.3 139.5 %collective-permute-start.25 = (bf16[480,2048]{1,0:T(8,128)(2,1)}, bf16[480,2048]{1,0:T(8,128)(2,1)}, u32[]{:S(2)}, u32[]{:S(2)}) collective-permute-start(bf16[480,2048]{1,0:T(8,128)(2,1)} %get-tuple-element.2466), channel_id=1, source_target_pairs={{0,2},{1,3},{2,0},{3,1},{4,6},{5,7},{6,4},{7,5}} | collective-permute-start | bytes 5898248 | tf_op jit(solution)/shard_map/while/body/ppermute | solution.py:440
  2057.2 139.6 %collective-permute-start.9 = (bf16[1024,1408]{1,0:T(8,128)(2,1)}, bf16[1024,1408]{1,0:T(8,128)(2,1)}, u32[]{:S(2)}, u32[]{:S(2)}) collective-permute-start(bf16[1024,1408]{1,0:T(8,128)(2,1)} %get-tuple-element.2692), channel_id=1, source_target_pairs={{0,4},{4,0},{1,5},{5,1},{2,6},{6,2},{3,7},{7,3}} | collective-permute-start | bytes 8650760 | tf_op jit(solution)/shard_map/while/body/ppermute | solution.py:446
  2058.6 139.2 %collective-permute-start.10 = (bf16[1024,1408]{1,0:T(8,128)(2,1)}, bf16[1024,1408]{1,0:T(8,128)(2,1)}, u32[]{:S(2)}, u32[]{:S(2)}) collective-permute-start(bf16[1024,1408]{1,0:T(8,128)(2,1)} %get-tuple-element.2693), channel_id=1, source_target_pairs={{0,4},{4,0},{1,5},{5,1},{2,6},{6,2},{3,7},{7,3}} | collective-permute-start | bytes 8650760 | tf_op jit(solution)/shard_map/while/body/ppermute | solution.py:446
  2076.3 170.2 %collective-permute-start.11 = (bf16[1408,1024]{1,0:T(8,128)(2,1)}, bf16[1408,1024]{1,0:T(8,128)(2,1)}, u32[]{:S(2)}, u32[]{:S(2)}) collective-permute-start(bf16[1408,1024]{1,0:T(8,128)(2,1)} %get-tuple-element.2694), channel_id=1, source_target_pairs={{0,4},{4,0},{1,5},{5,1},{2,6},{6,2},{3,7},{7,3}} | collective-permute-start | bytes 8650760 | tf_op jit(solution)/shard_map/while/body/ppermute | solution.py:446
  2195.8 174.3 %collective-permute-start.19 = (bf16[1024,1408]{1,0:T(8,128)(2,1)}, bf16[1024,1408]{1,0:T(8,128)(2,1)}, u32[]{:S(2)}, u32[]{:S(2)}) collective-permute-start(bf16[1024,1408]{1,0:T(8,128)(2,1)} %get-tuple-element.2458), channel_id=1, source_target_pairs={{0,4},{4,0},{1,5},{5,1},{2,6},{6,2},{3,7},{7,3}} | collective-permute-start | bytes 8650760 | tf_op jit(solution)/shard_map/while/body/ppermute | solution.py:446
  2196.8 234.3 %collective-permute-start.20 = (bf16[1408,1024]{1,0:T(8,128)(2,1)}, bf16[1408,1024]{1,0:T(8,128)(2,1)}, u32[]{:S(2)}, u32[]{:S(2)}) collective-permute-start(bf16[1408,1024]{1,0:T(8,128)(2,1)} %get-tuple-element.2459), channel_id=1, source_target_pairs={{0,4},{4,0},{1,5},{5,1},{2,6},{6,2},{3,7},{7,3}} | collective-permute-start | bytes 8650760 | tf_op jit(solution)/shard_map/while/body/ppermute | solution.py:446
  2259.7 171.4 %collective-permute-start.24 = (bf16[480,2048]{1,0:T(8,128)(2,1)}, bf16[480,2048]{1,0:T(8,128)(2,1)S(1)}, u32[]{:S(2)}, u32[]{:S(2)}) collective-permute-start(bf16[480,2048]{1,0:T(8,128)(2,1)} %get-tuple-element.2465), channel_id=1, source_target_pairs={{0,1},{1,0},{2,3},{3,2},{4,5},{5,4},{6,7},{7,6}} | collective-permute-start | bytes 5898248 | tf_op jit(solution)/shard_map/while/body/ppermute | solution.py:440
  2290.7 140.4 %collective-permute-start.25 = (bf16[480,2048]{1,0:T(8,128)(2,1)}, bf16[480,2048]{1,0:T(8,128)(2,1)}, u32[]{:S(2)}, u32[]{:S(2)}) collective-permute-start(bf16[480,2048]{1,0:T(8,128)(2,1)} %get-tuple-element.2466), channel_id=1, source_target_pairs={{0,2},{1,3},{2,0},{3,1},{4,6},{5,7},{6,4},{7,5}} | collective-permute-start | bytes 5898248 | tf_op jit(solution)/shard_map/while/body/ppermute | solution.py:440
  (104 other events, 8412.0 us)

commit v2 on v1

v2 whole, which is shorter than its diff:
```python
import functools

import jax
import jax.numpy as jnp
from jax import lax
from jax.experimental import pallas as pl
from jax.experimental.pallas import tpu as pltpu
from jax.sharding import PartitionSpec as P


LANES = 128
NO_EXPERT = LANES - 1
TILE = 256
WINDOW = 128
MIX_WINDOW = 64
MIX_STRIP = 512
AHEAD = 4
MOVES = 2
LIGHT = 160
TAIL, TAIL_CAP = 3, 16
BF16, F32, I32 = jnp.bfloat16, jnp.float32, jnp.int32
ANY = pl.BlockSpec(memory_space=pl.ANY)
SMEM = pl.BlockSpec(memory_space=pltpu.SMEM)
VMEM_LIMIT = 62 * 1024 * 1024
TOKEN = jax.ShapeDtypeStruct((1,), I32)


def capacity_rows(tok_rows, top_k, n_exp):
    return max(8, ((5 * top_k * tok_rows) // (4 * n_exp) + 7) // 8 * 8)


def params(n_axes=0):
    return pltpu.CompilerParams(dimension_semantics=("arbitrary",) * n_axes if n_axes else None, vmem_limit_bytes=VMEM_LIMIT)


def cost(flops, bytes_accessed):
    return pl.CostEstimate(flops=flops, bytes_accessed=bytes_accessed, transcendentals=0)


def route_body(capacity, ids_ref, gate_ref, pieces_ref, slot_t_ref, start_ref, count_ref, seen):
    @pl.when(pl.program_id(0) == 0)
    def _():
        seen[...] = jnp.zeros_like(seen)

    top_k, tile = ids_ref.shape[0], TILE
    tokens = pl.ds(pl.multiple_of(pl.program_id(0) * TILE, TILE), TILE)
    ids, gates = ids_ref[:, tokens], gate_ref[:, tokens]
    expert = lax.broadcasted_iota(I32, (LANES, tile), 0)
    mask = jnp.zeros((LANES, tile), F32)
    gate_t = jnp.zeros((LANES, tile), F32)
    for j in range(top_k):
        hit = ids[j : j + 1, :] == expert
        mask = jnp.where(hit, 1.0, mask)
        gate_t = jnp.where(hit, gates[j : j + 1, :], gate_t)
    before = lax.broadcasted_iota(I32, (tile, tile), 0) < lax.broadcasted_iota(I32, (tile, tile), 1)
    earlier = jnp.dot(mask.astype(BF16), jnp.where(before, 1.0, 0.0).astype(BF16), preferred_element_type=F32) + seen[:, 0:1]
    slot = jnp.where((mask > 0.0) & (earlier < capacity), earlier, -1.0)
    slot_t_ref[...] = slot.astype(I32)
    slot = slot.T
    high = jnp.floor(slot * (1.0 / 16.0))
    pieces = [high.astype(BF16), (slot - 16.0 * high).astype(BF16)]
    rest = gate_t.T
    for _ in range(3):
        piece = rest.astype(BF16)
        rest = rest - piece.astype(F32)
        pieces.append(piece)
    for i, piece in enumerate(pieces):
        pieces_ref[:, i * LANES : (i + 1) * LANES] = piece
    start_ref[0] = jnp.minimum(seen[...].T[:8], capacity).astype(I32)
    seen[...] = seen[...] + jnp.sum(mask, axis=1, keepdims=True)
    count_ref[...] = jnp.minimum(seen[...].T[:8], capacity).astype(I32)


def route(ids_t, gate_t, capacity):
    top_k, tok_rows = ids_t.shape
    n_tiles = tok_rows // TILE
    return pl.pallas_call(
        functools.partial(route_body, capacity),
        grid=(n_tiles,),
        in_specs=[pl.BlockSpec((top_k, tok_rows), lambda i: (0, 0))] * 2,
        out_specs=[
            pl.BlockSpec((TILE, 5 * LANES), lambda i: (i, 0)),
            pl.BlockSpec((LANES, TILE), lambda i: (0, i)),
            pl.BlockSpec((1, 8, LANES), lambda i: (i, 0, 0)),
            pl.BlockSpec((8, LANES), lambda i: (0, 0)),
        ],
        out_shape=[
            jax.ShapeDtypeStruct((tok_rows, 5 * LANES), BF16),
            jax.ShapeDtypeStruct((LANES, tok_rows), I32),
            jax.ShapeDtypeStruct((n_tiles, 8, LANES), I32),
            jax.ShapeDtypeStruct((8, LANES), I32),
        ],
        scratch_shapes=[pltpu.VMEM((LANES, LANES), F32)],
        compiler_params=params(1),
        name="route",
    )(ids_t, gate_t)


def windows(start_ref, tile, e, width):
    lo, hi = start_ref[tile, e], start_ref[tile + 1, e]
    floor = lo // 16 * 16
    return floor, jnp.where(hi > lo, (hi - floor + width - 1) // width, 0)


def stream_rows(tile, x_hbm, x_buf, sem):
    def copy(i):
        at = pl.ds(pl.multiple_of(i * TILE, TILE), TILE)
        return pltpu.make_async_copy(x_hbm.at[at], x_buf.at[at], sem.at[i])

    @pl.when(tile == 0)
    def _():
        @pl.loop(0, pl.num_programs(0))
        def _(i):
            copy(i).start()

    copy(tile).wait()
    return x_buf.at[pl.ds(pl.multiple_of(tile * TILE, TILE), TILE)]


def pick_body(r_ref, tab_ref, start_ref, slot_t_ref, x_hbm, *refs):
    *outs, token, picked, sem, x_buf, x_sem = refs
    n_pick, capacity, _ = picked.shape
    tile = pl.program_id(0)
    token[0] = 0

    x_ref = stream_rows(tile, x_hbm, x_buf, x_sem)

    @pl.when(tile == 0)
    def _():
        picked[...] = jnp.zeros_like(picked)

    @pl.loop(0, n_pick)
    def _(k):
        e = tab_ref[r_ref[0] + 1, k]
        floor, n_win = windows(start_ref, tile, e, WINDOW)

        @pl.loop(0, n_win)
        def _(w):
            first = floor + w * WINDOW
            base = pl.multiple_of(jnp.minimum(first, capacity - WINDOW), 16)
            slots = slot_t_ref[pl.ds(e, 1), :]
            row = lax.broadcasted_iota(I32, (WINDOW, TILE), 0) + base
            hot = jnp.where((row == slots) & (slots >= first), 1.0, 0.0).astype(BF16)
            picked[k, pl.ds(base, WINDOW), :] += jnp.dot(hot, x_ref[...], preferred_element_type=F32).astype(BF16)

    @pl.when(tile == pl.num_programs(0) - 1)
    def _():
        copies = [pltpu.make_async_copy(picked.at[k], out, sem.at[k]) for k, out in enumerate(outs)]
        for copy in copies:
            copy.start()
        for copy in copies:
            copy.wait()


def pick(r, table, starts, slot_t, x_loc, capacity):
    n_pick = table.shape[1]
    tok_rows, d_model = x_loc.shape
    return pl.pallas_call(
        pick_body,
        grid=(tok_rows // TILE,),
        in_specs=[
            SMEM,
            SMEM,
            SMEM,
            pl.BlockSpec((LANES, TILE), lambda i: (0, i)),
            ANY,
        ],
        out_specs=[ANY] * n_pick + [SMEM],
        out_shape=[jax.ShapeDtypeStruct((capacity, d_model), BF16)] * n_pick + [TOKEN],
        scratch_shapes=[
            pltpu.VMEM((n_pick, capacity, d_model), BF16),
            pltpu.SemaphoreType.DMA((n_pick,)),
            pltpu.VMEM((tok_rows, d_model), BF16),
            pltpu.SemaphoreType.DMA((tok_rows // TILE,)),
        ],
        compiler_params=params(1),
        cost_estimate=cost(2 * n_pick * capacity * TILE * d_model, 2 * tok_rows * d_model),
        name="pick",
    )(r, table, starts, slot_t, x_loc)


def pick_tail_body(tail_ref, slot_t_ref, x_hbm, *refs):
    *outs, x_buf, x_sem = refs
    tile = pl.program_id(0)
    x_ref = stream_rows(tile, x_hbm, x_buf, x_sem)
    n_tail = tail_ref.shape[1]
    group = n_tail * TAIL_CAP
    hots = []
    for k in range(len(outs)):
        for i in range(n_tail):
            row = lax.broadcasted_iota(I32, (TAIL_CAP, x_ref.shape[0]), 0)
            hots.append(jnp.where(row == slot_t_ref[pl.ds(tail_ref[k, i], 1), :], 1.0, 0.0).astype(BF16))
    picked = jnp.dot(jnp.concatenate(hots, axis=0), x_ref[...], preferred_element_type=F32).astype(BF16)

    @pl.when(tile == 0)
    def _():
        for out in outs:
            out[...] = jnp.zeros_like(out)

    for k, out in enumerate(outs):
        out[...] += picked[k * group : (k + 1) * group]


def pick_tail(tail, slot_t, x_loc):
    n_pos, n_tail = tail.shape
    tok_rows, d_model = x_loc.shape
    group = n_tail * TAIL_CAP
    return pl.pallas_call(
        pick_tail_body,
        grid=(tok_rows // TILE,),
        in_specs=[SMEM, pl.BlockSpec((LANES, TILE), lambda i: (0, i)), ANY],
        out_specs=[pl.BlockSpec((group, d_model), lambda i: (0, 0))] * n_pos,
        scratch_shapes=[pltpu.VMEM((tok_rows, d_model), BF16), pltpu.SemaphoreType.DMA((tok_rows // TILE,))],
        out_shape=[jax.ShapeDtypeStruct((group, d_model), BF16)] * n_pos,
        compiler_params=params(1),
        cost_estimate=cost(2 * n_pos * group * tok_rows * d_model, 2 * tok_rows * d_model),
        name="pick_tail",
    )(tail, slot_t, x_loc)


def ffn_body(n_local, r_ref, src_ref, used_ref, *refs):
    n_src = 1 + MOVES
    own, (pg, pu, pd) = refs[: 3 * n_src], refs[3 * n_src : 3 * n_src + 3]
    refs = refs[3 * n_src + 3 :]
    n_rows = used_ref.shape[1]
    rows, outs, token = refs[:n_rows], refs[n_rows : 2 * n_rows], refs[2 * n_rows]
    x_buf, w_in, w_out, o_buf, x_sem, w_sem, o_sem = refs[2 * n_rows + 1 :]
    half, ffn = pg.shape
    q = lax.axis_index("data")
    r = r_ref[0]
    src = src_ref[r]
    token[0] = 0

    def load(place, parts, first):
        at = pl.ds(pl.multiple_of(place * half, half), half)
        places = (w_in.at[at, pl.ds(0, ffn)], w_in.at[at, pl.ds(ffn, ffn)], w_out.at[:, at])
        return [pltpu.make_async_copy(part, dst, w_sem.at[first + i]) for i, (part, dst) in enumerate(zip(parts, places))]

    row_loads = [pltpu.make_async_copy(rows[i], x_buf.at[i], x_sem.at[i]) for i in range(n_rows)]
    row_loads[0].start()
    theirs = load(1 - q, (pg, pu, pd), 3)
    for copy in theirs[:2]:
        copy.start()
    for s in range(n_src):
        @pl.when(jnp.maximum(src - n_local + 1, 0) == s)
        def _():
            parts = own[3 * s : 3 * s + 3]
            for copy in load(q, [part.at[jnp.minimum(src, n_local - 1)] for part in parts] if s == 0 else parts, 0):
                copy.start()
    theirs[2].start()
    for copy in row_loads[1:]:
        copy.start()
    ours = load(q, (pg, pu, pd), 0)
    for copy in row_loads + ours + theirs:
        copy.wait()

    part = LIGHT
    n_part = x_buf.shape[1] // part

    @pl.loop(0, n_rows)
    def _(i):
        @pl.loop(0, n_part)
        def _(j):
            at = pl.ds(pl.multiple_of(j * part, part), part)

            @pl.when(used_ref[r, i] > j * part)
            def _():
                act = jnp.dot(x_buf[i, at], w_in[...], preferred_element_type=F32)
                gate_act, up_act = act[:, :ffn], act[:, ffn:]
                hidden = (jax.nn.silu(gate_act) * up_act).astype(BF16)
                o_buf[i, at] = jnp.dot(hidden, w_out[...], preferred_element_type=F32).astype(BF16)

            @pl.when(used_ref[r, i] <= j * part)
            def _():
                o_buf[i, at] = jnp.zeros((part, o_buf.shape[2]), BF16)

        for s in range(n_rows):
            @pl.when(i == s)
            def _():
                pltpu.make_async_copy(o_buf.at[s], outs[s], o_sem.at[s]).start()

    for s in range(n_rows):
        pltpu.make_async_copy(o_buf.at[s], outs[s], o_sem.at[s]).wait()


def expert_ffn(r, sources, used, weights, extras, peer, rows):
    capacity, d_model = rows[0].shape
    n_local, half, ffn = weights[0].shape
    n_rows = len(rows)
    own = list(weights) + [part for extra in extras for part in extra]
    out = pl.pallas_call(
        functools.partial(ffn_body, n_local),
        in_specs=[SMEM] * 3 + [ANY] * (len(own) + 3 + n_rows),
        out_specs=[ANY] * n_rows + [SMEM],
        out_shape=[jax.ShapeDtypeStruct((capacity, d_model), BF16)] * n_rows + [TOKEN],
        scratch_shapes=[
            pltpu.VMEM((n_rows, capacity, d_model), BF16),
            pltpu.VMEM((2 * half, 2 * ffn), BF16),
            pltpu.VMEM((ffn, d_model), BF16),
            pltpu.VMEM((n_rows, capacity, d_model), BF16),
            pltpu.SemaphoreType.DMA((n_rows,)),
            pltpu.SemaphoreType.DMA((6,)),
            pltpu.SemaphoreType.DMA((n_rows,)),
        ],
        compiler_params=params(),
        cost_estimate=cost(6 * n_rows * capacity * d_model * ffn, 6 * d_model * ffn),
        name="ffn",
    )(r, sources, used, *own, *peer, *rows)
    return tuple(out[:n_rows]), out[n_rows]


def choose(ids, width):
    shape = (LANES, len(ids) * width)
    group = lax.broadcasted_iota(I32, shape, 1) // width
    wanted = jnp.full(shape, NO_EXPERT, I32)
    for i, e in enumerate(ids):
        wanted = jnp.where(group == i, e, wanted)
    return jnp.where(lax.broadcasted_iota(I32, shape, 0) == wanted, 1.0, 0.0).astype(BF16)


def chosen(pieces_ref, select):
    stacked = jnp.concatenate([pieces_ref[:, i * LANES : (i + 1) * LANES] for i in range(5)], axis=0)
    picked = jnp.dot(stacked, select, preferred_element_type=F32)
    high, low, *gates = [picked[i * TILE : (i + 1) * TILE] for i in range(5)]
    return 16.0 * high + low, gates


def weigh(hot, gates):
    return [jnp.where(hot, gate, 0.0).astype(BF16) for gate in gates]


def add_rows(out_ref, base_ref, terms):
    @pl.loop(0, out_ref.shape[1] // MIX_STRIP)
    def _(n):
        at = pl.ds(pl.multiple_of(n * MIX_STRIP, MIX_STRIP), MIX_STRIP)
        strip = base_ref[:, at]
        for weights, rows in terms:
            part = rows(at)
            strip = strip + sum(jnp.dot(weight, part, preferred_element_type=F32) for weight in weights)
        out_ref[:, at] = strip.astype(out_ref.dtype)


def mix_body(n_sets, has_tail, r_ref, tab_ref, start_ref, pieces_ref, acc_hbm, *refs):
    tails, refs = (refs[:2], refs[2:]) if has_tail else ((), refs)
    n_pos = tab_ref.shape[1]
    n_groups = n_sets * n_pos
    rows, (out_ref, token, total, select, sem, acc_buf, acc_sem, *held) = refs[:n_groups], refs[n_groups:]
    tile, n_tiles = pl.program_id(0), pl.num_programs(0)
    groups = [(held[g // n_pos].at[g % n_pos], tab_ref[r_ref[g // n_pos] + 1, g % n_pos]) for g in range(n_groups)]
    copies = [pltpu.make_async_copy(row, spot, sem.at[g]) for g, (row, (spot, _)) in enumerate(zip(rows, groups))]
    tail_ids = [tails[0][k, i] for k in range(tails[0].shape[0]) for i in range(tails[0].shape[1])] if has_tail else []
    n_main = n_groups * MIX_WINDOW

    def fetch(i):
        spot = lax.rem(i, AHEAD)
        return pltpu.make_async_copy(acc_hbm.at[pl.ds(pl.multiple_of(i * TILE, TILE), TILE)], acc_buf.at[spot], acc_sem.at[spot])

    @pl.when(tile == 0)
    def _():
        for copy in copies:
            copy.start()
        for i in range(AHEAD - 1):
            fetch(i).start()
        select[:, :n_main] = choose([e for _, e in groups], MIX_WINDOW)
        if has_tail:
            select[:, n_main:] = choose(tail_ids, TAIL_CAP)
        for copy in copies:
            copy.wait()

    @pl.when(tile + AHEAD - 1 < n_tiles)
    def _():
        fetch(tile + AHEAD - 1).start()

    fetch(tile).wait()
    acc_ref = acc_buf.at[lax.rem(tile, AHEAD)]
    token[0] = 0
    floors, counts = zip(*[windows(start_ref, tile, e, MIX_WINDOW) for _, e in groups])
    n_pass = functools.reduce(jnp.maximum, counts)
    column = lax.broadcasted_iota(I32, (1, n_main), 1)

    def term(w, slots, gates):
        firsts = [floor + w * MIX_WINDOW for floor in floors]
        bases = [pl.multiple_of(jnp.minimum(first, spot.shape[0] - MIX_WINDOW), 16) for first, (spot, _) in zip(firsts, groups)]
        first, place = jnp.zeros_like(column), column % MIX_WINDOW
        for g in range(n_groups):
            mine = column // MIX_WINDOW == g
            first = jnp.where(mine, firsts[g], first)
            place = jnp.where(mine, place + bases[g], place)
        hot = (slots == place.astype(F32)) & (slots >= first.astype(F32))
        return weigh(hot, gates), lambda at: jnp.concatenate([spot[pl.ds(base, MIX_WINDOW), at] for base, (spot, _) in zip(bases, groups)], axis=0)

    slots, gates = chosen(pieces_ref, select[...])
    terms = []
    if has_tail:
        tail_slots = slots[:, n_main:]
        place = lax.broadcasted_iota(I32, tail_slots.shape, 1) % TAIL_CAP
        terms.append((weigh(tail_slots == place.astype(F32), [gate[:, n_main:] for gate in gates]), lambda at: tails[1][:, at]))
    slots, gates = slots[:, :n_main], [gate[:, :n_main] for gate in gates]
    terms.append(term(0, slots, gates))

    @pl.when(n_pass <= 1)
    def _():
        add_rows(out_ref, acc_ref, terms)

    @pl.when(n_pass > 1)
    def _():
        add_rows(total, acc_ref, terms)

        @pl.loop(1, n_pass)
        def _(w):
            add_rows(total, total, [term(w, slots, gates)])

        out_ref[...] = total[...].astype(out_ref.dtype)


def mix(r, table, starts, pieces, sets, acc, out_dtype, tail=()):
    tok_rows, d_model = acc.shape
    rows = [row for group in sets for row in group]
    wide = pl.BlockSpec((TILE, d_model), lambda i: (i, 0))
    n_columns = len(rows) * MIX_WINDOW + (tail[1].shape[0] if tail else 0)
    return pl.pallas_call(
        functools.partial(mix_body, len(sets), bool(tail)),
        grid=(tok_rows // TILE,),
        in_specs=[
            SMEM,
            SMEM,
            SMEM,
            pl.BlockSpec((TILE, 5 * LANES), lambda i: (i, 0)),
            ANY,
            *([SMEM, pl.BlockSpec(tail[1].shape, lambda i: (0, 0))] if tail else []),
            *[ANY] * len(rows),
        ],
        out_specs=[wide, SMEM],
        scratch_shapes=[
            pltpu.VMEM((TILE, d_model), F32),
            pltpu.VMEM((LANES, n_columns), BF16),
            pltpu.SemaphoreType.DMA((len(rows),)),
            pltpu.VMEM((AHEAD, TILE, d_model), F32),
            pltpu.SemaphoreType.DMA((AHEAD,)),
            *[pltpu.VMEM((len(group), *group[0].shape), BF16) for group in sets],
        ],
        out_shape=[jax.ShapeDtypeStruct((tok_rows, d_model), out_dtype), TOKEN],
        input_output_aliases={4: 0} if acc.dtype == out_dtype else {},
        compiler_params=params(1),
        cost_estimate=cost(2 * len(rows) * tok_rows * WINDOW * d_model, 8 * tok_rows * d_model),
        name="mix",
    )(r, table, starts, pieces, acc, *tail, *rows)


def unset_body(*refs):
    pass


def unset(*shapes):
    return pl.pallas_call(unset_body, out_specs=[ANY] * len(shapes), out_shape=list(shapes), name="unset")()


def tail_in_body(idx_ref, mine_ref, peer_ref, wg_ref, wu_ref, mine_out, peer_out):
    rows, ffn = mine_ref.shape[1], wg_ref.shape[2]
    x = jnp.concatenate([mine_ref[0], peer_ref[0]], axis=0)
    for w_ref, first in ((wg_ref, 0), (wu_ref, ffn)):
        part = jnp.dot(x, w_ref[0], preferred_element_type=F32)
        mine_out[0, :, first : first + ffn] = part[:rows]
        peer_out[0, :, first : first + ffn] = part[rows:]


def tail_in(idx, mine, peer, w_gate, w_up):
    n_tail, rows, half = mine.shape
    ffn = w_gate.shape[2]
    weight = pl.BlockSpec((1, half, ffn), lambda i, idx: (idx[i], 0, 0))
    x_spec = pl.BlockSpec((1, rows, half), lambda i, idx: (i, 0, 0))
    return pl.pallas_call(
        tail_in_body,
        grid_spec=pltpu.PrefetchScalarGridSpec(
            num_scalar_prefetch=1,
            grid=(n_tail,),
            in_specs=[x_spec, x_spec, weight, weight],
            out_specs=[pl.BlockSpec((1, rows, 2 * ffn), lambda i, idx: (i, 0, 0))] * 2,
        ),
        out_shape=[jax.ShapeDtypeStruct((n_tail, rows, 2 * ffn), F32)] * 2,
        compiler_params=params(1),
        cost_estimate=cost(8 * n_tail * rows * half * ffn, 4 * n_tail * half * ffn),
        name="tail_in",
    )(idx, mine, peer, w_gate, w_up)


def tail_out_body(idx_ref, mine_ref, peer_ref, wd_ref, mine_out, peer_out):
    rows = mine_ref.shape[1]
    out = jnp.dot(jnp.concatenate([mine_ref[0], peer_ref[0]], axis=0), wd_ref[0], preferred_element_type=F32).astype(BF16)
    mine_out[0] = out[:rows]
    peer_out[0] = out[rows:]


def tail_out(idx, mine, peer, w_down):
    n_tail, rows, ffn = mine.shape
    half = w_down.shape[2]
    h_spec = pl.BlockSpec((1, rows, ffn), lambda i, idx: (i, 0, 0))
    return pl.pallas_call(
        tail_out_body,
        grid_spec=pltpu.PrefetchScalarGridSpec(
            num_scalar_prefetch=1,
            grid=(n_tail,),
            in_specs=[h_spec, h_spec, pl.BlockSpec((1, ffn, half), lambda i, idx: (idx[i], 0, 0))],
            out_specs=[pl.BlockSpec((1, rows, half), lambda i, idx: (i, 0, 0))] * 2,
        ),
        out_shape=[jax.ShapeDtypeStruct((n_tail, rows, half), BF16)] * 2,
        compiler_params=params(1),
        cost_estimate=cost(4 * n_tail * rows * half * ffn, 2 * n_tail * half * ffn),
        name="tail_out",
    )(idx, mine, peer, w_down)


def plan(counts, n_group):
    load = jnp.max(counts, axis=0).reshape(n_group, -1)
    n_local = load.shape[1]
    ids = jnp.arange(n_local, dtype=I32)
    ahead = (load[:, None, :] > load[:, :, None]) | ((load[:, None, :] == load[:, :, None]) & (ids[None, None, :] < ids[None, :, None]))
    rank = jnp.sum(ahead.astype(I32), axis=2)
    active = jnp.sum((load > 0).astype(I32), axis=1)
    tail = jnp.minimum(jnp.sum(((load > 0) & (load <= TAIL_CAP)).astype(I32), axis=1), TAIL)
    full = active - tail
    position = jnp.arange(n_group, dtype=I32)
    per_chip = jnp.max(jnp.sum(full.reshape(-1, 2), axis=1))
    least = (per_chip + 1) // 2
    limit = jnp.where(least >= MOVES + 2, MOVES, 0)
    n_round = jnp.maximum(jnp.maximum(least, jnp.max(full) - limit), 1)
    half = ((per_chip == 2 * n_round - 1) & (jnp.max(full * (position % 2)) - limit < n_round)).astype(I32)
    skip = half * (position % 2)
    give = jnp.clip(full - (n_round - skip), 0, limit)
    keep = full - give
    partner_keep = keep.reshape(-1, 2)[:, ::-1].reshape(-1)
    position = position[:, None]
    kept = rank < keep[:, None]
    in_round = rank < full[:, None]
    to = jnp.where(kept, position, position ^ 1)
    at = jnp.where(kept, rank + skip[:, None], jnp.maximum(partner_keep[:, None] + half * (1 - position % 2), 2) + rank - keep[:, None])
    source = jnp.where(kept, ids[None, :], n_local + rank - keep[:, None])
    tail_at = jnp.where((rank >= full[:, None]) & (rank < active[:, None]), rank - full[:, None], -1)
    n_slots = n_local + MOVES + 2
    flat = lambda a: jnp.broadcast_to(a, load.shape).reshape(-1)
    expert = jnp.arange(load.size, dtype=I32)
    rounds = jnp.arange(n_slots, dtype=I32)
    hit = (flat(to)[None, None, :] == position[:, :, None]) & (flat(at)[None, None, :] == rounds[None, :, None]) & flat(in_round)[None, None, :]
    table = jnp.max(jnp.where(hit, (expert + LANES * flat(source))[None, None, :], -1), axis=2)
    experts = jnp.where(table < 0, NO_EXPERT, table % LANES)
    sources = jnp.where(table < 0, 0, table // LANES)
    steps = jnp.arange(max(TAIL, MOVES), dtype=I32)
    tail_hit = tail_at[:, None, :] == steps[None, :TAIL, None]
    tails = jnp.max(jnp.where(tail_hit, ids[None, None, :], -1), axis=2)
    move_hit = (rank - keep[:, None])[:, None, :] == steps[None, :MOVES, None]
    moves = jnp.max(jnp.where(move_hit, ids[None, None, :], 0), axis=2)
    last_load = jnp.max(jnp.where((at == n_round - 1) & in_round, load, 0))
    return experts, sources, tails, moves, n_round, half, last_load


def solution(mesh):
    n_group, n_data = mesh.shape["expert"], mesh.shape["data"]
    assert n_group == 4 and n_data == 2
    tok_spec = P(("rep", "expert", "data"), None)
    wide_spec = P("expert", "data", None)
    down_spec = P("expert", None, "data")
    swap = [(0, 1), (1, 0)]

    def across(value, k):
        return lax.ppermute(value, "expert", [(p, p ^ k) for p in range(n_group)])

    def spread(groups):
        return (groups[0],) + tuple(across(groups[k], k) for k in range(1, n_group))

    def swapped(parts):
        return tuple(lax.ppermute(part, "data", swap) for part in parts)

    def device_body(x_loc, idx_loc, gate_loc, wg_loc, wu_loc, wd_loc):
        tok_rows, d_model = x_loc.shape
        top_k = idx_loc.shape[1]
        n_local = wg_loc.shape[0]
        n_exp = n_local * n_group
        capacity = capacity_rows(tok_rows, top_k, n_exp)
        me, q = lax.axis_index("expert"), lax.axis_index("data")
        weights = (wg_loc, wu_loc, wd_loc)
        pieces, slot_t, tile_starts, count = route(idx_loc.T, gate_loc.T, capacity)
        starts = jnp.concatenate([tile_starts[:, 0], count[:1]], axis=0)
        counts = lax.all_gather(count[0, :n_exp], ("expert", "data"))
        experts, sources, tails, moves, n_round, half_first, last_load = plan(counts, n_group)
        mine = me ^ jnp.arange(n_group, dtype=I32)
        table = jnp.concatenate([jnp.full((1, n_group), NO_EXPERT, I32), experts[mine].T], axis=0)
        my_sources = sources[me]
        my_hot = (experts[me][:, None] == jnp.arange(n_exp, dtype=I32)[None, :]).astype(I32)
        my_counts = counts.reshape(n_group, n_data, n_exp)[mine, q]
        used = jnp.sum(my_hot[:, None, :] * my_counts[None, :, :], axis=2)
        tail_local = jnp.maximum(tails[me], 0)
        tail_global = jnp.where(tails < 0, NO_EXPERT, tails + n_local * jnp.arange(n_group, dtype=I32)[:, None])[mine]

        def slices(e, source=None):
            return tuple(lax.dynamic_index_in_dim(w, e, axis=0, keepdims=False) for w in source or weights)

        def outgoing(r, extras):
            s = my_sources[r]
            kind = jnp.maximum(s - n_local + 1, 0)
            return lax.switch(kind, [lambda: slices(jnp.minimum(s, n_local - 1))] + [lambda i=i: extras[i] for i in range(MOVES)])

        half = d_model // n_data

        def one_round(r, carry, extras, first=False):
            token, peer, rows, back, send, acc = carry
            peer_next = swapped(send)
            *picked, token = pick(r + 1 + token, table, starts, slot_t, x_loc, capacity)
            rows_next = spread(picked)
            out_rows, token = expert_ffn(r + token, my_sources, used, weights, extras, peer, rows)
            back_next = spread(out_rows)
            send_next, token = lax.optimization_barrier((outgoing(r[0] + 2 + token[0], extras), token))
            if not first:
                acc, token = mix(r - 1 + token, table, starts, pieces, [back], acc, F32)
            return token, peer_next, rows_next, back_next, send_next, acc

        def front(i):
            only = (0, 2) if i % 2 else range(n_group)
            pairs = [(s * n_group + p, (1 - s) * n_group + p) for p in only for s in range(n_data)]
            peer = tuple(lax.ppermute(part, ("data", "expert"), pairs) for part in slices(first_sources[0]))
            tail_picked, token = lax.optimization_barrier((tuple(pick_tail(tail_global, slot_t, x_loc)), jnp.zeros((1,), I32)))
            tail_rows = spread(tail_picked)
            *picked, token = pick(token, table, starts, slot_t, x_loc, capacity)
            rows = (picked[0],) + tuple(lax.ppermute(picked[k], "expert", [(p ^ k, p) for p in only]) for k in range(1, n_group))
            later, token = lax.optimization_barrier((weights, token))
            moved, token = lax.optimization_barrier(([slices(move + token[0], later) for move in my_moves], token))
            extras = tuple(tuple(across(part, 1) for part in parts) for parts in moved)
            later, token = lax.optimization_barrier((weights, token))
            send, token = lax.optimization_barrier((slices(first_sources[1] + token[0], later), token))
            tail_x = jnp.stack([group.reshape(TAIL, TAIL_CAP, d_model) for group in tail_rows], axis=1).reshape(TAIL, n_group * TAIL_CAP, d_model)
            tail_mine = lax.dynamic_slice_in_dim(tail_x, q * half, half, axis=2)
            tail_half, token = lax.optimization_barrier((lax.dynamic_slice_in_dim(tail_x, (1 - q) * half, half, axis=2), token))
            tail_peer = lax.ppermute(tail_half, "data", swap)
            x_later, token = lax.optimization_barrier((x_loc, token))
            acc, token = lax.optimization_barrier((x_later.astype(F32), token))
            blank = tuple(unset(*[jax.ShapeDtypeStruct((capacity, d_model), BF16)] * n_group))
            carry = (token, peer, rows, blank, send, acc)
            if i >= 2:
                carry = one_round(jnp.zeros((1,), I32), carry, extras, first=True)
            return carry, extras, tail_mine, tail_peer

        first_sources = [my_sources[0], my_sources[1]]
        my_moves = [moves[me, m] for m in range(MOVES)]
        odd = (n_round - 1) % 2
        carry, extras, tail_mine, tail_peer = lax.switch(2 * odd + half_first, [functools.partial(front, i) for i in range(4)])

        def two_rounds(i, c):
            r = jnp.full((1,), odd + 2 * i, I32)
            return one_round(r + 1, one_round(r, c, extras), extras)

        token, peer, rows, back, _, acc = lax.fori_loop(0, (n_round - 1) // 2, two_rounds, carry)
        last = jnp.full((1,), n_round - 1, I32)
        ffn = wg_loc.shape[2]

        partial, partial_peer = tail_in(tail_local + token, tail_mine, tail_peer, wg_loc, wu_loc)
        (partial, partial_peer), token = lax.optimization_barrier(((partial, partial_peer), token))
        partial_sum = partial + lax.ppermute(partial_peer, "data", swap)
        out_last, token = expert_ffn(last + token, my_sources, used, weights, extras, peer, rows)

        def diagonal(value, k):
            pairs = [(s * n_group + p, (1 - s) * n_group + (p ^ k)) for p in range(n_group) for s in range(n_data)]
            return lax.ppermute(value, ("data", "expert"), pairs)

        def finish(keep):
            def run():
                back_last = spread([group[:keep] for group in out_last])
                tail_h = (jax.nn.silu(partial_sum[..., :ffn]) * partial_sum[..., ffn:]).astype(BF16)
                tail_h_peer = lax.ppermute(tail_h, "data", swap)
                if keep == LIGHT:
                    acc_late, go = acc, token
                else:
                    acc_late, go = mix(last - 1 + token, table, starts, pieces, [back], acc, F32)
                mine, theirs = tail_out(tail_local + go, tail_h, tail_h_peer, wd_loc)
                mine, theirs = (o.reshape(TAIL, n_group, TAIL_CAP, half) for o in (mine, theirs))
                tail_halves = []
                for k in range(n_group):
                    near, far = mine[:, k].reshape(TAIL * TAIL_CAP, half), theirs[:, k].reshape(TAIL * TAIL_CAP, half)
                    tail_halves.append((across(near, k) if k else near, diagonal(far, k)))
                near, far = (jnp.concatenate(parts, axis=0) for parts in zip(*tail_halves))
                tail_rows = jnp.where(q == 0, jnp.concatenate([near, far], axis=1), jnp.concatenate([far, near], axis=1))
                tail = (tail_global, tail_rows)
                if keep == LIGHT:
                    return mix(jnp.concatenate([last - 1 + go, last]), table, starts, pieces, [back, back_last], acc_late, BF16, tail)[0]
                return mix(last + go, table, starts, pieces, [back_last], acc_late, BF16, tail)[0]

            return run

        return lax.cond(last_load <= LIGHT, finish(LIGHT), finish(capacity))

    return jax.shard_map(device_body, mesh=mesh, in_specs=(tok_spec, tok_spec, tok_spec, wide_spec, wide_spec, down_spec), out_specs=tok_spec, check_vma=False)
```

time: 2730 us -> 2680 us (0.982)
  local copies, waits for them, and re-layouts: 186 us -> 139 us
    ppermute x4 -> x13, waiting for transfers between devices: 40.7 us -> 254 us  [the longest x3 175 us: front(): lax.ppermute(part, ('data', 'expert'), pairs)]
    ppermute x72 -> x69, waiting for transfers between devices: 478 us -> 288 us  [across(): return lax.ppermute(value, 'expert', [(p, p ^ k) for p in range(n_group)])]
    ppermute x30 -> x27, waiting for transfers between devices: 641 us -> 602 us  [swapped(): return tuple((lax.ppermute(part, 'data', swap) for part in parts))]
    while x36 -> x17, local copies, waits for them, and re-layouts: 29.6 us -> 1.38 us  [the longest x1 1.35 us: device_body(): lax.fori_loop(0, (n_round - 1) // 2, two_rounds, carry)]
    ppermute x72 -> x69, starting transfers between devices: 113 us -> 109 us  [across(): return lax.ppermute(value, 'expert', [(p, p ^ k) for p in range(n_group)])]
    pallas_call x11 -> x10, Pallas kernels: 460 us -> 457 us  [mix(): pl.pallas_call(functools.partial(mix_body, len(sets), bool(tail)), grid=(...]
  transfers between devices with their start and end apart: 106 -> 109, of which waited for: 40 -> 43; matrix products, arithmetic and copies ran while one was open for 7% -> 6% of each run, Pallas kernels for 33% -> 35%
where the time goes in v2:
time: 2680 us; the launch traced here: 2670 us
  waiting for transfers between devices  1140 us (43%)
  Pallas kernels  1120 us (42%)
  starting transfers between devices  155 us (6%)
  local copies, waits for them, and re-layouts  139 us (5%)
  loops' own time  60.9 us (2%)
  other arithmetic  30.9 us (1%)
    ppermute x27, waiting for transfers between devices, swapped(): return tuple((lax.ppermute(part, 'data', swap) for part in parts))  602 us
    pallas_call x10, Pallas kernels, mix(): pl.pallas_call(functools.partial(mix_body, len(sets), bool(tail)), grid=(...  457 us
    pallas_call x10, Pallas kernels, expert_ffn(): pl.pallas_call(functools.partial(ffn_body, n_local), in_specs=[SMEM] * 3...  369 us
    ppermute x69, waiting for transfers between devices, across(): return lax.ppermute(value, 'expert', [(p, p ^ k) for p in range(n_group)])  288 us
    pallas_call x10, Pallas kernels, pick(): pl.pallas_call(pick_body, grid=(tok_rows // TILE,), in_specs=[SMEM, SMEM,...  248 us
    ppermute x3, waiting for transfers between devices, front(): lax.ppermute(part, ('data', 'expert'), pairs)  175 us
    squeeze x26, local copies, waits for them, and re-layouts, slices(): lax.dynamic_index_in_dim(w, e, axis=0, keepdims=False)  115 us
    ppermute x69, starting transfers between devices, across(): return lax.ppermute(value, 'expert', [(p, p ^ k) for p in range(n_group)])  109 us
  transfers between devices with their start and end apart: 109, of which 43 were waited for; matrix products, arithmetic and copies ran while one was open for 6% of the time, Pallas kernels for 35%

profile of v2, /device:TPU:0, one launch (start us, length us, event | category | flops | bytes accessed | tf_op | source)
XLA Modules:
  0.0 2665.9 jit_solution(16889121263520272148)
XLA Ops:
  38.9 536.8 %conditional.6 = (s32[1]{0:T(128)}, bf16[1024,1408]{1,0:T(8,128)(2,1)}, bf16[1024,1408]{1,0:T(8,128)(2,1)}, bf16[1408,1024]{1,0:T(8,128)(2,1)}, bf16[480,2048]{1...) conditional(s32[]{:T(128)} %clamp.29, (s32[4,3]{1,0:T(4,128)}, ...), branch_computations={%region_13.14_spmd, %region_14.15_spmd, %region_15.19_spmd, %regio... | conditional | flops 40476213248 | bytes 488638656 | solution.py:644
  200.7 55.0 %collective-permute-done.41.refs_9_ = bf16[1024,1408]{1,0:T(8,128)(2,1)S(1)} collective-permute-done((bf16[1024,1408]{1,0:T(8,128)(2,1)S(1)}, bf16[1024,1408]{1,0:T(8,128)(2,1)S(1)}, u32[]{:S(2)}, u32[]{:S(2)}) %collective-permute-start.41) | collective-permute-done | bytes 2883616 | tf_op jit(solution)/shard_map/cond/branch_2_fun/ppermute | solution.py:619
  257.4 60.1 %collective-permute-done.42.refs_10_ = bf16[1024,1408]{1,0:T(8,128)(2,1)S(1)} collective-permute-done((bf16[1024,1408]{1,0:T(8,128)(2,1)S(1)}, bf16[1024,1408]{1,0:T(8,128)(2,1)S(1)}, u32[]{:S(2)}, u32[]{:S(2)}) %collective-permute-start.42) | collective-permute-done | bytes 2883616 | tf_op jit(solution)/shard_map/cond/branch_2_fun/ppermute | solution.py:619
  319.2 60.1 %collective-permute-done.43.refs_11_ = bf16[1408,1024]{1,0:T(8,128)(2,1)S(1)} collective-permute-done((bf16[1408,1024]{1,0:T(8,128)(2,1)S(1)}, bf16[1408,1024]{1,0:T(8,128)(2,1)S(1)}, u32[]{:S(2)}, u32[]{:S(2)}) %collective-permute-start.43) | collective-permute-done | bytes 2883616 | tf_op jit(solution)/shard_map/cond/branch_2_fun/ppermute | solution.py:619
  380.8 53.9 %ffn.19 = (bf16[480,2048]{1,0:T(8,128)(2,1)S(1)}, bf16[480,2048]{1,0:T(8,128)(2,1)}, bf16[480,2048]{1,0:T(8,128)(2,1)}, bf16[480,2048]{1,0:T(8,128)(2,1)}, s32[1]{0:T(128)}) custom-call(s32[1]{0:T(128)} %get-tuple-element.1163.r_ref, s32[20]{0:T(128)S(1)} %get-tuple-element.1126.src_ref, s32[20,4]{1,0:T(8,128)S(1)} %get-tuple-element.1164.used_ref, ...), custom_call_target="tpu_custom_call" | custom-call | flops 33218887680 | bytes 17301504 | tf_op jit(solution)/shard_map/cond/branch_2_fun/ffn/pallas_call | solution.py:291
  454.2 48.8 %collective-permute-done.48 = bf16[1024,1408]{1,0:T(8,128)(2,1)} collective-permute-done((bf16[1024,1408]{1,0:T(8,128)(2,1)}, bf16[1024,1408]{1,0:T(8,128)(2,1)}, u32[]{:S(2)}, u32[]{:S(2)}) %collective-permute-start.48) | collective-permute-done | bytes 2883616 | tf_op jit(solution)/shard_map/cond/branch_2_fun/ppermute | solution.py:571
  503.0 61.3 %collective-permute-done.49 = bf16[1408,1024]{1,0:T(8,128)(2,1)} collective-permute-done((bf16[1408,1024]{1,0:T(8,128)(2,1)}, bf16[1408,1024]{1,0:T(8,128)(2,1)}, u32[]{:S(2)}, u32[]{:S(2)}) %collective-permute-start.49) | collective-permute-done | bytes 2883616 | tf_op jit(solution)/shard_map/cond/branch_2_fun/ppermute | solution.py:571
  575.7 1873.3 %while.45 = (s32[]{:T(128)}, s32[1]{0:T(128)}, bf16[1024,1408]{1,0:T(8,128)(2,1)}, bf16[1024,1408]{1,0:T(8,128)(2,1)}, bf16[1408,1024]{1,0:T(8,128)(2,1)}, /*ind...) while((s32[]{:T(128)}, s32[1]{0:T(128)}, ...), condition=%wide.region_30.31_spmd, body=%wide.region_23.30_spmd.sunk | while | flops 87644176384 | bytes 416286144 | solution.py:650
  602.1 52.9 %ffn.22 = (bf16[480,2048]{1,0:T(8,128)(2,1)}, bf16[480,2048]{1,0:T(8,128)(2,1)}, bf16[480,2048]{1,0:T(8,128)(2,1)}, bf16[480,2048]{1,0:T(8,128)(2,1)}, s32[1]{0:T(128)}) custom-call(s32[1]{0:T(128)S(6)} %add.707.r_ref, s32[20]{0:T(128)S(1)} %get-tuple-element.2704.src_ref, s32[20,4]{1,0:T(8,128)S(1)} %get-tuple-element.2705.used_ref, ...), custom_call_target="tpu_custom_call" | custom-call | flops 33218887680 | bytes 17301504 | tf_op jit(solution)/shard_map/while/body/ffn/pallas_call | solution.py:291
  688.8 49.1 %mix.22 = (f32[4096,2048]{1,0:T(8,128)}, s32[1]{0:T(128)}) custom-call(s32[1]{0:T(128)S(6)} %add.711.r_ref, s32[21,4]{1,0:T(8,128)S(1)} %get-tuple-element.2700.tab_ref, s32[17,128]{1,0:T(8,128)S(1)} %get-tuple-element.2701.start_ref, bf16[4096,640]{1,0:T(8,128)(2,1)} %get-tuple-element.2715.pieces_ref, ...), custom_call_target="tpu_custom_call", output_to_operand_aliasing={{0}: (4, {})} | custom-call | flops 8589934592 | bytes 67108864 | tf_op jit(solution)/shard_map/while/body/mix/pallas_call | solution.py:421
  810.3 48.3 %collective-permute-done.106.refs_11_ = bf16[1408,1024]{1,0:T(8,128)(2,1)} collective-permute-done((bf16[1408,1024]{1,0:T(8,128)(2,1)}, bf16[1408,1024]{1,0:T(8,128)(2,1)}, u32[]{:S(2)}, u32[]{:S(2)}) %collective-permute-start.106) | collective-permute-done | bytes 2883616 | tf_op jit(solution)/shard_map/while/body/ppermute | solution.py:571
  858.6 53.3 %ffn.23 = (bf16[480,2048]{1,0:T(8,128)(2,1)S(1)}, bf16[480,2048]{1,0:T(8,128)(2,1)}, bf16[480,2048]{1,0:T(8,128)(2,1)}, bf16[480,2048]{1,0:T(8,128)(2,1)}, s32[1]{0:T(128)}) custom-call(s32[1]{0:T(128)S(6)} %add.713.r_ref, s32[20]{0:T(128)S(1)} %get-tuple-element.2704.src_ref, s32[20,4]{1,0:T(8,128)S(1)} %get-tuple-element.2705.used_ref, ...), custom_call_target="tpu_custom_call" | custom-call | flops 33218887680 | bytes 17301504 | tf_op jit(solution)/shard_map/while/body/ffn/pallas_call | solution.py:291
  932.7 47.7 %mix.23 = (f32[4096,2048]{1,0:T(8,128)}, s32[1]{0:T(128)}) custom-call(s32[1]{0:T(128)S(6)} %add.717.r_ref, s32[21,4]{1,0:T(8,128)S(1)} %get-tuple-element.2700.tab_ref, s32[17,128]{1,0:T(8,128)S(1)} %get-tuple-element.2701.start_ref, bf16[4096,640]{1,0:T(8,128)(2,1)} %get-tuple-element.2715.pieces_ref, ...), custom_call_target="tpu_custom_call", output_to_operand_aliasing={{0}: (4, {})} | custom-call | flops 8589934592 | bytes 67108864 | tf_op jit(solution)/shard_map/while/body/mix/pallas_call | solution.py:421
  982.2 60.7 %collective-permute-done.115 = bf16[1408,1024]{1,0:T(8,128)(2,1)} collective-permute-done((bf16[1408,1024]{1,0:T(8,128)(2,1)}, bf16[1408,1024]{1,0:T(8,128)(2,1)}, u32[]{:S(2)}, u32[]{:S(2)}) %collective-permute-start.115) | collective-permute-done | bytes 2883616 | tf_op jit(solution)/shard_map/while/body/ppermute | solution.py:571
  1068.7 53.0 %ffn.22 = (bf16[480,2048]{1,0:T(8,128)(2,1)}, bf16[480,2048]{1,0:T(8,128)(2,1)}, bf16[480,2048]{1,0:T(8,128)(2,1)}, bf16[480,2048]{1,0:T(8,128)(2,1)}, s32[1]{0:T(128)}) custom-call(s32[1]{0:T(128)S(6)} %add.707.r_ref, s32[20]{0:T(128)S(1)} %get-tuple-element.2704.src_ref, s32[20,4]{1,0:T(8,128)S(1)} %get-tuple-element.2705.used_ref, ...), custom_call_target="tpu_custom_call" | custom-call | flops 33218887680 | bytes 17301504 | tf_op jit(solution)/shard_map/while/body/ffn/pallas_call | solution.py:291
  1154.3 47.4 %mix.22 = (f32[4096,2048]{1,0:T(8,128)}, s32[1]{0:T(128)}) custom-call(s32[1]{0:T(128)S(6)} %add.711.r_ref, s32[21,4]{1,0:T(8,128)S(1)} %get-tuple-element.2700.tab_ref, s32[17,128]{1,0:T(8,128)S(1)} %get-tuple-element.2701.start_ref, bf16[4096,640]{1,0:T(8,128)(2,1)} %get-tuple-element.2715.pieces_ref, ...), custom_call_target="tpu_custom_call", output_to_operand_aliasing={{0}: (4, {})} | custom-call | flops 8589934592 | bytes 67108864 | tf_op jit(solution)/shard_map/while/body/mix/pallas_call | solution.py:421
  1398.3 49.4 %mix.23 = (f32[4096,2048]{1,0:T(8,128)}, s32[1]{0:T(128)}) custom-call(s32[1]{0:T(128)S(6)} %add.717.r_ref, s32[21,4]{1,0:T(8,128)S(1)} %get-tuple-element.2700.tab_ref, s32[17,128]{1,0:T(8,128)S(1)} %get-tuple-element.2701.start_ref, bf16[4096,640]{1,0:T(8,128)(2,1)} %get-tuple-element.2715.pieces_ref, ...), custom_call_target="tpu_custom_call", output_to_operand_aliasing={{0}: (4, {})} | custom-call | flops 8589934592 | bytes 67108864 | tf_op jit(solution)/shard_map/while/body/mix/pallas_call | solution.py:421
  1447.8 60.8 %collective-permute-done.115 = bf16[1408,1024]{1,0:T(8,128)(2,1)} collective-permute-done((bf16[1408,1024]{1,0:T(8,128)(2,1)}, bf16[1408,1024]{1,0:T(8,128)(2,1)}, u32[]{:S(2)}, u32[]{:S(2)}) %collective-permute-start.115) | collective-permute-done | bytes 2883616 | tf_op jit(solution)/shard_map/while/body/ppermute | solution.py:571
  1629.0 53.6 %mix.22 = (f32[4096,2048]{1,0:T(8,128)}, s32[1]{0:T(128)}) custom-call(s32[1]{0:T(128)S(6)} %add.711.r_ref, s32[21,4]{1,0:T(8,128)S(1)} %get-tuple-element.2700.tab_ref, s32[17,128]{1,0:T(8,128)S(1)} %get-tuple-element.2701.start_ref, bf16[4096,640]{1,0:T(8,128)(2,1)} %get-tuple-element.2715.pieces_ref, ...), custom_call_target="tpu_custom_call", output_to_operand_aliasing={{0}: (4, {})} | custom-call | flops 8589934592 | bytes 67108864 | tf_op jit(solution)/shard_map/while/body/mix/pallas_call | solution.py:421
  1922.1 61.0 %collective-permute-done.115 = bf16[1408,1024]{1,0:T(8,128)(2,1)} collective-permute-done((bf16[1408,1024]{1,0:T(8,128)(2,1)}, bf16[1408,1024]{1,0:T(8,128)(2,1)}, u32[]{:S(2)}, u32[]{:S(2)}) %collective-permute-start.115) | collective-permute-done | bytes 2883616 | tf_op jit(solution)/shard_map/while/body/ppermute | solution.py:571
  2202.4 61.8 %collective-permute-done.106.refs_11_ = bf16[1408,1024]{1,0:T(8,128)(2,1)} collective-permute-done((bf16[1408,1024]{1,0:T(8,128)(2,1)}, bf16[1408,1024]{1,0:T(8,128)(2,1)}, u32[]{:S(2)}, u32[]{:S(2)}) %collective-permute-start.106) | collective-permute-done | bytes 2883616 | tf_op jit(solution)/shard_map/while/body/ppermute | solution.py:571
  2387.7 61.0 %collective-permute-done.115 = bf16[1408,1024]{1,0:T(8,128)(2,1)} collective-permute-done((bf16[1408,1024]{1,0:T(8,128)(2,1)}, bf16[1408,1024]{1,0:T(8,128)(2,1)}, u32[]{:S(2)}, u32[]{:S(2)}) %collective-permute-start.115) | collective-permute-done | bytes 2883616 | tf_op jit(solution)/shard_map/while/body/ppermute | solution.py:571
  2511.8 152.8 %conditional.7 = (bf16[4096,2048]{1,0:T(8,128)(2,1)}) conditional(s32[]{:T(128)} %convert_element_type.44, (s32[1]{0:T(128)}, s32[1]{0:T(128)}, s32[21,4]{0,1:T(4,128)}, s32[17,128]{1,0:T(8,128)S(1)}, bf16[4096,640]{1,0:T(8,128)(2,1)}, /*index=5*/f32[4096,2048]{1,0:T(8,128)}, bf16[480,2048]{1,0:T(8,128)(2,1)S(1)}, bf16[480,2048]{1,0:T(8,128)(2,1)}, ...), branch_computations={%region_31.32_spmd, %region_32.33_spmd} | conditional | flops 18297044992 | bytes 185877696 | solution.py:687
  2612.7 51.7 %mix.20 = (bf16[4096,2048]{1,0:T(8,128)(2,1)}, s32[1]{0:T(128)}) custom-call(s32[1]{0:T(128)S(6)} %add.558.r_ref, s32[21,4]{1,0:T(8,128)} %copy.130.tab_ref, s32[17,128]{1,0:T(8,128)S(1)} %get-tuple-element.1358.start_ref, bf16[4096,640]{1,0:T(8,128)(2,1)} %get-tuple-element.1359.pieces_ref, f32[4096,2048]{1,0:T(8,128)} %get-tuple-element.1366.acc_hbm, ...), custom_call_target="tpu_custom_call" | custom-call | flops 8589934592 | bytes 67108864 | tf_op jit(solution)/shard_map/cond/branch_0_fun/mix/pallas_call | solution.py:421
  (393 shorter events, 1537.7 us)
Async XLA Ops:
  194.5 184.8 %collective-permute-start.43 = (bf16[1408,1024]{1,0:T(8,128)(2,1)S(1)}, bf16[1408,1024]{1,0:T(8,128)(2,1)S(1)}, u32[]{:S(2)}, u32[]{:S(2)}) collective-permute-start(bf16[1408,1024]{1,0:T(8,128)(2,1)S(1)} %dynamic-slice_bitcast_fusion.27), channel_id=1, source_target_pairs={{0,4},{4,0},{1,5},{5,1},{2,6},{6,2},{3,7},{7,3}} | collective-permute-start | bytes 8650760 | tf_op jit(solution)/shard_map/cond/branch_2_fun/ppermute | solution.py:619
  196.2 245.0 %collective-permute-start.47 = (bf16[1024,1408]{1,0:T(8,128)(2,1)}, bf16[1024,1408]{1,0:T(8,128)(2,1)}, u32[]{:S(2)}, u32[]{:S(2)}) collective-permute-start(bf16[1024,1408]{1,0:T(8,128)(2,1)} %dynamic-slice_bitcast_fusion.32), channel_id=1, source_target_pairs={{0,4},{4,0},{1,5},{5,1},{2,6},{6,2},{3,7},{7,3}} | collective-permute-start | bytes 8650760 | tf_op jit(solution)/shard_map/cond/branch_2_fun/ppermute | solution.py:571
  199.0 304.0 %collective-permute-start.48 = (bf16[1024,1408]{1,0:T(8,128)(2,1)}, bf16[1024,1408]{1,0:T(8,128)(2,1)}, u32[]{:S(2)}, u32[]{:S(2)}) collective-permute-start(bf16[1024,1408]{1,0:T(8,128)(2,1)} %dynamic-slice_bitcast_fusion.31), channel_id=1, source_target_pairs={{0,4},{4,0},{1,5},{5,1},{2,6},{6,2},{3,7},{7,3}} | collective-permute-start | bytes 8650760 | tf_op jit(solution)/shard_map/cond/branch_2_fun/ppermute | solution.py:571
  255.7 308.6 %collective-permute-start.49 = (bf16[1408,1024]{1,0:T(8,128)(2,1)}, bf16[1408,1024]{1,0:T(8,128)(2,1)}, u32[]{:S(2)}, u32[]{:S(2)}) collective-permute-start(bf16[1408,1024]{1,0:T(8,128)(2,1)} %dynamic-slice_bitcast_fusion.30), channel_id=1, source_target_pairs={{0,4},{4,0},{1,5},{5,1},{2,6},{6,2},{3,7},{7,3}} | collective-permute-start | bytes 8650760 | tf_op jit(solution)/shard_map/cond/branch_2_fun/ppermute | solution.py:571
  687.0 171.6 %collective-permute-start.106 = (bf16[1408,1024]{1,0:T(8,128)(2,1)}, bf16[1408,1024]{1,0:T(8,128)(2,1)}, u32[]{:S(2)}, u32[]{:S(2)}) collective-permute-start(bf16[1408,1024]{1,0:T(8,128)(2,1)} %get-tuple-element.2652), channel_id=1, source_target_pairs={{0,4},{4,0},{1,5},{5,1},{2,6},{6,2},{3,7},{7,3}} | collective-permute-start | bytes 8650760 | tf_op jit(solution)/shard_map/while/body/ppermute | solution.py:571
  808.1 174.1 %collective-permute-start.114 = (bf16[1024,1408]{1,0:T(8,128)(2,1)}, bf16[1024,1408]{1,0:T(8,128)(2,1)}, u32[]{:S(2)}, u32[]{:S(2)}) collective-permute-start(bf16[1024,1408]{1,0:T(8,128)(2,1)} %get-tuple-element.2447), channel_id=1, source_target_pairs={{0,4},{4,0},{1,5},{5,1},{2,6},{6,2},{3,7},{7,3}} | collective-permute-start | bytes 8650760 | tf_op jit(solution)/shard_map/while/body/ppermute | solution.py:571
  809.0 233.9 %collective-permute-start.115 = (bf16[1408,1024]{1,0:T(8,128)(2,1)}, bf16[1408,1024]{1,0:T(8,128)(2,1)}, u32[]{:S(2)}, u32[]{:S(2)}) collective-permute-start(bf16[1408,1024]{1,0:T(8,128)(2,1)} %get-tuple-element.2448), channel_id=1, source_target_pairs={{0,4},{4,0},{1,5},{5,1},{2,6},{6,2},{3,7},{7,3}} | collective-permute-start | bytes 8650760 | tf_op jit(solution)/shard_map/while/body/ppermute | solution.py:571
  1134.9 144.5 %collective-permute-start.104 = (bf16[1024,1408]{1,0:T(8,128)(2,1)}, bf16[1024,1408]{1,0:T(8,128)(2,1)}, u32[]{:S(2)}, u32[]{:S(2)}) collective-permute-start(bf16[1024,1408]{1,0:T(8,128)(2,1)} %get-tuple-element.2650), channel_id=1, source_target_pairs={{0,4},{4,0},{1,5},{5,1},{2,6},{6,2},{3,7},{7,3}} | collective-permute-start | bytes 8650760 | tf_op jit(solution)/shard_map/while/body/ppermute | solution.py:571
  1136.7 143.1 %collective-permute-start.105 = (bf16[1024,1408]{1,0:T(8,128)(2,1)}, bf16[1024,1408]{1,0:T(8,128)(2,1)}, u32[]{:S(2)}, u32[]{:S(2)}) collective-permute-start(bf16[1024,1408]{1,0:T(8,128)(2,1)} %get-tuple-element.2651), channel_id=1, source_target_pairs={{0,4},{4,0},{1,5},{5,1},{2,6},{6,2},{3,7},{7,3}} | collective-permute-start | bytes 8650760 | tf_op jit(solution)/shard_map/while/body/ppermute | solution.py:571
  1153.4 170.8 %collective-permute-start.106 = (bf16[1408,1024]{1,0:T(8,128)(2,1)}, bf16[1408,1024]{1,0:T(8,128)(2,1)}, u32[]{:S(2)}, u32[]{:S(2)}) collective-permute-start(bf16[1408,1024]{1,0:T(8,128)(2,1)} %get-tuple-element.2652), channel_id=1, source_target_pairs={{0,4},{4,0},{1,5},{5,1},{2,6},{6,2},{3,7},{7,3}} | collective-permute-start | bytes 8650760 | tf_op jit(solution)/shard_map/while/body/ppermute | solution.py:571
  1277.7 170.1 %collective-permute-start.114 = (bf16[1024,1408]{1,0:T(8,128)(2,1)}, bf16[1024,1408]{1,0:T(8,128)(2,1)}, u32[]{:S(2)}, u32[]{:S(2)}) collective-permute-start(bf16[1024,1408]{1,0:T(8,128)(2,1)} %get-tuple-element.2447), channel_id=1, source_target_pairs={{0,4},{4,0},{1,5},{5,1},{2,6},{6,2},{3,7},{7,3}} | collective-permute-start | bytes 8650760 | tf_op jit(solution)/shard_map/while/body/ppermute | solution.py:571
  1279.5 229.1 %collective-permute-start.115 = (bf16[1408,1024]{1,0:T(8,128)(2,1)}, bf16[1408,1024]{1,0:T(8,128)(2,1)}, u32[]{:S(2)}, u32[]{:S(2)}) collective-permute-start(bf16[1408,1024]{1,0:T(8,128)(2,1)} %get-tuple-element.2448), channel_id=1, source_target_pairs={{0,4},{4,0},{1,5},{5,1},{2,6},{6,2},{3,7},{7,3}} | collective-permute-start | bytes 8650760 | tf_op jit(solution)/shard_map/while/body/ppermute | solution.py:571
  1363.8 144.8 %collective-permute-start.119 = (bf16[480,2048]{1,0:T(8,128)(2,1)}, bf16[480,2048]{1,0:T(8,128)(2,1)}, u32[]{:S(2)}, u32[]{:S(2)}) collective-permute-start(bf16[480,2048]{1,0:T(8,128)(2,1)} %get-tuple-element.2454), channel_id=1, source_target_pairs={{0,1},{1,0},{2,3},{3,2},{4,5},{5,4},{6,7},{7,6}} | collective-permute-start | bytes 5898248 | tf_op jit(solution)/shard_map/while/body/ppermute | solution.py:565
  1609.2 149.2 %collective-permute-start.104 = (bf16[1024,1408]{1,0:T(8,128)(2,1)}, bf16[1024,1408]{1,0:T(8,128)(2,1)}, u32[]{:S(2)}, u32[]{:S(2)}) collective-permute-start(bf16[1024,1408]{1,0:T(8,128)(2,1)} %get-tuple-element.2650), channel_id=1, source_target_pairs={{0,4},{4,0},{1,5},{5,1},{2,6},{6,2},{3,7},{7,3}} | collective-permute-start | bytes 8650760 | tf_op jit(solution)/shard_map/while/body/ppermute | solution.py:571
  1610.0 150.4 %collective-permute-start.105 = (bf16[1024,1408]{1,0:T(8,128)(2,1)}, bf16[1024,1408]{1,0:T(8,128)(2,1)}, u32[]{:S(2)}, u32[]{:S(2)}) collective-permute-start(bf16[1024,1408]{1,0:T(8,128)(2,1)} %get-tuple-element.2651), channel_id=1, source_target_pairs={{0,4},{4,0},{1,5},{5,1},{2,6},{6,2},{3,7},{7,3}} | collective-permute-start | bytes 8650760 | tf_op jit(solution)/shard_map/while/body/ppermute | solution.py:571
  1627.2 171.3 %collective-permute-start.106 = (bf16[1408,1024]{1,0:T(8,128)(2,1)}, bf16[1408,1024]{1,0:T(8,128)(2,1)}, u32[]{:S(2)}, u32[]{:S(2)}) collective-permute-start(bf16[1408,1024]{1,0:T(8,128)(2,1)} %get-tuple-element.2652), channel_id=1, source_target_pairs={{0,4},{4,0},{1,5},{5,1},{2,6},{6,2},{3,7},{7,3}} | collective-permute-start | bytes 8650760 | tf_op jit(solution)/shard_map/while/body/ppermute | solution.py:571
  1758.4 163.7 %collective-permute-start.114 = (bf16[1024,1408]{1,0:T(8,128)(2,1)}, bf16[1024,1408]{1,0:T(8,128)(2,1)}, u32[]{:S(2)}, u32[]{:S(2)}) collective-permute-start(bf16[1024,1408]{1,0:T(8,128)(2,1)} %get-tuple-element.2447), channel_id=1, source_target_pairs={{0,4},{4,0},{1,5},{5,1},{2,6},{6,2},{3,7},{7,3}} | collective-permute-start | bytes 8650760 | tf_op jit(solution)/shard_map/while/body/ppermute | solution.py:571
  1758.4 224.7 %collective-permute-start.115 = (bf16[1408,1024]{1,0:T(8,128)(2,1)}, bf16[1408,1024]{1,0:T(8,128)(2,1)}, u32[]{:S(2)}, u32[]{:S(2)}) collective-permute-start(bf16[1408,1024]{1,0:T(8,128)(2,1)} %get-tuple-element.2448), channel_id=1, source_target_pairs={{0,4},{4,0},{1,5},{5,1},{2,6},{6,2},{3,7},{7,3}} | collective-permute-start | bytes 8650760 | tf_op jit(solution)/shard_map/while/body/ppermute | solution.py:571
  1824.3 158.8 %collective-permute-start.119 = (bf16[480,2048]{1,0:T(8,128)(2,1)}, bf16[480,2048]{1,0:T(8,128)(2,1)}, u32[]{:S(2)}, u32[]{:S(2)}) collective-permute-start(bf16[480,2048]{1,0:T(8,128)(2,1)} %get-tuple-element.2454), channel_id=1, source_target_pairs={{0,1},{1,0},{2,3},{3,2},{4,5},{5,4},{6,7},{7,6}} | collective-permute-start | bytes 5898248 | tf_op jit(solution)/shard_map/while/body/ppermute | solution.py:565
  2093.7 170.4 %collective-permute-start.106 = (bf16[1408,1024]{1,0:T(8,128)(2,1)}, bf16[1408,1024]{1,0:T(8,128)(2,1)}, u32[]{:S(2)}, u32[]{:S(2)}) collective-permute-start(bf16[1408,1024]{1,0:T(8,128)(2,1)} %get-tuple-element.2652), channel_id=1, source_target_pairs={{0,4},{4,0},{1,5},{5,1},{2,6},{6,2},{3,7},{7,3}} | collective-permute-start | bytes 8650760 | tf_op jit(solution)/shard_map/while/body/ppermute | solution.py:571
  2200.1 187.6 %collective-permute-start.114 = (bf16[1024,1408]{1,0:T(8,128)(2,1)}, bf16[1024,1408]{1,0:T(8,128)(2,1)}, u32[]{:S(2)}, u32[]{:S(2)}) collective-permute-start(bf16[1024,1408]{1,0:T(8,128)(2,1)} %get-tuple-element.2447), channel_id=1, source_target_pairs={{0,4},{4,0},{1,5},{5,1},{2,6},{6,2},{3,7},{7,3}} | collective-permute-start | bytes 8650760 | tf_op jit(solution)/shard_map/while/body/ppermute | solution.py:571
  2201.1 247.7 %collective-permute-start.115 = (bf16[1408,1024]{1,0:T(8,128)(2,1)}, bf16[1408,1024]{1,0:T(8,128)(2,1)}, u32[]{:S(2)}, u32[]{:S(2)}) collective-permute-start(bf16[1408,1024]{1,0:T(8,128)(2,1)} %get-tuple-element.2448), channel_id=1, source_target_pairs={{0,4},{4,0},{1,5},{5,1},{2,6},{6,2},{3,7},{7,3}} | collective-permute-start | bytes 8650760 | tf_op jit(solution)/shard_map/while/body/ppermute | solution.py:571
  2277.3 171.5 %collective-permute-start.119 = (bf16[480,2048]{1,0:T(8,128)(2,1)}, bf16[480,2048]{1,0:T(8,128)(2,1)}, u32[]{:S(2)}, u32[]{:S(2)}) collective-permute-start(bf16[480,2048]{1,0:T(8,128)(2,1)} %get-tuple-element.2454), channel_id=1, source_target_pairs={{0,1},{1,0},{2,3},{3,2},{4,5},{5,4},{6,7},{7,6}} | collective-permute-start | bytes 5898248 | tf_op jit(solution)/shard_map/while/body/ppermute | solution.py:565
  2308.3 140.4 %collective-permute-start.120 = (bf16[480,2048]{1,0:T(8,128)(2,1)}, bf16[480,2048]{1,0:T(8,128)(2,1)}, u32[]{:S(2)}, u32[]{:S(2)}) collective-permute-start(bf16[480,2048]{1,0:T(8,128)(2,1)} %get-tuple-element.2455), channel_id=1, source_target_pairs={{0,2},{1,3},{2,0},{3,1},{4,6},{5,7},{6,4},{7,5}} | collective-permute-start | bytes 5898248 | tf_op jit(solution)/shard_map/while/body/ppermute | solution.py:565
  (103 other events, 9506.0 us)

commit v3 on v1

--- a/solution.py
+++ b/solution.py
@@ -13,6 +13,8 @@
 TILE = 256
 WINDOW = 128
 MOVES = 2
+LAST_PART = 160
+LIGHT = 320
 TAIL, TAIL_CAP = 3, 16
 BF16, F32, I32 = jnp.bfloat16, jnp.float32, jnp.int32
 ANY = pl.BlockSpec(memory_space=pl.ANY)
@@ -266,6 +268,162 @@
     return tuple(out[:n_rows]), out[n_rows]
 
 
+def choose_source(src, n_local, sources, act):
+    for s, parts in enumerate(sources):
+        @pl.when(jnp.maximum(src - n_local + 1, 0) == s)
+        def _():
+            act([part.at[jnp.minimum(src, n_local - 1)] for part in parts] if s == 0 else parts)
+
+
+def ffn_up_body(n_local, r_ref, src_ref, used_ref, *refs):
+    n_src, n_rows = 1 + MOVES, used_ref.shape[1]
+    own, refs = refs[: 2 * n_src], refs[2 * n_src :]
+    pg, pu, *refs = refs
+    rows, (h_out, token, x_buf, w_in, h_buf, x_sem, w_sem, h_sem) = refs[:n_rows], refs[n_rows:]
+    half, ffn = pg.shape
+    q = lax.axis_index("data")
+    r = r_ref[0]
+    token[0] = 0
+
+    def load(place, parts, first):
+        at = pl.ds(pl.multiple_of(place * half, half), half)
+        return [pltpu.make_async_copy(part, w_in.at[at, pl.ds(i * ffn, ffn)], w_sem.at[first + i]) for i, part in enumerate(parts)]
+
+    def start_all(parts):
+        for copy in load(q, parts, 0):
+            copy.start()
+
+    row_loads = [pltpu.make_async_copy(rows[i], x_buf.at[i], x_sem.at[i]) for i in range(n_rows)]
+    for copy in row_loads + load(1 - q, (pg, pu), 2):
+        copy.start()
+    choose_source(src_ref[r], n_local, [own[2 * s : 2 * s + 2] for s in range(n_src)], start_all)
+    for copy in row_loads + load(q, (pg, pu), 0) + load(1 - q, (pg, pu), 2):
+        copy.wait()
+
+    part = LAST_PART
+
+    @pl.loop(0, n_rows)
+    def _(i):
+        @pl.loop(0, x_buf.shape[1] // part)
+        def _(j):
+            at = pl.ds(pl.multiple_of(j * part, part), part)
+
+            @pl.when(used_ref[r, i] > j * part)
+            def _():
+                act = jnp.dot(x_buf[i, at], w_in[...], preferred_element_type=F32)
+                h_buf[i, at] = (jax.nn.silu(act[:, :ffn]) * act[:, ffn:]).astype(BF16)
+
+            @pl.when(used_ref[r, i] <= j * part)
+            def _():
+                h_buf[i, at] = jnp.zeros((part, ffn), BF16)
+
+        pltpu.make_async_copy(h_buf.at[i], h_out.at[i], h_sem.at[i]).start()
+
+    for i in range(n_rows):
+        pltpu.make_async_copy(h_buf.at[i], h_out.at[i], h_sem.at[i]).wait()
+
+
+def ffn_up(r, sources, used, weights, extras, peer, rows):
+    capacity, d_model = rows[0].shape
+    n_local, half, ffn = weights[0].shape
+    n_rows = len(rows)
+    own = list(weights[:2]) + [part for extra in extras for part in extra[:2]]
+    return pl.pallas_call(
+        functools.partial(ffn_up_body, n_local),
+        in_specs=[SMEM] * 3 + [ANY] * (len(own) + 2 + n_rows),
+        out_specs=[ANY, SMEM],
+        out_shape=[jax.ShapeDtypeStruct((n_rows, capacity, ffn), BF16), TOKEN],
+        scratch_shapes=[
+            pltpu.VMEM((n_rows, capacity, d_model), BF16),
+            pltpu.VMEM((2 * half, 2 * ffn), BF16),
+            pltpu.VMEM((n_rows, capacity, ffn), BF16),
+            pltpu.SemaphoreType.DMA((n_rows,)),
+            pltpu.SemaphoreType.DMA((4,)),
+            pltpu.SemaphoreType.DMA((n_rows,)),
+        ],
+        compiler_params=params(),
+        cost_estimate=cost(4 * n_rows * capacity * d_model * ffn, 4 * d_model * ffn),
+        name="ffn_up",
+    )(r, sources, used, *own, *peer[:2], *rows)
+
+
+def ffn_down_body(n_local, r_ref, src_ref, used_ref, *refs):
+    n_src, n_rows = 1 + MOVES, used_ref.shape[1]
+    own, refs = refs[:n_src], refs[n_src:]
+    pd, h_in, *refs = refs
+    outs, (token, h_buf, w_out, o_buf, h_sem, w_sem, o_sem) = refs[: 2 * n_rows], refs[2 * n_rows :]
+    half = pd.shape[1]
+    q = lax.axis_index("data")
+    r = r_ref[0]
+    token[0] = 0
+
+    def load(place, part, i):
+        return pltpu.make_async_copy(part, w_out.at[:, pl.ds(pl.multiple_of(place * half, half), half)], w_sem.at[i])
+
+    def store(s):
+        parts = (o_buf.at[s, pl.ds(0, LIGHT)], o_buf.at[s, pl.ds(LIGHT, o_buf.shape[1] - LIGHT)])
+        return [pltpu.make_async_copy(part, outs[2 * s + i], o_sem.at[s, i]) for i, part in enumerate(parts)]
+
+    h_load = pltpu.make_async_copy(h_in, h_buf, h_sem)
+    h_load.start()
+    load(1 - q, pd, 1).start()
+    choose_source(src_ref[r], n_local, [own[s : s + 1] for s in range(n_src)], lambda parts: load(q, parts[0], 0).start())
+    h_load.wait()
+    load(q, pd, 0).wait()
+    load(1 - q, pd, 1).wait()
+    part = LAST_PART
+
+    @pl.loop(0, n_rows)
+    def _(i):
+        @pl.loop(0, h_buf.shape[1] // part)
+        def _(j):
+            at = pl.ds(pl.multiple_of(j * part, part), part)
+
+            @pl.when(used_ref[r, i] > j * part)
+            def _():
+                o_buf[i, at] = jnp.dot(h_buf[i, at], w_out[...], preferred_element_type=F32).astype(BF16)
+
+            @pl.when(used_ref[r, i] <= j * part)
+            def _():
+                o_buf[i, at] = jnp.zeros((part, o_buf.shape[2]), BF16)
+
+        for s in range(n_rows):
+            @pl.when(i == s)
+            def _():
+                for copy in store(s):
+                    copy.start()
+
+    for s in range(n_rows):
+        for copy in store(s):
+            copy.wait()
+
+
+def ffn_down(r, sources, used, weights, extras, peer, hidden):
+    n_rows, capacity, ffn = hidden.shape
+    n_local, _, half = weights[2].shape
+    d_model = 2 * half
+    own = [weights[2]] + [extra[2] for extra in extras]
+    pieces = [jax.ShapeDtypeStruct((LIGHT, d_model), BF16), jax.ShapeDtypeStruct((capacity - LIGHT, d_model), BF16)]
+    out = pl.pallas_call(
+        functools.partial(ffn_down_body, n_local),
+        in_specs=[SMEM] * 3 + [ANY] * (len(own) + 2),
+        out_specs=[ANY] * (2 * n_rows) + [SMEM],
+        out_shape=pieces * n_rows + [TOKEN],
+        scratch_shapes=[
+            pltpu.VMEM((n_rows, capacity, ffn), BF16),
+            pltpu.VMEM((ffn, d_model), BF16),
+            pltpu.VMEM((n_rows, capacity, d_model), BF16),
+            pltpu.SemaphoreType.DMA,
+            pltpu.SemaphoreType.DMA((2,)),
+            pltpu.SemaphoreType.DMA((n_rows, 2)),
+        ],
+        compiler_params=params(),
+        cost_estimate=cost(2 * n_rows * capacity * d_model * ffn, 2 * d_model * ffn),
+        name="ffn_down",
+    )(r, sources, used, *own, peer[2], hidden)
+    return out[0 : 2 * n_rows : 2], out[1 : 2 * n_rows : 2], out[2 * n_rows]
+
+
 def tail_sum(tail_ref, slot_ref, gate_ref, rows_ref, total):
     n_pos, n_tail = tail_ref.shape
     n_col = rows_ref.shape[0]
@@ -291,8 +449,23 @@
 
 def mix_body(has_tail, r_ref, tab_ref, start_ref, slot_ref, gate_ref, *refs):
     n_rows = tab_ref.shape[1]
-    rows, refs = refs[:n_rows], refs[n_rows:]
-    acc_ref, tails, (out_ref, token, total) = refs[0], refs[1:-3], refs[-3:]
+    if has_tail:
+        firsts, others, refs = refs[:n_rows], refs[n_rows : 2 * n_rows], refs[2 * n_rows :]
+        acc_ref, *tails, out_ref, token, total, held, sem = refs
+        rows = [held.at[k] for k in range(n_rows)]
+        copies = []
+        for k in range(n_rows):
+            for i, (part, spot) in enumerate(((firsts[k], pl.ds(0, LIGHT)), (others[k], pl.ds(LIGHT, others[k].shape[0])))):
+                copies.append(pltpu.make_async_copy(part, held.at[k, spot], sem.at[k, i]))
+
+        @pl.when(pl.program_id(0) == 0)
+        def _():
+            for copy in copies:
+                copy.start()
+            for copy in copies:
+                copy.wait()
+    else:
+        rows, (acc_ref, out_ref, token, total) = refs[:n_rows], refs[n_rows:]
     tile = pl.program_id(0)
     token[0] = 0
     total[...] = acc_ref[...]
@@ -315,22 +488,25 @@
 
 
 def mix(r, table, starts, slot, gate_te, rows, acc, out_dtype, tail=()):
-    _, d_model = rows[0].shape
-    tok_rows = acc.shape[0]
-    n_rows = len(rows)
+    n_rows = table.shape[1]
+    tok_rows, d_model = acc.shape
     col = pl.BlockSpec((TILE, LANES), lambda i: (i, 0))
     wide = pl.BlockSpec((TILE, d_model), lambda i: (i, 0))
 
     def held(value):
         return pl.BlockSpec(value.shape, lambda i: (0, 0), pipeline_mode=pl.Buffered(1))
 
+    scratch = [pltpu.VMEM((TILE, d_model), F32)]
+    if tail:
+        capacity = rows[0].shape[0] + rows[n_rows].shape[0]
+        scratch += [pltpu.VMEM((n_rows, capacity, d_model), BF16), pltpu.SemaphoreType.DMA((n_rows, 2))]
     return pl.pallas_call(
         functools.partial(mix_body, bool(tail)),
         grid=(tok_rows // TILE,),
-        in_specs=[SMEM, SMEM, SMEM, col, col] + [held(row) for row in rows] + [wide] + ([SMEM, held(tail[1])] if tail else []),
+        in_specs=[SMEM, SMEM, SMEM, col, col] + [ANY if tail else held(row) for row in rows] + [wide] + ([SMEM, held(tail[1])] if tail else []),
         out_specs=[wide, SMEM],
         out_shape=[jax.ShapeDtypeStruct((tok_rows, d_model), out_dtype), TOKEN],
-        scratch_shapes=[pltpu.VMEM((TILE, d_model), F32)],
+        scratch_shapes=scratch,
         input_output_aliases={5 + n_rows: 0} if acc.dtype == out_dtype else {},
         compiler_params=params(1),
         cost_estimate=cost(2 * n_rows * tok_rows * WINDOW * d_model, 8 * tok_rows * d_model),
@@ -338,58 +514,67 @@
     )(r, table, starts, slot, gate_te, *rows, acc, *tail)
 
 
-def tail_in_body(idx_ref, x_ref, wg_ref, wu_ref, out_ref):
-    n_src, _, rows, half = x_ref.shape
-    ffn = wg_ref.shape[2]
-    x = x_ref[...].reshape(n_src * rows, half)
-    out_ref[:, 0, :, :ffn] = jnp.dot(x, wg_ref[0], preferred_element_type=F32).reshape(n_src, rows, ffn)
-    out_ref[:, 0, :, ffn:] = jnp.dot(x, wu_ref[0], preferred_element_type=F32).reshape(n_src, rows, ffn)
-
-
-def tail_in(idx, x, w_gate, w_up):
-    n_src, n_tail, rows, half = x.shape
+def unset_body(*refs):
+    pass
+
+
+def unset(*shapes):
+    return pl.pallas_call(unset_body, out_specs=[ANY] * len(shapes), out_shape=list(shapes), name="unset")()
+
+
+def tail_in_body(idx_ref, mine_ref, peer_ref, wg_ref, wu_ref, mine_out, peer_out):
+    rows, ffn = mine_ref.shape[1], wg_ref.shape[2]
+    x = jnp.concatenate([mine_ref[0], peer_ref[0]], axis=0)
+    for w_ref, first in ((wg_ref, 0), (wu_ref, ffn)):
+        part = jnp.dot(x, w_ref[0], preferred_element_type=F32)
+        mine_out[0, :, first : first + ffn] = part[:rows]
+        peer_out[0, :, first : first + ffn] = part[rows:]
+
+
+def tail_in(idx, mine, peer, w_gate, w_up):
+    n_tail, rows, half = mine.shape
     ffn = w_gate.shape[2]
     weight = pl.BlockSpec((1, half, ffn), lambda i, idx: (idx[i], 0, 0))
+    x_spec = pl.BlockSpec((1, rows, half), lambda i, idx: (i, 0, 0))
     return pl.pallas_call(
         tail_in_body,
         grid_spec=pltpu.PrefetchScalarGridSpec(
             num_scalar_prefetch=1,
             grid=(n_tail,),
-            in_specs=[pl.BlockSpec((n_src, 1, rows, half), lambda i, idx: (0, i, 0, 0)), weight, weight],
-            out_specs=pl.BlockSpec((n_src, 1, rows, 2 * ffn), lambda i, idx: (0, i, 0, 0)),
+            in_specs=[x_spec, x_spec, weight, weight],
+            out_specs=[pl.BlockSpec((1, rows, 2 * ffn), lambda i, idx: (i, 0, 0))] * 2,
         ),
-        out_shape=jax.ShapeDtypeStruct((n_src, n_tail, rows, 2 * ffn), F32),
+        out_shape=[jax.ShapeDtypeStruct((n_tail, rows, 2 * ffn), F32)] * 2,
         compiler_params=params(1),
-        cost_estimate=cost(4 * n_src * n_tail * rows * half * ffn, 4 * n_tail * half * ffn),
+        cost_estimate=cost(8 * n_tail * rows * half * ffn, 4 * n_tail * half * ffn),
         name="tail_in",
-    )(idx, x, w_gate, w_up)
-
-
-def tail_out_body(idx_ref, h_ref, wd_ref, out_ref):
-    n_src, _, rows, ffn = h_ref.shape
-    out = jnp.dot(h_ref[...].reshape(n_src * rows, ffn), wd_ref[0], preferred_element_type=F32)
-    out_ref[:, 0] = out.reshape(n_src, rows, -1).astype(BF16)
-
-
-def tail_out(idx, hidden, w_down):
-    n_src, n_tail, rows, ffn = hidden.shape
+    )(idx, mine, peer, w_gate, w_up)
+
+
+def tail_out_body(idx_ref, mine_ref, peer_ref, wd_ref, mine_out, peer_out):
+    rows = mine_ref.shape[1]
+    out = jnp.dot(jnp.concatenate([mine_ref[0], peer_ref[0]], axis=0), wd_ref[0], preferred_element_type=F32).astype(BF16)
+    mine_out[0] = out[:rows]
+    peer_out[0] = out[rows:]
+
+
+def tail_out(idx, mine, peer, w_down):
+    n_tail, rows, ffn = mine.shape
     half = w_down.shape[2]
+    h_spec = pl.BlockSpec((1, rows, ffn), lambda i, idx: (i, 0, 0))
     return pl.pallas_call(
         tail_out_body,
         grid_spec=pltpu.PrefetchScalarGridSpec(
             num_scalar_prefetch=1,
             grid=(n_tail,),
-            in_specs=[
-                pl.BlockSpec((n_src, 1, rows, ffn), lambda i, idx: (0, i, 0, 0)),
-                pl.BlockSpec((1, ffn, half), lambda i, idx: (idx[i], 0, 0)),
-            ],
-            out_specs=pl.BlockSpec((n_src, 1, rows, half), lambda i, idx: (0, i, 0, 0)),
+            in_specs=[h_spec, h_spec, pl.BlockSpec((1, ffn, half), lambda i, idx: (idx[i], 0, 0))],
+            out_specs=[pl.BlockSpec((1, rows, half), lambda i, idx: (i, 0, 0))] * 2,
         ),
-        out_shape=jax.ShapeDtypeStruct((n_src, n_tail, rows, half), BF16),
+        out_shape=[jax.ShapeDtypeStruct((n_tail, rows, half), BF16)] * 2,
         compiler_params=params(1),
-        cost_estimate=cost(2 * n_src * n_tail * rows * half * ffn, 2 * n_tail * half * ffn),
+        cost_estimate=cost(4 * n_tail * rows * half * ffn, 2 * n_tail * half * ffn),
         name="tail_out",
-    )(idx, hidden, w_down)
+    )(idx, mine, peer, w_down)
 
 
 def plan(counts, n_group):
@@ -401,15 +586,17 @@
     active = jnp.sum((load > 0).astype(I32), axis=1)
     tail = jnp.minimum(jnp.sum(((load > 0) & (load <= TAIL_CAP)).astype(I32), axis=1), TAIL)
     full = active - tail
-    partner = full.reshape(-1, 2)[:, ::-1].reshape(-1)
-    give = jnp.clip((full - partner) // 2, 0, MOVES)
+    position = jnp.arange(n_group, dtype=I32)[:, None]
+    least = (jnp.max(jnp.sum(full.reshape(-1, 2), axis=1)) + 1) // 2
+    limit = jnp.where(least >= MOVES + 2, MOVES, 0)
+    n_round = jnp.maximum(jnp.maximum(least, jnp.max(full) - limit), 2)
+    give = jnp.clip(full - n_round, 0, limit)
     keep = full - give
     partner_keep = keep.reshape(-1, 2)[:, ::-1].reshape(-1)
-    position = jnp.arange(n_group, dtype=I32)[:, None]
     kept = rank < keep[:, None]
     in_round = rank < full[:, None]
     to = jnp.where(kept, position, position ^ 1)
-    at = jnp.where(kept, rank, partner_keep[:, None] + rank - keep[:, None])
+    at = jnp.where(kept, rank, jnp.maximum(partner_keep[:, None], 2) + rank - keep[:, None])
     source = jnp.where(kept, ids[None, :], n_local + rank - keep[:, None])
     tail_at = jnp.where((rank >= full[:, None]) & (rank < active[:, None]), rank - full[:, None], -1)
     n_slots = n_local + MOVES + 2
@@ -425,7 +612,8 @@
     tails = jnp.max(jnp.where(tail_hit, ids[None, None, :], -1), axis=2)
     move_hit = (rank - keep[:, None])[:, None, :] == steps[None, :MOVES, None]
     moves = jnp.max(jnp.where(move_hit, ids[None, None, :], 0), axis=2)
-    return experts, sources, tails, moves, jnp.maximum(jnp.max(keep + give.reshape(-1, 2)[:, ::-1].reshape(-1)), 1)
+    last_load = jnp.max(jnp.where((at == n_round - 1) & in_round, load, 0))
+    return experts, sources, tails, moves, n_round, last_load
 
 
 def solution(mesh):
@@ -456,7 +644,7 @@
         slot, slot_t, gate_te, tile_starts, count = route(idx_loc.T, gate_loc.T, capacity)
         starts = jnp.concatenate([tile_starts[:, 0], count[:1]], axis=0)
         counts = lax.all_gather(count[0, :n_exp], ("expert", "data"))
-        experts, sources, tails, moves, n_round = plan(counts, n_group)
+        experts, sources, tails, moves, n_round, last_load = plan(counts, n_group)
         mine = me ^ jnp.arange(n_group, dtype=I32)
         table = jnp.concatenate([jnp.full((1, n_group), NO_EXPERT, I32), experts[mine].T], axis=0)
         my_sources = sources[me]
@@ -474,54 +662,82 @@
             kind = jnp.maximum(s - n_local + 1, 0)
             return lax.switch(kind, [lambda: slices(jnp.minimum(s, n_local - 1))] + [lambda i=i: extras[i] for i in range(MOVES)])
 
-        def one_round(r, carry):
+        def one_round(r, carry, tag):
             token, peer, rows, back, send, acc = carry
             peer_next = swapped(send)
             *picked, token = pick(r + 1 + token, table, starts, slot_t, x_loc, capacity)
             rows_next = spread(picked)
             out_rows, token = expert_ffn(r + token, my_sources, used, weights, extras, peer, rows)
             back_next = spread(out_rows)
-            send_next, token = lax.optimization_barrier((outgoing(r[0] + 2 + token[0]), token))
+            send_next, token = lax.optimization_barrier((outgoing(r[0] + 2 + token[0]), token)) if not tag.endswith("1") else (None, token)
             acc, token = mix(r - 1 + token, table, starts, slot, gate_te, back, acc, F32)
             return token, peer_next, rows_next, back_next, send_next, acc
 
+        half = d_model // n_data
         peer = swapped(slices(my_sources[0]))
         *picked, token = pick(jnp.zeros((1,), I32), table, starts, slot_t, x_loc, capacity)
         rows = spread(picked)
         later, token = lax.optimization_barrier((weights, token))
         extras = tuple(tuple(across(part, 1) for part in slices(moves[me, i] + token[0], later)) for i in range(MOVES))
-        send, token = lax.optimization_barrier((outgoing(1 + token[0]), token))
-        tail_rows = spread(pick_tail(tail_global + token, slot_t, x_loc))
-        blank = tuple(jnp.zeros((capacity, d_model), BF16) for _ in range(n_group))
+        tail_picked, token = lax.optimization_barrier((tuple(pick_tail(tail_global + token, slot_t, x_loc)), token))
+        tail_rows = spread(tail_picked)
+        later, token = lax.optimization_barrier((weights, token))
+        send = slices(my_sources[1] + token[0], later)
+        blank = tuple(unset(*[jax.ShapeDtypeStruct((capacity, d_model), BF16)] * n_group))
         carry = (token, peer, rows, blank, send, x_loc.astype(F32))
-        tail_x = jnp.stack([rows.reshape(TAIL, TAIL_CAP, d_model) for rows in tail_rows], axis=1).reshape(TAIL, n_group * TAIL_CAP, d_model)
-        half = d_model // n_data
+        tail_x = jnp.stack([group.reshape(TAIL, TAIL_CAP, d_model) for group in tail_rows], axis=1).reshape(TAIL, n_group * TAIL_CAP, d_model)
         tail_mine = lax.dynamic_slice_in_dim(tail_x, q * half, half, axis=2)
         tail_peer = lax.ppermute(lax.dynamic_slice_in_dim(tail_x, (1 - q) * half, half, axis=2), "data", swap)
 
-        odd = (n_round - 1) % 2
-        carry = lax.fori_loop(0, odd, lambda i, c: one_round(jnp.full((1,), i, I32), c), carry)
+        odd = n_round % 2
 
         def two_rounds(i, c):
-            r = jnp.full((1,), odd + 2 * i, I32)
-            return one_round(r + 1, one_round(r, c))
-
-        token, peer, rows, back, _, acc = lax.fori_loop(0, (n_round - 1) // 2, two_rounds, carry)
+            r = jnp.full((1,), 2 * i, I32)
+            return one_round(r + 1, one_round(r, c, "a"), "b")
+
+        carry = lax.fori_loop(0, (n_round - 2) // 2, two_rounds, carry)
         last = jnp.full((1,), n_round - 1, I32)
-        partial = tail_in(tail_local + token, jnp.stack([tail_mine, tail_peer]), wg_loc, wu_loc)
-        partial, token = lax.optimization_barrier((partial, token))
-        partial_sum = partial[0] + lax.ppermute(partial[1], "data", swap)
-        out_last, token = expert_ffn(last + token, my_sources, used, weights, extras, peer, rows)
-        back_last = spread(out_last)
-        acc, token = mix(last - 1 + token, table, starts, slot, gate_te, back, acc, F32)
         ffn = wg_loc.shape[2]
-        tail_h = (jax.nn.silu(partial_sum[..., :ffn]) * partial_sum[..., ffn:]).astype(BF16)
-        tail_o = tail_out(tail_local + token, jnp.stack([tail_h, lax.ppermute(tail_h, "data", swap)]), wd_loc)
-        other_half = lax.ppermute(tail_o[1], "data", swap)
-        whole = jnp.where(q == 0, jnp.concatenate([tail_o[0], other_half], axis=2), jnp.concatenate([other_half, tail_o[0]], axis=2))
-        whole = whole.reshape(TAIL, n_group, TAIL_CAP, d_model)
-        tail_back = spread([whole[:, k].reshape(TAIL * TAIL_CAP, d_model) for k in range(n_group)])
-        tail = (tail_global, jnp.concatenate(tail_back, axis=0))
-        return mix(last + token, table, starts, slot, gate_te, back_last, acc, BF16, tail)[0]
+
+        def diagonal(value, k):
+            pairs = [(s * n_group + p, (1 - s) * n_group + (p ^ k)) for p in range(n_group) for s in range(n_data)]
+            return lax.ppermute(value, ("data", "expert"), pairs)
+
+        def finish(n_peel):
+            def run():
+                state = carry
+                for left in range(n_peel, 0, -1):
+                    state = one_round(last - left, state, f"peel{n_peel}{left}")
+                token, peer, rows, back, _, acc = state
+                (partial, partial_peer), token = lax.optimization_barrier((tuple(tail_in(tail_local + token, tail_mine, tail_peer, wg_loc, wu_loc)), token))
+                partial_peer = lax.ppermute(partial_peer, "data", swap)
+                hidden, token = ffn_up(last + token, my_sources, used, weights, extras, peer, rows)
+                out_first, out_others, token = ffn_down(last + token, my_sources, used, weights, extras, peer, hidden)
+                back_first = spread(out_first)
+                acc, token = mix(last - 1 + token, table, starts, slot, gate_te, back, acc, F32)
+                (partial, partial_peer), token = lax.optimization_barrier(((partial, partial_peer), token))
+                partial_sum = partial + partial_peer
+                tail_h = (jax.nn.silu(partial_sum[..., :ffn]) * partial_sum[..., ffn:]).astype(BF16)
+                tail_h_peer = lax.ppermute(tail_h, "data", swap)
+                mine, theirs = tail_out(tail_local + token, tail_h, tail_h_peer, wd_loc)
+                mine, theirs = (o.reshape(TAIL, n_group, TAIL_CAP, half) for o in (mine, theirs))
+                tail_halves = []
+                for k in range(n_group):
+                    near, far = mine[:, k].reshape(TAIL * TAIL_CAP, half), theirs[:, k].reshape(TAIL * TAIL_CAP, half)
+                    tail_halves.append((across(near, k) if k else near, diagonal(far, k)))
+                near, far = (jnp.concatenate(parts, axis=0) for parts in zip(*tail_halves))
+                tail_back = jnp.where(q == 0, jnp.concatenate([near, far], axis=1), jnp.concatenate([far, near], axis=1))
+                away = tuple(out_others[1:])
+                others = lax.cond(
+                    last_load > LIGHT,
+                    lambda: tuple(across(group, k) for k, group in enumerate(away, 1)),
+                    lambda: tuple(jnp.zeros_like(group) for group in away),
+                )
+                back_last = list(back_first) + [out_others[0], *others]
+                return mix(last + token, table, starts, slot, gate_te, back_last, acc, BF16, (tail_global, tail_back))[0]
+
+            return run
+
+        return lax.cond(odd == 1, finish(2), finish(1))
 
     return jax.shard_map(device_body, mesh=mesh, in_specs=(tok_spec, tok_spec, tok_spec, wide_spec, wide_spec, down_spec), out_specs=tok_spec, check_vma=False)

time: 2730 us -> 2600 us (0.952)
  waiting for transfers between devices: 1160 us -> 1070 us
  local copies, waits for them, and re-layouts: 186 us -> 129 us
    ppermute x72, waiting for transfers between devices: 478 us -> 320 us  [across(): return lax.ppermute(value, 'expert', [(p, p ^ k) for p in range(n_group)])]
    ppermute x1, waiting for transfers between devices: 7.9 us -> 63.8 us  [device_body(): lax.ppermute(lax.dynamic_slice_in_dim(tail_x, (1 - q) * half, half, axis=...]
    while x36 -> x24, local copies, waits for them, and re-layouts: 29.6 us -> 0.05 us
    pallas_call x10 -> x9, Pallas kernels: 374 us -> 362 us  [expert_ffn(): pl.pallas_call(functools.partial(ffn_body, n_local), in_specs=[SMEM] * 3...]
    squeeze x26 -> x24, local copies, waits for them, and re-layouts: 119 us -> 110 us  [slices(): lax.dynamic_index_in_dim(w, e, axis=0, keepdims=False)]
  transfers between devices with their start and end apart: 106 -> 109, of which waited for: 40 -> 38; matrix products, arithmetic and copies ran while one was open for 7% -> 6% of each run, Pallas kernels for 33% -> 36%
where the time goes in v3:
time: 2600 us; the launch traced here: 2590 us
  Pallas kernels  1120 us (43%)
  waiting for transfers between devices  1070 us (41%)
  starting transfers between devices  172 us (7%)
  local copies, waits for them, and re-layouts  129 us (5%)
  loops' own time  46.2 us (2%)
  other arithmetic  32 us (1%)
    ppermute x30, waiting for transfers between devices, swapped(): return tuple((lax.ppermute(part, 'data', swap) for part in parts))  637 us
    pallas_call x11, Pallas kernels, mix(): pl.pallas_call(functools.partial(mix_body, bool(tail)), grid=(tok_rows //...  462 us
    pallas_call x9, Pallas kernels, expert_ffn(): pl.pallas_call(functools.partial(ffn_body, n_local), in_specs=[SMEM] * 3...  362 us
    ppermute x72, waiting for transfers between devices, across(): return lax.ppermute(value, 'expert', [(p, p ^ k) for p in range(n_group)])  320 us
    pallas_call x10, Pallas kernels, pick(): pl.pallas_call(pick_body, grid=(tok_rows // TILE,), in_specs=[SMEM, SMEM,...  232 us
    ppermute x72, starting transfers between devices, across(): return lax.ppermute(value, 'expert', [(p, p ^ k) for p in range(n_group)])  126 us
    squeeze x24, local copies, waits for them, and re-layouts, slices(): lax.dynamic_index_in_dim(w, e, axis=0, keepdims=False)  110 us
    ppermute x1, waiting for transfers between devices, device_body(): lax.ppermute(lax.dynamic_slice_in_dim(tail_x, (1 - q) * half, half, axis=...  63.8 us
  transfers between devices with their start and end apart: 109, of which 38 were waited for; matrix products, arithmetic and copies ran while one was open for 6% of the time, Pallas kernels for 36%

profile of v3, /device:TPU:0, one launch (start us, length us, event | category | flops | bytes accessed | tf_op | source)
XLA Modules:
  0.0 2585.4 jit_solution(17495041451220172840)
XLA Ops:
  99.6 63.8 %collective-permute-done.90 = bf16[3,64,1024]{2,1,0:T(8,128)(2,1)S(1)} collective-permute-done((bf16[3,64,1024]{2,1,0:T(8,128)(2,1)S(1)}, bf16[3,64,1024]{2,1,0:T(8,128)(2,1)S(1)}, u32[]{:S(2)}, u32[]{:S(2)}) %collective-permute-start.90) | collective-permute-done | bytes 393248 | tf_op jit(solution)/shard_map/ppermute | solution.py:690
  225.4 60.6 %collective-permute-done.77 = bf16[1408,1024]{1,0:T(8,128)(2,1)} collective-permute-done((bf16[1408,1024]{1,0:T(8,128)(2,1)S(1)}, bf16[1408,1024]{1,0:T(8,128)(2,1)}, u32[]{:S(2)}, u32[]{:S(2)}) %collective-permute-start.77) | collective-permute-done | bytes 2883616 | tf_op jit(solution)/shard_map/ppermute | solution.py:634
  317.7 1866.1 %while.45 = (s32[]{:T(128)}, s32[1]{0:T(128)}, bf16[1024,1408]{1,0:T(8,128)(2,1)}, bf16[1024,1408]{1,0:T(8,128)(2,1)}, bf16[1408,1024]{1,0:T(8,128)(2,1)}, /*ind...) while((s32[]{:T(128)}, s32[1]{0:T(128)}, ...), condition=%wide.region_18.19_spmd, body=%wide.region_11.18_spmd.sunk | while | flops 87644176384 | bytes 424150528 | solution.py:698
  344.1 51.5 %ffn.22 = (bf16[480,2048]{1,0:T(8,128)(2,1)}, bf16[480,2048]{1,0:T(8,128)(2,1)}, bf16[480,2048]{1,0:T(8,128)(2,1)}, bf16[480,2048]{1,0:T(8,128)(2,1)}, s32[1]{0:T(128)}) custom-call(s32[1]{0:T(128)S(6)} %add.554.r_ref, s32[20]{0:T(128)S(1)} %get-tuple-element.1893.src_ref, s32[20,4]{1,0:T(8,128)S(1)} %get-tuple-element.1894.used_ref, ...), custom_call_target="tpu_custom_call" | custom-call | flops 33218887680 | bytes 17301504 | tf_op jit(solution)/shard_map/while/body/ffn/pallas_call | solution.py:250
  486.7 41.9 %collective-permute-done.65.refs_3_ = bf16[480,2048]{1,0:T(8,128)(2,1)S(1)} collective-permute-done((bf16[480,2048]{1,0:T(8,128)(2,1)S(1)}, bf16[480,2048]{1,0:T(8,128)(2,1)S(1)}, u32[]{:S(2)}, u32[]{:S(2)}) %collective-permute-start.65) | collective-permute-done | bytes 1966112 | tf_op jit(solution)/shard_map/while/body/ppermute | solution.py:628
  537.9 61.0 %collective-permute-done.57.refs_9_ = bf16[1024,1408]{1,0:T(8,128)(2,1)} collective-permute-done((bf16[1024,1408]{1,0:T(8,128)(2,1)}, bf16[1024,1408]{1,0:T(8,128)(2,1)}, u32[]{:S(2)}, u32[]{:S(2)}) %collective-permute-start.57) | collective-permute-done | bytes 2883616 | tf_op jit(solution)/shard_map/while/body/ppermute | solution.py:634
  598.9 51.9 %ffn.23 = (bf16[480,2048]{1,0:T(8,128)(2,1)S(1)}, bf16[480,2048]{1,0:T(8,128)(2,1)}, bf16[480,2048]{1,0:T(8,128)(2,1)}, bf16[480,2048]{1,0:T(8,128)(2,1)}, s32[1]{0:T(128)}) custom-call(s32[1]{0:T(128)S(6)} %add.560.r_ref, s32[20]{0:T(128)S(1)} %get-tuple-element.1893.src_ref, s32[20,4]{1,0:T(8,128)S(1)} %get-tuple-element.1894.used_ref, ...), custom_call_target="tpu_custom_call" | custom-call | flops 33218887680 | bytes 17301504 | tf_op jit(solution)/shard_map/while/body/ffn/pallas_call | solution.py:250
  722.5 60.8 %collective-permute-done.68 = bf16[1408,1024]{1,0:T(8,128)(2,1)} collective-permute-done((bf16[1408,1024]{1,0:T(8,128)(2,1)}, bf16[1408,1024]{1,0:T(8,128)(2,1)}, u32[]{:S(2)}, u32[]{:S(2)}) %collective-permute-start.68) | collective-permute-done | bytes 2883616 | tf_op jit(solution)/shard_map/while/body/ppermute | solution.py:634
  809.3 51.8 %ffn.22 = (bf16[480,2048]{1,0:T(8,128)(2,1)}, bf16[480,2048]{1,0:T(8,128)(2,1)}, bf16[480,2048]{1,0:T(8,128)(2,1)}, bf16[480,2048]{1,0:T(8,128)(2,1)}, s32[1]{0:T(128)}) custom-call(s32[1]{0:T(128)S(6)} %add.554.r_ref, s32[20]{0:T(128)S(1)} %get-tuple-element.1893.src_ref, s32[20,4]{1,0:T(8,128)S(1)} %get-tuple-element.1894.used_ref, ...), custom_call_target="tpu_custom_call" | custom-call | flops 33218887680 | bytes 17301504 | tf_op jit(solution)/shard_map/while/body/ffn/pallas_call | solution.py:250
  962.6 42.0 %collective-permute-done.65.refs_3_ = bf16[480,2048]{1,0:T(8,128)(2,1)S(1)} collective-permute-done((bf16[480,2048]{1,0:T(8,128)(2,1)S(1)}, bf16[480,2048]{1,0:T(8,128)(2,1)S(1)}, u32[]{:S(2)}, u32[]{:S(2)}) %collective-permute-start.65) | collective-permute-done | bytes 1966112 | tf_op jit(solution)/shard_map/while/body/ppermute | solution.py:628
  1008.4 55.6 %collective-permute-done.57.refs_9_ = bf16[1024,1408]{1,0:T(8,128)(2,1)} collective-permute-done((bf16[1024,1408]{1,0:T(8,128)(2,1)}, bf16[1024,1408]{1,0:T(8,128)(2,1)}, u32[]{:S(2)}, u32[]{:S(2)}) %collective-permute-start.57) | collective-permute-done | bytes 2883616 | tf_op jit(solution)/shard_map/while/body/ppermute | solution.py:634
  1064.0 51.9 %ffn.23 = (bf16[480,2048]{1,0:T(8,128)(2,1)S(1)}, bf16[480,2048]{1,0:T(8,128)(2,1)}, bf16[480,2048]{1,0:T(8,128)(2,1)}, bf16[480,2048]{1,0:T(8,128)(2,1)}, s32[1]{0:T(128)}) custom-call(s32[1]{0:T(128)S(6)} %add.560.r_ref, s32[20]{0:T(128)S(1)} %get-tuple-element.1893.src_ref, s32[20,4]{1,0:T(8,128)S(1)} %get-tuple-element.1894.used_ref, ...), custom_call_target="tpu_custom_call" | custom-call | flops 33218887680 | bytes 17301504 | tf_op jit(solution)/shard_map/while/body/ffn/pallas_call | solution.py:250
  1187.6 60.8 %collective-permute-done.68 = bf16[1408,1024]{1,0:T(8,128)(2,1)} collective-permute-done((bf16[1408,1024]{1,0:T(8,128)(2,1)}, bf16[1408,1024]{1,0:T(8,128)(2,1)}, u32[]{:S(2)}, u32[]{:S(2)}) %collective-permute-start.68) | collective-permute-done | bytes 2883616 | tf_op jit(solution)/shard_map/while/body/ppermute | solution.py:634
  1276.7 46.5 %ffn.22 = (bf16[480,2048]{1,0:T(8,128)(2,1)}, bf16[480,2048]{1,0:T(8,128)(2,1)}, bf16[480,2048]{1,0:T(8,128)(2,1)}, bf16[480,2048]{1,0:T(8,128)(2,1)}, s32[1]{0:T(128)}) custom-call(s32[1]{0:T(128)S(6)} %add.554.r_ref, s32[20]{0:T(128)S(1)} %get-tuple-element.1893.src_ref, s32[20,4]{1,0:T(8,128)S(1)} %get-tuple-element.1894.used_ref, ...), custom_call_target="tpu_custom_call" | custom-call | flops 33218887680 | bytes 17301504 | tf_op jit(solution)/shard_map/while/body/ffn/pallas_call | solution.py:250
  1481.4 50.6 %collective-permute-done.57.refs_9_ = bf16[1024,1408]{1,0:T(8,128)(2,1)} collective-permute-done((bf16[1024,1408]{1,0:T(8,128)(2,1)}, bf16[1024,1408]{1,0:T(8,128)(2,1)}, u32[]{:S(2)}, u32[]{:S(2)}) %collective-permute-start.57) | collective-permute-done | bytes 2883616 | tf_op jit(solution)/shard_map/while/body/ppermute | solution.py:634
  1606.4 42.6 %mix.31 = (f32[4096,2048]{1,0:T(8,128)}, s32[1]{0:T(128)}) custom-call(s32[1]{0:T(128)S(6)} %add.564.r_ref, s32[21,4]{1,0:T(8,128)S(1)} %get-tuple-element.1889.tab_ref, s32[17,128]{1,0:T(8,128)S(1)} %get-tuple-element.1890.start_ref, s32[4096,128]{1,0:T(8,128)} %get-tuple-element.1904.slot_ref, ...), custom_call_target="tpu_custom_call", output_to_operand_aliasing={{0}: (9, {})} | custom-call | flops 8589934592 | bytes 67108864 | tf_op jit(solution)/shard_map/while/body/mix/pallas_call | solution.py:503
  1655.6 60.6 %collective-permute-done.68 = bf16[1408,1024]{1,0:T(8,128)(2,1)} collective-permute-done((bf16[1408,1024]{1,0:T(8,128)(2,1)}, bf16[1408,1024]{1,0:T(8,128)(2,1)}, u32[]{:S(2)}, u32[]{:S(2)}) %collective-permute-start.68) | collective-permute-done | bytes 2883616 | tf_op jit(solution)/shard_map/while/body/ppermute | solution.py:634
  1830.5 45.0 %mix.30 = (f32[4096,2048]{1,0:T(8,128)}, s32[1]{0:T(128)}) custom-call(s32[1]{0:T(128)S(6)} %add.558.r_ref, s32[21,4]{1,0:T(8,128)S(1)} %get-tuple-element.1889.tab_ref, s32[17,128]{1,0:T(8,128)S(1)} %get-tuple-element.1890.start_ref, s32[4096,128]{1,0:T(8,128)} %get-tuple-element.1904.slot_ref, ...), custom_call_target="tpu_custom_call", output_to_operand_aliasing={{0}: (9, {})} | custom-call | flops 8589934592 | bytes 67108864 | tf_op jit(solution)/shard_map/while/body/mix/pallas_call | solution.py:503
  1946.4 52.0 %collective-permute-done.57.refs_9_ = bf16[1024,1408]{1,0:T(8,128)(2,1)} collective-permute-done((bf16[1024,1408]{1,0:T(8,128)(2,1)}, bf16[1024,1408]{1,0:T(8,128)(2,1)}, u32[]{:S(2)}, u32[]{:S(2)}) %collective-permute-start.57) | collective-permute-done | bytes 2883616 | tf_op jit(solution)/shard_map/while/body/ppermute | solution.py:634
  2073.3 51.7 %mix.31 = (f32[4096,2048]{1,0:T(8,128)}, s32[1]{0:T(128)}) custom-call(s32[1]{0:T(128)S(6)} %add.564.r_ref, s32[21,4]{1,0:T(8,128)S(1)} %get-tuple-element.1889.tab_ref, s32[17,128]{1,0:T(8,128)S(1)} %get-tuple-element.1890.start_ref, s32[4096,128]{1,0:T(8,128)} %get-tuple-element.1904.slot_ref, ...), custom_call_target="tpu_custom_call", output_to_operand_aliasing={{0}: (9, {})} | custom-call | flops 8589934592 | bytes 67108864 | tf_op jit(solution)/shard_map/while/body/mix/pallas_call | solution.py:503
  2125.0 58.4 %collective-permute-done.68 = bf16[1408,1024]{1,0:T(8,128)(2,1)} collective-permute-done((bf16[1408,1024]{1,0:T(8,128)(2,1)}, bf16[1408,1024]{1,0:T(8,128)(2,1)}, u32[]{:S(2)}, u32[]{:S(2)}) %collective-permute-start.68) | collective-permute-done | bytes 2883616 | tf_op jit(solution)/shard_map/while/body/ppermute | solution.py:634
  2183.8 400.3 %conditional.6 = (bf16[4096,2048]{1,0:T(8,128)(2,1)}) conditional(s32[]{:T(128)} %convert_element_type.36, (s32[1]{0:T(128)}, s32[1]{0:T(128)}, s32[21,4]{1,0:T(8,128)S(1)}, s32[17,128]{1,0:T(8,128)S(1)}, s32[128,4096]{1,0:T(8,128)}, /*index=5*/bf16[4096,2048]{1,0:T(8,128)(2,1)}, s32[20]{0:T(128)S(1)}, s32[20,4]{1,0:T(8,128)S(1)}, ...), branch_computations={%region_20.23_spmd, %region_23.29_spmd} | conditional | flops 141375242240 | bytes 642532992 | solution.py:741
  2225.2 43.3 %mix.23 = (f32[4096,2048]{1,0:T(8,128)}, s32[1]{0:T(128)}) custom-call(s32[1]{0:T(128)S(6)} %add.407.r_ref, s32[21,4]{1,0:T(8,128)S(1)} %get-tuple-element.1062.tab_ref, s32[17,128]{1,0:T(8,128)S(1)} %get-tuple-element.1063.start_ref, s32[4096,128]{1,0:T(8,128)} %get-tuple-element.1086.slot_ref, ...), custom_call_target="tpu_custom_call", output_to_operand_aliasing={{0}: (9, {})} | custom-call | flops 8589934592 | bytes 67108864 | tf_op jit(solution)/shard_map/cond/branch_0_fun/mix/pallas_call | solution.py:503
  2529.5 45.4 %mix.25 = (bf16[4096,2048]{1,0:T(8,128)(2,1)}, s32[1]{0:T(128)}) custom-call(s32[1]{0:T(128)S(6)} %add.414.r_ref, s32[21,4]{1,0:T(8,128)S(1)} %get-tuple-element.1062.tab_ref, s32[17,128]{1,0:T(8,128)S(1)} %get-tuple-element.1063.start_ref, s32[4096,128]{1,0:T(8,128)} %get-tuple-element.1086.slot_ref, f32[4096,128]{1,0:T(8,128)} %get-tuple-element.1087.gate_ref, ...), custom_call_target="tpu_custom_call" | custom-call | flops 8589934592 | bytes 67108864 | tf_op jit(solution)/shard_map/cond/branch_0_fun/mix/pallas_call | solution.py:503
  (409 shorter events, 1463.9 us)
Async XLA Ops:
  428.7 170.2 %collective-permute-start.57 = (bf16[1024,1408]{1,0:T(8,128)(2,1)}, bf16[1024,1408]{1,0:T(8,128)(2,1)}, u32[]{:S(2)}, u32[]{:S(2)}) collective-permute-start(bf16[1024,1408]{1,0:T(8,128)(2,1)} %get-tuple-element.1840), channel_id=1, source_target_pairs={{0,4},{4,0},{1,5},{5,1},{2,6},{6,2},{3,7},{7,3}} | collective-permute-start | bytes 8650760 | tf_op jit(solution)/shard_map/while/body/ppermute | solution.py:634
  529.6 192.9 %collective-permute-start.67 = (bf16[1024,1408]{1,0:T(8,128)(2,1)}, bf16[1024,1408]{1,0:T(8,128)(2,1)}, u32[]{:S(2)}, u32[]{:S(2)}) collective-permute-start(bf16[1024,1408]{1,0:T(8,128)(2,1)} %get-tuple-element.1730), channel_id=1, source_target_pairs={{0,4},{4,0},{1,5},{5,1},{2,6},{6,2},{3,7},{7,3}} | collective-permute-start | bytes 8650760 | tf_op jit(solution)/shard_map/while/body/ppermute | solution.py:634
  530.7 252.6 %collective-permute-start.68 = (bf16[1408,1024]{1,0:T(8,128)(2,1)}, bf16[1408,1024]{1,0:T(8,128)(2,1)}, u32[]{:S(2)}, u32[]{:S(2)}) collective-permute-start(bf16[1408,1024]{1,0:T(8,128)(2,1)} %get-tuple-element.1731), channel_id=1, source_target_pairs={{0,4},{4,0},{1,5},{5,1},{2,6},{6,2},{3,7},{7,3}} | collective-permute-start | bytes 8650760 | tf_op jit(solution)/shard_map/while/body/ppermute | solution.py:634
  650.8 132.4 %collective-permute-start.72 = (bf16[480,2048]{1,0:T(8,128)(2,1)}, bf16[480,2048]{1,0:T(8,128)(2,1)}, u32[]{:S(2)}, u32[]{:S(2)}) collective-permute-start(bf16[480,2048]{1,0:T(8,128)(2,1)} %get-tuple-element.1737), channel_id=1, source_target_pairs={{0,1},{1,0},{2,3},{3,2},{4,5},{5,4},{6,7},{7,6}} | collective-permute-start | bytes 5898248 | tf_op jit(solution)/shard_map/while/body/ppermute | solution.py:628
  893.9 170.0 %collective-permute-start.57 = (bf16[1024,1408]{1,0:T(8,128)(2,1)}, bf16[1024,1408]{1,0:T(8,128)(2,1)}, u32[]{:S(2)}, u32[]{:S(2)}) collective-permute-start(bf16[1024,1408]{1,0:T(8,128)(2,1)} %get-tuple-element.1840), channel_id=1, source_target_pairs={{0,4},{4,0},{1,5},{5,1},{2,6},{6,2},{3,7},{7,3}} | collective-permute-start | bytes 8650760 | tf_op jit(solution)/shard_map/while/body/ppermute | solution.py:634
  1005.3 182.2 %collective-permute-start.67 = (bf16[1024,1408]{1,0:T(8,128)(2,1)}, bf16[1024,1408]{1,0:T(8,128)(2,1)}, u32[]{:S(2)}, u32[]{:S(2)}) collective-permute-start(bf16[1024,1408]{1,0:T(8,128)(2,1)} %get-tuple-element.1730), channel_id=1, source_target_pairs={{0,4},{4,0},{1,5},{5,1},{2,6},{6,2},{3,7},{7,3}} | collective-permute-start | bytes 8650760 | tf_op jit(solution)/shard_map/while/body/ppermute | solution.py:634
  1006.7 241.7 %collective-permute-start.68 = (bf16[1408,1024]{1,0:T(8,128)(2,1)}, bf16[1408,1024]{1,0:T(8,128)(2,1)}, u32[]{:S(2)}, u32[]{:S(2)}) collective-permute-start(bf16[1408,1024]{1,0:T(8,128)(2,1)} %get-tuple-element.1731), channel_id=1, source_target_pairs={{0,4},{4,0},{1,5},{5,1},{2,6},{6,2},{3,7},{7,3}} | collective-permute-start | bytes 8650760 | tf_op jit(solution)/shard_map/while/body/ppermute | solution.py:634
  1115.9 132.5 %collective-permute-start.72 = (bf16[480,2048]{1,0:T(8,128)(2,1)}, bf16[480,2048]{1,0:T(8,128)(2,1)}, u32[]{:S(2)}, u32[]{:S(2)}) collective-permute-start(bf16[480,2048]{1,0:T(8,128)(2,1)} %get-tuple-element.1737), channel_id=1, source_target_pairs={{0,1},{1,0},{2,3},{3,2},{4,5},{5,4},{6,7},{7,6}} | collective-permute-start | bytes 5898248 | tf_op jit(solution)/shard_map/while/body/ppermute | solution.py:628
  1342.8 135.6 %collective-permute-start.59 = (bf16[1408,1024]{1,0:T(8,128)(2,1)}, bf16[1408,1024]{1,0:T(8,128)(2,1)}, u32[]{:S(2)}, u32[]{:S(2)}) collective-permute-start(bf16[1408,1024]{1,0:T(8,128)(2,1)} %get-tuple-element.1842), channel_id=1, source_target_pairs={{0,4},{4,0},{1,5},{5,1},{2,6},{6,2},{3,7},{7,3}} | collective-permute-start | bytes 8650760 | tf_op jit(solution)/shard_map/while/body/ppermute | solution.py:634
  1344.1 136.2 %collective-permute-start.58 = (bf16[1024,1408]{1,0:T(8,128)(2,1)}, bf16[1024,1408]{1,0:T(8,128)(2,1)}, u32[]{:S(2)}, u32[]{:S(2)}) collective-permute-start(bf16[1024,1408]{1,0:T(8,128)(2,1)} %get-tuple-element.1841), channel_id=1, source_target_pairs={{0,4},{4,0},{1,5},{5,1},{2,6},{6,2},{3,7},{7,3}} | collective-permute-start | bytes 8650760 | tf_op jit(solution)/shard_map/while/body/ppermute | solution.py:634
  1361.4 170.7 %collective-permute-start.57 = (bf16[1024,1408]{1,0:T(8,128)(2,1)}, bf16[1024,1408]{1,0:T(8,128)(2,1)}, u32[]{:S(2)}, u32[]{:S(2)}) collective-permute-start(bf16[1024,1408]{1,0:T(8,128)(2,1)} %get-tuple-element.1840), channel_id=1, source_target_pairs={{0,4},{4,0},{1,5},{5,1},{2,6},{6,2},{3,7},{7,3}} | collective-permute-start | bytes 8650760 | tf_op jit(solution)/shard_map/while/body/ppermute | solution.py:634
  1478.3 177.3 %collective-permute-start.67 = (bf16[1024,1408]{1,0:T(8,128)(2,1)}, bf16[1024,1408]{1,0:T(8,128)(2,1)}, u32[]{:S(2)}, u32[]{:S(2)}) collective-permute-start(bf16[1024,1408]{1,0:T(8,128)(2,1)} %get-tuple-element.1730), channel_id=1, source_target_pairs={{0,4},{4,0},{1,5},{5,1},{2,6},{6,2},{3,7},{7,3}} | collective-permute-start | bytes 8650760 | tf_op jit(solution)/shard_map/while/body/ppermute | solution.py:634
  1478.4 237.8 %collective-permute-start.68 = (bf16[1408,1024]{1,0:T(8,128)(2,1)}, bf16[1408,1024]{1,0:T(8,128)(2,1)}, u32[]{:S(2)}, u32[]{:S(2)}) collective-permute-start(bf16[1408,1024]{1,0:T(8,128)(2,1)} %get-tuple-element.1731), channel_id=1, source_target_pairs={{0,4},{4,0},{1,5},{5,1},{2,6},{6,2},{3,7},{7,3}} | collective-permute-start | bytes 8650760 | tf_op jit(solution)/shard_map/while/body/ppermute | solution.py:634
  1564.0 152.2 %collective-permute-start.72 = (bf16[480,2048]{1,0:T(8,128)(2,1)}, bf16[480,2048]{1,0:T(8,128)(2,1)}, u32[]{:S(2)}, u32[]{:S(2)}) collective-permute-start(bf16[480,2048]{1,0:T(8,128)(2,1)} %get-tuple-element.1737), channel_id=1, source_target_pairs={{0,1},{1,0},{2,3},{3,2},{4,5},{5,4},{6,7},{7,6}} | collective-permute-start | bytes 5898248 | tf_op jit(solution)/shard_map/while/body/ppermute | solution.py:628
  1808.9 135.4 %collective-permute-start.59 = (bf16[1408,1024]{1,0:T(8,128)(2,1)}, bf16[1408,1024]{1,0:T(8,128)(2,1)}, u32[]{:S(2)}, u32[]{:S(2)}) collective-permute-start(bf16[1408,1024]{1,0:T(8,128)(2,1)} %get-tuple-element.1842), channel_id=1, source_target_pairs={{0,4},{4,0},{1,5},{5,1},{2,6},{6,2},{3,7},{7,3}} | collective-permute-start | bytes 8650760 | tf_op jit(solution)/shard_map/while/body/ppermute | solution.py:634
  1811.2 134.2 %collective-permute-start.58 = (bf16[1024,1408]{1,0:T(8,128)(2,1)}, bf16[1024,1408]{1,0:T(8,128)(2,1)}, u32[]{:S(2)}, u32[]{:S(2)}) collective-permute-start(bf16[1024,1408]{1,0:T(8,128)(2,1)} %get-tuple-element.1841), channel_id=1, source_target_pairs={{0,4},{4,0},{1,5},{5,1},{2,6},{6,2},{3,7},{7,3}} | collective-permute-start | bytes 8650760 | tf_op jit(solution)/shard_map/while/body/ppermute | solution.py:634
  1828.3 170.1 %collective-permute-start.57 = (bf16[1024,1408]{1,0:T(8,128)(2,1)}, bf16[1024,1408]{1,0:T(8,128)(2,1)}, u32[]{:S(2)}, u32[]{:S(2)}) collective-permute-start(bf16[1024,1408]{1,0:T(8,128)(2,1)} %get-tuple-element.1840), channel_id=1, source_target_pairs={{0,4},{4,0},{1,5},{5,1},{2,6},{6,2},{3,7},{7,3}} | collective-permute-start | bytes 8650760 | tf_op jit(solution)/shard_map/while/body/ppermute | solution.py:634
  1943.3 181.6 %collective-permute-start.67 = (bf16[1024,1408]{1,0:T(8,128)(2,1)}, bf16[1024,1408]{1,0:T(8,128)(2,1)}, u32[]{:S(2)}, u32[]{:S(2)}) collective-permute-start(bf16[1024,1408]{1,0:T(8,128)(2,1)} %get-tuple-element.1730), channel_id=1, source_target_pairs={{0,4},{4,0},{1,5},{5,1},{2,6},{6,2},{3,7},{7,3}} | collective-permute-start | bytes 8650760 | tf_op jit(solution)/shard_map/while/body/ppermute | solution.py:634
  1944.3 239.0 %collective-permute-start.68 = (bf16[1408,1024]{1,0:T(8,128)(2,1)}, bf16[1408,1024]{1,0:T(8,128)(2,1)}, u32[]{:S(2)}, u32[]{:S(2)}) collective-permute-start(bf16[1408,1024]{1,0:T(8,128)(2,1)} %get-tuple-element.1731), channel_id=1, source_target_pairs={{0,4},{4,0},{1,5},{5,1},{2,6},{6,2},{3,7},{7,3}} | collective-permute-start | bytes 8650760 | tf_op jit(solution)/shard_map/while/body/ppermute | solution.py:634
  2030.8 152.5 %collective-permute-start.72 = (bf16[480,2048]{1,0:T(8,128)(2,1)}, bf16[480,2048]{1,0:T(8,128)(2,1)}, u32[]{:S(2)}, u32[]{:S(2)}) collective-permute-start(bf16[480,2048]{1,0:T(8,128)(2,1)} %get-tuple-element.1737), channel_id=1, source_target_pairs={{0,1},{1,0},{2,3},{3,2},{4,5},{5,4},{6,7},{7,6}} | collective-permute-start | bytes 5898248 | tf_op jit(solution)/shard_map/while/body/ppermute | solution.py:628
  2043.2 140.2 %collective-permute-start.73 = (bf16[480,2048]{1,0:T(8,128)(2,1)}, bf16[480,2048]{1,0:T(8,128)(2,1)}, u32[]{:S(2)}, u32[]{:S(2)}) collective-permute-start(bf16[480,2048]{1,0:T(8,128)(2,1)} %get-tuple-element.1738), channel_id=1, source_target_pairs={{0,2},{1,3},{2,0},{3,1},{4,6},{5,7},{6,4},{7,5}} | collective-permute-start | bytes 5898248 | tf_op jit(solution)/shard_map/while/body/ppermute | solution.py:628
  2183.8 137.7 %collective-permute-start.7 = (bf16[1024,1408]{1,0:T(8,128)(2,1)}, bf16[1024,1408]{1,0:T(8,128)(2,1)}, u32[]{:S(2)}, u32[]{:S(2)}) collective-permute-start(bf16[1024,1408]{1,0:T(8,128)(2,1)} %get-tuple-element.1101), channel_id=1, source_target_pairs={{0,4},{4,0},{1,5},{5,1},{2,6},{6,2},{3,7},{7,3}} | collective-permute-start | bytes 8650760 | tf_op jit(solution)/shard_map/cond/branch_0_fun/ppermute | solution.py:634
  2185.5 136.1 %collective-permute-start.8 = (bf16[1024,1408]{1,0:T(8,128)(2,1)}, bf16[1024,1408]{1,0:T(8,128)(2,1)}, u32[]{:S(2)}, u32[]{:S(2)}) collective-permute-start(bf16[1024,1408]{1,0:T(8,128)(2,1)} %get-tuple-element.1102), channel_id=1, source_target_pairs={{0,4},{4,0},{1,5},{5,1},{2,6},{6,2},{3,7},{7,3}} | collective-permute-start | bytes 8650760 | tf_op jit(solution)/shard_map/cond/branch_0_fun/ppermute | solution.py:634
  2223.4 149.6 %collective-permute-start.12 = (bf16[1408,1024]{1,0:T(8,128)(2,1)}, bf16[1408,1024]{1,0:T(8,128)(2,1)}, u32[]{:S(2)}, u32[]{:S(2)}) collective-permute-start(bf16[1408,1024]{1,0:T(8,128)(2,1)} %get-tuple-element.1108), channel_id=1, source_target_pairs={{0,4},{4,0},{1,5},{5,1},{2,6},{6,2},{3,7},{7,3}} | collective-permute-start | bytes 8650760 | tf_op jit(solution)/shard_map/cond/branch_0_fun/ppermute | solution.py:634
  (111 other events, 9430.8 us)
